TPU v7x, 32 devices: a whole 2x2x4 slice. The times are simulated.
32 devices in a mesh: dp: 8 (over z, x), mp: 4 (over y, core).
Axes of the slice: x: 2, y: 2, z: 4, core: 2. Of those that a mesh axis runs over, the one named last changes fastest.
Arguments:
- grad_tiles: bfloat16 [16, 512, 512], P(None, 'dp', 'mp'), may hold values from -8 to 8
- factor_stats: float32 [16, 2, 512, 512], P('dp', None, 'mp'), may hold values from -80 to 500, as said below
- owner_blocks: int32 [8, 2], replicated, may hold values from 0 to 15, as said below
- rotation: int32 [1], replicated, may hold values from 0 to 7
Outputs:
- preconditioned: bfloat16 [16, 512, 512], P(None, 'dp', 'mp')
- new_stats: float32 [16, 2, 512, 512], P('dp', None, 'mp')
Inputs may be any that keep to these rules, and one draw needn't show every extreme that they name: Each matrix factor_stats[slot, side] is symmetric and positive definite. `owner_blocks`: every block number 0 to 15 stands exactly once.
All inputs are finite; a program needn't handle non-finite values.
Results may differ from a plain program's by a relative error of at most 0.0092.
Values may be sent and summed in bfloat16 or wider, within the bound.
No kernel may reach another device: no remote copies, remote signals or barrier semaphores. Data moves between devices by JAX's collectives and lax.ppermute only.
A program may use at most 64 MiB of HBM per device.

v0:
```python
import jax
import jax.numpy as jnp
from jax import lax
from jax.sharding import PartitionSpec as P

ITERS = 2


decay_rate = 0.9
damping = 1.0


def newton_root(factor):
    order = factor.shape[-1]
    identity = jnp.eye(order, dtype=jnp.float32)
    squares = jnp.sum(jnp.square(factor.astype(jnp.float32)), axis=(1, 2), keepdims=True)
    norm_scale = 2.5 / jnp.sqrt(squares)
    moment = (norm_scale * factor.astype(jnp.float32)).astype(jnp.bfloat16)
    current = None
    for newton_step in range(ITERS):
        step_t = ((5.0 * identity - moment.astype(jnp.float32)) * 0.25).astype(jnp.bfloat16)
        if newton_step == 0:
            current = step_t
        else:
            current = jnp.einsum(
                "sij,sjk->sik", current, step_t, preferred_element_type=jnp.float32
            ).astype(jnp.bfloat16)
        if newton_step + 1 < ITERS:
            square = jnp.einsum(
                "sij,sjk->sik", step_t, step_t, preferred_element_type=jnp.float32
            ).astype(jnp.bfloat16)
            partial_m = jnp.einsum(
                "sij,sjk->sik", square, moment, preferred_element_type=jnp.float32
            ).astype(jnp.bfloat16)
            moment = jnp.einsum(
                "sij,sjk->sik", square, partial_m, preferred_element_type=jnp.float32
            ).astype(jnp.bfloat16)
    return current


def body(grad_tiles, factor_stats, owner_blocks, rotation):
    dp_count = lax.axis_size("dp")
    mp_count = lax.axis_size("mp")
    block_count = grad_tiles.shape[0]
    tile_rows = grad_tiles.shape[1]
    tile_cols = grad_tiles.shape[2]
    slots = owner_blocks.shape[1]
    rows_each = factor_stats.shape[2]
    order = factor_stats.shape[3]
    per_slot = mp_count // slots
    part_width = order // per_slot
    my_index = lax.axis_index("mp")
    my_slot = my_index // per_slot
    my_part = my_index % per_slot
    owners = jnp.roll(owner_blocks, rotation[0], axis=0)
    outgoing = jnp.take(grad_tiles, owners.T, axis=0)
    arrived = lax.all_to_all(outgoing, "dp", split_axis=1, concat_axis=1, tiled=True)
    col_part = arrived.reshape(slots, order, tile_cols)
    blocks = lax.all_gather(col_part, "mp", axis=2, tiled=True)
    row_part = lax.dynamic_slice_in_dim(blocks, my_index * rows_each, rows_each, 1)
    left_rows = jnp.einsum("kij,klj->kil", row_part, blocks, preferred_element_type=jnp.float32)
    right_rows = jnp.einsum("kji,kjl->kil", col_part, blocks, preferred_element_type=jnp.float32)
    fresh_rows = jnp.stack([left_rows, right_rows], axis=1)
    new_stats = decay_rate * factor_stats + (1.0 - decay_rate) * fresh_rows
    row_ids = my_index * rows_each + jnp.arange(rows_each)
    identity_rows = (row_ids[:, None] == jnp.arange(order)[None, :]).astype(jnp.float32)
    factor_rows = (new_stats + damping * identity_rows).astype(jnp.bfloat16)
    spread_rows = jnp.repeat(factor_rows, per_slot, axis=0)
    factor = lax.all_to_all(spread_rows, "mp", split_axis=0, concat_axis=2, tiled=True)[0]
    inverse_roots = newton_root(factor)
    grad_block = lax.dynamic_index_in_dim(blocks, my_slot, 0, keepdims=False)
    right_part = lax.dynamic_slice_in_dim(inverse_roots[1], my_part * part_width, part_width, 1)
    right_applied = jnp.dot(grad_block, right_part, preferred_element_type=jnp.float32).astype(
        jnp.bfloat16
    )
    result = jnp.dot(inverse_roots[0], right_applied, preferred_element_type=jnp.float32).astype(
        jnp.bfloat16
    )
    all_parts = lax.all_gather(result, "mp", axis=1, tiled=True)
    slot_parts = all_parts.reshape(order, slots, order)
    grad_squares = jnp.sum(jnp.square(blocks.astype(jnp.float32)), axis=(1, 2))
    result_squares = jnp.sum(jnp.square(slot_parts.astype(jnp.float32)), axis=(0, 2))
    graft_scale = jnp.sqrt(grad_squares) / (jnp.sqrt(result_squares) + 1e-06)
    my_cols = lax.dynamic_slice_in_dim(slot_parts, my_index * tile_cols, tile_cols, 2)
    scaled = (my_cols.astype(jnp.float32) * graft_scale[None, :, None]).astype(jnp.bfloat16)
    outgoing_back = scaled.reshape(dp_count, tile_rows, slots, tile_cols)
    returned = lax.all_to_all(outgoing_back, "dp", split_axis=0, concat_axis=0, tiled=True)
    owner_flat = owners.reshape(-1)
    position = (
        jnp.zeros((block_count,), jnp.int32)
        .at[owner_flat]
        .set(jnp.arange(owner_flat.shape[0], dtype=jnp.int32))
    )
    holder_row = position // slots
    holder_slot = position % slots
    preconditioned = returned[holder_row, :, holder_slot, :]
    return (preconditioned, new_stats)


def solution(mesh):
    return jax.shard_map(
        body,
        mesh=mesh,
        in_specs=(P(None, "dp", "mp"), P("dp", None, "mp", None), P(), P()),
        out_specs=(P(None, "dp", "mp"), P("dp", None, "mp", None)),
        check_vma=False,
    )
```

profile of v0, /device:TPU:0, one launch (start us, length us, event | category | flops | bytes accessed | tf_op | source)
XLA Modules:
  0.0 122.4 jit_solution(869235592168875510)
XLA Ops:
  7.9 0.8 pad_add_fusion
  8.9 0.6 gather_fusion
  9.7 16.0 %all_to_all.19 = bf16[2,8,64,128]{3,2,0,1:T(8,128)(2,1)S(1)} all-to-all(bf16[2,8,64,128]{3,2,0,1:T(8,128)(2,1)S(1)} %copy.41), channel_id=1, replica_groups=mesh['dp'=8,'mp'=4] {'dp'}, dimensions={1} | all-to-all | bytes 524288 | tf_op jit(solution)/shard_map/all_to_all | solution.py:57
  25.7 0.7 copy.42
  26.4 0.8 fusion.12
  27.2 15.2 %all-gather.3.cloned.1.call-done = bf16[2,512,512]{2,1,0:T(8,128)(2,1)} async-done(((bf16[2,512,128]{2,1,0:T(8,128)(2,1)}), bf16[2,512,512]{2,1,0:T(8,128)(2,1)}) %all-gather.3.cloned.1.call-update) | async-done | bytes 1048592 | tf_op jit(solution)/shard_map/all_gather | solution.py:59
  42.4 1.7 %convolution_bitcast_fusion = f32[2,1,128,512]{3,2,0,1:T(8,128)S(1)} fusion(bf16[2,512,128]{2,1,0:T(8,128)(2,1)} %bitcast.43, bf16[2,512,512]{2,1,0:T(8,128)(2,1)} %all-gather.3.cloned.1.call-done), kind=kOutput, calls=%fused_computation.15 | convolution fusion | flops 134217728 | bytes 1835008 | tf_op jit(solution)/shard_map/kji,kjl->kil/dot_general | solution.py:62
  44.2 0.5 convolution_bitcast_fusion.1
  44.7 0.3 add_convert_fusion
  45.0 1.1 broadcast_in_dim.32
  46.1 3.5 %all-to-all-start.1 = ((bf16[4,2,128,512]{3,2,1,0:T(8,128)(2,1)}), bf16[4,2,128,512]{3,2,1,0:T(8,128)(2,1)S(1)}, u32[]{:S(2)}, u32[]{:S(2)}) async-start(bf16[4,2,128,512]{3,2,1,0:T(8,128)(2,1)} %bitcast.6), calls=%async_computation.1 | async-start | bytes 2097152 | tf_op jit(solution)/shard_map/all_to_all | solution.py:69
  49.7 1.2 fusion.2
  50.9 13.2 %all-to-all-done.1 = bf16[4,2,128,512]{3,2,1,0:T(8,128)(2,1)S(1)} async-done(((bf16[4,2,128,512]{3,2,1,0:T(8,128)(2,1)}), bf16[4,2,128,512]{3,2,1,0:T(8,128)(2,1)S(1)}, u32[]{:S(2)}, u32[]{:S(2)}) %all-to-all-start.1) | async-done | bytes 1048608 | tf_op jit(solution)/shard_map/all_to_all | solution.py:69
  64.0 0.3 convert_bitcast_fusion
  64.5 0.4 fusion
  64.9 0.3 multiply_convert_fusion.2
  65.3 1.0 copy-done.4
  66.2 1.7 %convolution_convert_fusion.3 = bf16[2,512,512]{2,1,0:T(8,128)(2,1)} fusion(bf16[2,512,512]{2,1,0:T(8,128)(2,1)S(1)} %multiply_convert_fusion.2, f32[512,512]{1,0:T(8,128)S(1)} %copy-done.2), kind=kOutput, calls=%fused_computation.14 | convolution fusion | flops 539492352 | bytes 3145728 | tf_op jit(solution)/shard_map/sij,sjk->sik/dot_general | solution.py:29
  67.9 4.2 %multiply_convert_fusion = bf16[2,512,512]{2,1,0:T(8,128)(2,1)} fusion(bf16[2,512,512]{2,1,0:T(8,128)(2,1)} %convolution_convert_fusion.3, bf16[2,512,512]{2,1,0:T(8,128)(2,1)} %copy-done.4, f32[512,512]{1,0:T(8,128)S(1)} %copy-done.3), kind=kOutput, calls=%fused_computation.8 | convolution fusion | flops 1076887552 | bytes 4194304 | tf_op jit(solution)/shard_map/sij,sjk->sik/dot_general | solution.py:35
  72.2 2.3 %convolution_convert_fusion = bf16[2,512,512]{2,1,0:T(8,128)(2,1)S(1)} fusion(bf16[2,512,512]{2,1,0:T(8,128)(2,1)} %multiply_convert_fusion, bf16[2,512,512]{2,1,0:T(8,128)(2,1)} %copy-done.4, f32[512,512]{1,0:T(8,128)S(1)} %copy-done.3), kind=kOutput, calls=%fused_computation.11 | convolution fusion | flops 539492352 | bytes 4194304 | tf_op jit(solution)/shard_map/sij,sjk->sik/dot_general | solution.py:25
  74.4 1.0 copy-done.7
  75.4 2.5 %convolution_convert_fusion.4 = bf16[512,256]{1,0:T(8,128)(2,1)} fusion(bf16[2,512,512]{2,1,0:T(8,128)(2,1)} %copy-done.7, bf16[2,512,512]{2,1,0:T(8,128)(2,1)S(1)} %copy-done.1, s32[]{:T(128)S(6)} %select_n.76, bf16[1,512,512]{2,1,0:T(8,128)(2,1)S(1)} %slice.13, s32[]{:T(128)S(6)} %select_n.78), kind=kOutput, calls=%fused_computation.17 | convolution fusion | flops 268697600 | bytes 1572872 | tf_op jit(solution)/shard_map/dot_general | solution.py:76
  78.0 0.4 multiply_reduce_fusion.1
  78.3 16.6 %all-gather.5.cloned.1.call-done = bf16[512,1024]{1,0:T(8,128)(2,1)} async-done(((bf16[512,256]{1,0:T(8,128)(2,1)}), bf16[512,1024]{1,0:T(8,128)(2,1)}) %all-gather.5.cloned.1.call-update) | async-done | bytes 1048592 | tf_op jit(solution)/shard_map/all_gather | solution.py:79
  94.9 1.5 %multiply_reduce_fusion = f32[1024]{0:T(1024)S(1)} fusion(bf16[512,1024]{1,0:T(8,128)(2,1)} %all-gather.5.cloned.1.call-done), kind=kLoop, calls=%fused_computation.6 | loop fusion | flops 1571840 | bytes 1052672 | tf_op jit(solution)/shard_map/reduce_sum | solution.py:82
  96.4 1.8 %reshape.109 = bf16[512,2,512]{2,1,0:T(2,128)(2,1)S(1)} reshape(bf16[512,1024]{1,0:T(8,128)(2,1)} %all-gather.5.cloned.1.call-done) | data formatting | bytes 2097152 | tf_op jit(solution)/shard_map/reshape | solution.py:80
  98.7 0.7 copy.47
  99.4 5.5 %all-to-all-start.2 = ((bf16[8,64,2,128]{3,1,2,0:T(8,128)(2,1)}), bf16[8,64,2,128]{3,1,2,0:T(8,128)(2,1)S(1)}, u32[]{:S(2)}, u32[]{:S(2)}) async-start(bf16[8,64,2,128]{3,1,2,0:T(8,128)(2,1)} %copy.47), calls=%async_computation.2 | async-start | bytes 524288 | tf_op jit(solution)/shard_map/all_to_all | solution.py:87
  105.1 0.6 scatter_custom_fusion
  105.8 1.0 copy.49
  106.8 7.5 %all-to-all-done.2 = bf16[8,64,2,128]{3,1,2,0:T(8,128)(2,1)S(1)} async-done(((bf16[8,64,2,128]{3,1,2,0:T(8,128)(2,1)}), bf16[8,64,2,128]{3,1,2,0:T(8,128)(2,1)S(1)}, u32[]{:S(2)}, u32[]{:S(2)}) %all-to-all-start.2) | async-done | bytes 262176 | tf_op jit(solution)/shard_map/all_to_all | solution.py:87
  114.3 1.3 %gather_fusion.1 = bf16[16,64,128]{2,1,0:T(8,128)(2,1)} fusion(bf16[8,64,2,128]{3,1,2,0:T(8,128)(2,1)S(1)} %all-to-all-done.2, s32[16]{0:T(128)S(1)} %fusion.19), kind=kCustom, calls=%fused_computation.1 | custom fusion | bytes 524416 | tf_op jit(solution)/shard_map/gather | solution.py:96
  (39 shorter events, 1.3 us)
Async XLA Ops:
  7.2 1.8 %copy-start = (bf16[16,64,128]{2,1,0:T(8,128)(2,1)S(1)}, bf16[16,64,128]{2,1,0:T(8,128)(2,1)}, u32[]{:S(2)}) copy-start(bf16[16,64,128]{2,1,0:T(8,128)(2,1)} %param.4) | copy-start | bytes 786436
  7.2 35.2 %all-gather.3.cloned.1.call-start = ((), (), s32[]{:S(2)}) async-start(), calls=%async_computation.3 | async-start | bytes 1310720 | tf_op jit(solution)/shard_map/all_gather | solution.py:59
  26.4 18.3 %copy-start.5 = (f32[2,2,128,512]{3,2,1,0:T(8,128)S(1)}, f32[2,2,128,512]{3,2,1,0:T(8,128)}, u32[]{:S(2)}) copy-start(f32[2,2,128,512]{3,2,1,0:T(8,128)} %param.5) | copy-start | bytes 3145732
  42.4 1.8 %copy-start.1 = (bf16[2,512,512]{2,1,0:T(8,128)(2,1)S(1)}, bf16[2,512,512]{2,1,0:T(8,128)(2,1)}, u32[]{:S(2)}) copy-start(bf16[2,512,512]{2,1,0:T(8,128)(2,1)} %all-gather.3.cloned.1.call-done) | copy-start | bytes 3145732
  42.4 2.3 %copy-start.6 = (f32[128,512]{1,0:T(8,128)S(1)}, f32[128,512]{1,0:T(8,128)}, u32[]{:S(2)}) copy-start(f32[128,512]{1,0:T(8,128)} %fusion.12) | copy-start | bytes 786436
  46.1 17.9 %all-to-all-start.1 = ((bf16[4,2,128,512]{3,2,1,0:T(8,128)(2,1)}), bf16[4,2,128,512]{3,2,1,0:T(8,128)(2,1)S(1)}, u32[]{:S(2)}, u32[]{:S(2)}) async-start(bf16[4,2,128,512]{3,2,1,0:T(8,128)(2,1)} %bitcast.6), calls=%async_computation.1 | async-start | bytes 2097152 | tf_op jit(solution)/shard_map/all_to_all | solution.py:69
  49.6 45.3 %all-gather.5.cloned.1.call-start = ((), (), s32[]{:S(2)}) async-start(), calls=%async_computation.4 | async-start | bytes 1310720 | tf_op jit(solution)/shard_map/all_gather | solution.py:79
  64.5 1.7 %copy-start.2 = (f32[512,512]{1,0:T(8,128)S(1)}, f32[512,512]{1,0:T(8,128)}, u32[]{:S(2)}) copy-start(f32[512,512]{1,0:T(8,128)} %fusion.2) | copy-start | bytes 3145732
  65.2 1.0 copy-start.4
  66.2 1.7 %copy-start.3 = (f32[512,512]{1,0:T(8,128)S(1)}, f32[512,512]{1,0:T(8,128)}, u32[]{:S(2)}) copy-start(f32[512,512]{1,0:T(8,128)} %fusion.2) | copy-start | bytes 3145732
  74.4 1.0 copy-start.7
  99.4 14.8 %all-to-all-start.2 = ((bf16[8,64,2,128]{3,1,2,0:T(8,128)(2,1)}), bf16[8,64,2,128]{3,1,2,0:T(8,128)(2,1)S(1)}, u32[]{:S(2)}, u32[]{:S(2)}) async-start(bf16[8,64,2,128]{3,1,2,0:T(8,128)(2,1)} %copy.47), calls=%async_computation.2 | async-start | bytes 524288 | tf_op jit(solution)/shard_map/all_to_all | solution.py:87
Sparse Core Ops, SparseCore 0:
  26.5 15.8 all-gather.2
  78.1 16.8 all-gather.4
where the time goes:
time: 123 us; the launch traced here: 122 us
  waiting for transfers between devices  52.4 us (43%)
  blocking collectives  16 us (13%)
  between operations  15 us (12%)
  matrix products  12.9 us (10%)
  local copies, waits for them, and re-layouts  10.6 us (9%)
  starting transfers between devices  9.11 us (7%)
  other arithmetic  6.43 us (5%)
    all_gather x1, waiting for transfers between devices, body(): all_parts = lax.all_gather(result, 'mp', axis=1, tiled=True)  16.6 us
    all_to_all x1, blocking collectives, body(): lax.all_to_all(outgoing, 'dp', split_axis=1, concat_axis=1, tiled=True)  16 us
    all_gather x1, waiting for transfers between devices, body(): blocks = lax.all_gather(col_part, 'mp', axis=2, tiled=True)  15.2 us
    all_to_all x1, waiting for transfers between devices, body(): lax.all_to_all(spread_rows, 'mp', split_axis=0, concat_axis=2, tiled=True)  13.2 us
    all_to_all x1, waiting for transfers between devices, body(): lax.all_to_all(outgoing_back, 'dp', split_axis=0, concat_axis=0, tiled=True)  7.46 us
    all_to_all x1, starting transfers between devices, body(): lax.all_to_all(outgoing_back, 'dp', split_axis=0, concat_axis=0, tiled=True)  5.51 us
    dot_general x1, matrix products, newton_root(): jnp.einsum('sij,sjk->sik', square, partial_m, preferred_element_type=jnp....  4.21 us
    all_to_all x1, starting transfers between devices, body(): lax.all_to_all(spread_rows, 'mp', split_axis=0, concat_axis=2, tiled=True)  3.52 us
  transfers between devices with their start and end apart: 4, of which 4 were waited for; matrix products, arithmetic and copies ran while one was open for 3% of the time, Pallas kernels for 0%

commit v1 on v0

v1 whole, which is shorter than its diff:
```python
import functools

import jax
import jax.numpy as jnp
from jax import lax
from jax.experimental import pallas as pl
from jax.experimental.pallas import tpu as pltpu
from jax.sharding import PartitionSpec as P

ITERS = 2


decay_rate = 0.9
damping = 1.0
bf16 = jnp.bfloat16
f32 = jnp.float32

VMEM = pl.BlockSpec(memory_space=pltpu.VMEM)
SMEM = pl.BlockSpec(memory_space=pltpu.SMEM)


def owner_of(owners_ref, rot, o, s, dp_count):
    row = o - rot
    return owners_ref[s, jnp.where(row < 0, row + dp_count, row)]


def pick_kernel(owners_ref, rot_ref, tiles_ref, out_ref, *, dp_count, slots):
    rot = rot_ref[0]

    def one(j, carry):
        out_ref[j] = tiles_ref[owner_of(owners_ref, rot, j // slots, j % slots, dp_count)]
        return carry

    lax.fori_loop(0, dp_count * slots, one, 0, unroll=dp_count * slots <= 16)


def place_kernel(owners_ref, rot_ref, in_ref, out_ref, *, dp_count, slots):
    rot = rot_ref[0]

    def one(j, carry):
        out_ref[owner_of(owners_ref, rot, j // slots, j % slots, dp_count)] = in_ref[j]
        return carry

    lax.fori_loop(0, dp_count * slots, one, 0, unroll=dp_count * slots <= 16)


def dot(a, b, dims=(((1,), (0,)), ((), ()))):
    return lax.dot_general(a, b, dims, preferred_element_type=f32)


def newton_root(factor, eye5):
    norm = jnp.sum(jnp.square(factor.astype(f32)))
    moment = (2.5 / jnp.sqrt(norm) * factor.astype(f32)).astype(bf16)
    current = None
    for newton_step in range(ITERS):
        step_t = ((eye5 - moment.astype(f32)) * 0.25).astype(bf16)
        current = step_t if newton_step == 0 else dot(current, step_t).astype(bf16)
        if newton_step + 1 < ITERS:
            square = dot(step_t, step_t).astype(bf16)
            partial_m = dot(square, moment).astype(bf16)
            moment = dot(square, partial_m).astype(bf16)
    return current


def owner_kernel(*refs, n_g, n_s, dp_count, mp_count, slots, piece_rows, tile_cols, split):
    meta_ref, refs = refs[0], refs[1:]
    g_refs, refs = refs[:n_g], refs[n_g:]
    s_refs, refs = refs[:n_s], refs[n_s:]
    own_ref, out_ref, send_ref, new_ref, g_scr, s_scr, gram_scr, res_scr = refs
    order = g_scr.shape[0]
    rows = own_ref.shape[1]
    tile_rows = order // dp_count
    parts = mp_count // slots
    if split:
        for k, g_ref in enumerate(g_refs):
            at = pl.multiple_of(meta_ref[1 + k], piece_rows)
            for o in range(dp_count):
                for m in range(mp_count):
                    g_scr[pl.ds(o * tile_rows + at, piece_rows), m * tile_cols : (m + 1) * tile_cols] = g_ref[
                        o * mp_count + m
                    ]
    else:
        g_scr[...] = g_refs[0][...]
    for k, s_ref in enumerate(s_refs):
        at = pl.multiple_of(meta_ref[1 + parts + k], rows)
        s_scr[:, pl.ds(at, rows), :] = s_ref[...]
    own_at = pl.multiple_of(meta_ref[1 + parts + mp_count + slots - 1], rows)
    ids = lax.broadcasted_iota(jnp.int32, (order, order), 0)
    eye = ids == lax.broadcasted_iota(jnp.int32, (order, order), 1)
    roots = []
    for side in range(2):
        grad = g_scr[...]
        across = 1 - side
        gram_scr[side] = dot(grad, grad, (((across,), (across,)), ((), ())))
        for k in range(slots - 1):
            at = pl.multiple_of(meta_ref[1 + parts + mp_count + k], rows)
            send_ref[k, side] = gram_scr[side, pl.ds(at, rows), :].astype(bf16)
        new_ref[side] = decay_rate * own_ref[side] + (1.0 - decay_rate) * gram_scr[side, pl.ds(own_at, rows), :]
        updated = decay_rate * s_scr[side].astype(f32) + (1.0 - decay_rate) * gram_scr[side]
        factor = (updated + jnp.where(eye, damping, 0.0)).astype(bf16)
        roots.append(newton_root(factor, jnp.where(eye, 5.0, 0.0)))
    right_applied = dot(g_scr[...], roots[1]).astype(bf16)
    result = dot(roots[0], right_applied).astype(bf16).astype(f32)
    grad_norm = jnp.sqrt(jnp.sum(jnp.square(g_scr[...].astype(f32))))
    result_norm = jnp.sqrt(jnp.sum(jnp.square(result)))
    res_scr[...] = (result * (grad_norm / (result_norm + 1e-06))).astype(bf16)
    if split:
        at = pl.multiple_of(meta_ref[0] * piece_rows, piece_rows)
        for o in range(dp_count):
            for m in range(mp_count):
                out_ref[o * mp_count + m] = res_scr[
                    pl.ds(o * tile_rows + at, piece_rows), m * tile_cols : (m + 1) * tile_cols
                ]
    else:
        out_ref[...] = res_scr[...]


def body(grad_tiles, factor_stats, owner_blocks, rotation):
    dp_count = lax.axis_size("dp")
    mp_count = lax.axis_size("mp")
    block_count, tile_rows, tile_cols = grad_tiles.shape
    slots = owner_blocks.shape[1]
    rows, order = factor_stats.shape[2:]
    parts = mp_count // slots
    piece_rows = tile_rows // parts
    split = piece_rows % 16 == 0 and tile_cols % 128 == 0
    my_index = lax.axis_index("mp")
    my_slot = my_index // parts
    my_part = my_index % parts
    owners = owner_blocks.T
    sizes = dict(dp_count=dp_count, slots=slots)

    def to_slot(x, ahead):
        return lax.ppermute(x, "mp", [(i, (i + ahead * parts) % mp_count) for i in range(mp_count)])

    def to_part(x, ahead):
        return lax.ppermute(
            x, "mp", [(i, i // parts * parts + (i + ahead) % parts) for i in range(mp_count)]
        )

    def slot_stats(ahead):
        return lax.dynamic_index_in_dim(factor_stats, (my_slot + ahead) % slots, 0, keepdims=False)

    chunks = [slot_stats(0).astype(bf16)]
    chunk_of = [my_index]
    for ahead in range(1, slots):
        chunks.append(to_slot(slot_stats(ahead).astype(bf16), ahead))
        chunk_of.append((my_slot - ahead) % slots * parts + my_part)
    for ahead in range(1, parts):
        for k in range(slots):
            chunks.append(to_part(chunks[k], ahead))
            chunk_of.append(chunk_of[k] // parts * parts + (my_part - ahead) % parts)

    picked = pl.pallas_call(
        functools.partial(pick_kernel, **sizes),
        out_shape=jax.ShapeDtypeStruct(grad_tiles.shape, bf16),
        in_specs=[SMEM, SMEM, VMEM],
        out_specs=VMEM,
    )(owners, rotation, grad_tiles)
    outgoing = picked.reshape(dp_count * mp_count, piece_rows, tile_cols)
    arrived = lax.all_to_all(outgoing, ("dp", "mp"), split_axis=0, concat_axis=0, tiled=True)
    pieces = [arrived] + [to_part(arrived, ahead) for ahead in range(1, parts)]
    if not split:
        held = jnp.take(jnp.stack(pieces), (my_part - jnp.arange(parts)) % parts, axis=0)
        held = held.reshape(parts, dp_count, mp_count, piece_rows, tile_cols)
        pieces = [held.transpose(1, 0, 3, 2, 4).reshape(order, order)]

    meta = jnp.stack(
        [my_part]
        + [(my_part - k) % parts * piece_rows for k in range(parts)]
        + [c * rows for c in chunk_of]
        + [((my_slot + k) % slots * parts + my_part) * rows for k in range(1, slots)]
        + [my_index * rows]
    ).astype(jnp.int32)
    result_shape = (dp_count * mp_count, piece_rows, tile_cols) if split else (order, order)
    result, gram_rows, own_rows = pl.pallas_call(
        functools.partial(
            owner_kernel,
            n_g=len(pieces),
            n_s=len(chunks),
            mp_count=mp_count,
            piece_rows=piece_rows,
            tile_cols=tile_cols,
            split=split,
            **sizes,
        ),
        out_shape=(
            jax.ShapeDtypeStruct(result_shape, bf16),
            jax.ShapeDtypeStruct((slots - 1, 2, rows, order), bf16),
            jax.ShapeDtypeStruct((2, rows, order), f32),
        ),
        in_specs=[SMEM] + [VMEM] * (len(pieces) + len(chunks) + 1),
        out_specs=(VMEM, VMEM, VMEM),
        scratch_shapes=[
            pltpu.VMEM((order, order), bf16),
            pltpu.VMEM((2, order, order), bf16),
            pltpu.VMEM((2, order, order), f32),
            pltpu.VMEM((order, order), bf16),
        ],
    )(meta, *pieces, *chunks, slot_stats(0))
    if not split:
        result = result.reshape(dp_count, parts, piece_rows, mp_count, tile_cols)
        result = lax.dynamic_index_in_dim(result, my_part, 1, keepdims=False)
        result = result.transpose(0, 2, 1, 3).reshape(dp_count * mp_count, piece_rows, tile_cols)

    stats_rows = [own_rows]
    for ahead in range(1, slots):
        theirs = to_slot(gram_rows[ahead - 1], ahead).astype(f32)
        stats_rows.append(decay_rate * slot_stats(-ahead) + (1.0 - decay_rate) * theirs)
    if slots == 2:
        new_stats = jnp.stack(
            [jnp.where(my_slot == s, stats_rows[0], stats_rows[1]) for s in range(2)]
        )
    else:
        new_stats = jnp.take(jnp.stack(stats_rows), (my_slot - jnp.arange(slots)) % slots, axis=0)

    returned = lax.all_to_all(result, ("dp", "mp"), split_axis=0, concat_axis=0, tiled=True)
    preconditioned = pl.pallas_call(
        functools.partial(place_kernel, **sizes),
        out_shape=jax.ShapeDtypeStruct(grad_tiles.shape, bf16),
        in_specs=[SMEM, SMEM, VMEM],
        out_specs=VMEM,
    )(owners, rotation, returned.reshape(grad_tiles.shape))
    return (preconditioned, new_stats)


def solution(mesh):
    return jax.shard_map(
        body,
        mesh=mesh,
        in_specs=(P(None, "dp", "mp"), P("dp", None, "mp", None), P(), P()),
        out_specs=(P(None, "dp", "mp"), P("dp", None, "mp", None)),
        check_vma=False,
    )
```

time: 123 us -> 51.9 us (0.42)
  waiting for transfers between devices: 52.4 us -> 18.5 us
  blocking collectives: 16 us -> 0 us
  between operations: 15 us -> 1.5 us
  matrix products: 12.9 us -> 0 us
  Pallas kernels: 0 us -> 11.6 us
  local copies, waits for them, and re-layouts: 10.6 us -> 2.15 us
  starting transfers between devices: 9.11 us -> 15.7 us
  other arithmetic: 6.43 us -> 2.08 us
    all_gather x2 -> x0, waiting for transfers between devices: 31.8 us -> none  [the longest x1 16.6 us: body(): all_parts = lax.all_gather(result, 'mp', axis=1, tiled=True)]
    all_to_all x1 -> x0, blocking collectives: 16 us -> none  [body(): lax.all_to_all(outgoing, 'dp', split_axis=1, concat_axis=1, tiled=True)]
    all_to_all x2, waiting for transfers between devices: 20.6 us -> 6.84 us  [the longest x1 6.83 us: body(): lax.all_to_all(result, ('dp', 'mp'), split_axis=0, concat_axis=0, tiled=T...]
    dot_general x6 -> x0, matrix products: 12.9 us -> none  [the longest x1 4.21 us: newton_root(): jnp.einsum('sij,sjk->sik', square, partial_m, preferred_element_type=jnp....]
    ppermute x0 -> x5, waiting for transfers between devices: none -> 11.7 us  [the longest x2 11 us: to_slot(): lax.ppermute(x, 'mp', [(i, (i + ahead * parts) % mp_count) for i in range...]
    pallas_call x0 -> x3, Pallas kernels: none -> 11.6 us  [the longest x1 8.23 us: body(): pl.pallas_call(functools.partial(owner_kernel, n_g=len(pieces), n_s=len(c...]
    ppermute x0 -> x5, starting transfers between devices: none -> 3.61 us  [the longest x2 3.11 us: to_slot(): lax.ppermute(x, 'mp', [(i, (i + ahead * parts) % mp_count) for i in range...]
    all_to_all x2, starting transfers between devices: 9.03 us -> 12.1 us  [the longest x1 7.33 us: body(): lax.all_to_all(outgoing, ('dp', 'mp'), split_axis=0, concat_axis=0, tiled...]
  transfers between devices with their start and end apart: 4 -> 7, of which waited for: 4 -> 5; matrix products, arithmetic and copies ran while one was open for 3% -> 5% of each run, Pallas kernels for 0% -> 0%
where the time goes in v1:
time: 51.9 us; the launch traced here: 51.5 us
  waiting for transfers between devices  18.5 us (36%)
  starting transfers between devices  15.7 us (30%)
  Pallas kernels  11.6 us (22%)
  local copies, waits for them, and re-layouts  2.15 us (4%)
  other arithmetic  2.08 us (4%)
  between operations  1.5 us (3%)
    ppermute x2, waiting for transfers between devices, to_slot(): lax.ppermute(x, 'mp', [(i, (i + ahead * parts) % mp_count) for i in range...  11 us
    pallas_call x1, Pallas kernels, body(): pl.pallas_call(functools.partial(owner_kernel, n_g=len(pieces), n_s=len(c...  8.23 us
    all_to_all x1, starting transfers between devices, body(): lax.all_to_all(outgoing, ('dp', 'mp'), split_axis=0, concat_axis=0, tiled...  7.33 us
    all_to_all x1, waiting for transfers between devices, body(): lax.all_to_all(result, ('dp', 'mp'), split_axis=0, concat_axis=0, tiled=T...  6.83 us
    all_to_all x1, starting transfers between devices, body(): lax.all_to_all(result, ('dp', 'mp'), split_axis=0, concat_axis=0, tiled=T...  4.77 us
    ppermute x2, starting transfers between devices, to_slot(): lax.ppermute(x, 'mp', [(i, (i + ahead * parts) % mp_count) for i in range...  3.11 us
    pallas_call x1, Pallas kernels, body(): pl.pallas_call(functools.partial(pick_kernel, **sizes), out_shape=jax.Sha...  1.7 us
    pallas_call x1, Pallas kernels, body(): pl.pallas_call(functools.partial(place_kernel, **sizes), out_shape=jax.Sh...  1.7 us
  transfers between devices with their start and end apart: 7, of which 5 were waited for; matrix products, arithmetic and copies ran while one was open for 5% of the time, Pallas kernels for 0%

profile of v1, /device:TPU:0, one launch (start us, length us, event | category | flops | bytes accessed | tf_op | source)
XLA Modules:
  0.0 51.5 jit_solution(15987329316669109713)
XLA Ops:
  0.6 0.0 copy-start
  1.4 1.7 %shard_map.59 = bf16[16,64,128]{2,1,0:T(8,128)(2,1)} custom-call(s32[2,8]{1,0:T(2,128)} %bitcast.29, s32[1]{0:T(128)S(6)} %copy.6.rot_ref, bf16[16,64,128]{2,1,0:T(8,128)(2,1)} %tiles_ref.1), custom_call_target="tpu_custom_call" | custom-call | tf_op jit(solution)/shard_map/pallas_call | solution.py:154
  3.1 7.3 %all-to-all-start = ((bf16[32,32,128]{2,1,0:T(8,128)(2,1)}), bf16[32,32,128]{2,1,0:T(8,128)(2,1)S(1)}, u32[]{:S(2)}, u32[]{:S(2)}) async-start(bf16[32,32,128]{2,1,0:T(8,128)(2,1)} %bitcast.27), calls=%async_computation | async-start | bytes 524288 | tf_op jit(solution)/shard_map/all_to_all | solution.py:161
  10.4 0.0 copy-done
  10.5 1.8 %collective-permute-start.1 = (bf16[2,128,512]{2,1,0:T(8,128)(2,1)S(1)}, bf16[2,128,512]{2,1,0:T(8,128)(2,1)S(1)}, u32[]{:S(2)}, u32[]{:S(2)}) collective-permute-start(bf16[2,128,512]{2,1,0:T(8,128)(2,1)S(1)} %fusion), channel_id=1, source_target_pairs={{0,2},{1,3},{2,0},{3,1},{4,6},{5,7},{6,4},{7,5},{8,10},{9,11},{10,... | collective-permute-start | bytes 786440 | tf_op jit(solution)/shard_map/ppermute | solution.py:134
  12.3 0.9 %fusion.1 = (bf16[2,128,512]{2,1,0:T(8,128)(2,1)S(1)}, f32[2,128,512]{2,1,0:T(8,128)}) fusion(f32[2,2,128,512]{3,2,1,0:T(8,128)S(1)} %copy-done, s32[]{:T(128)S(6)} %select_n.78), kind=kLoop, calls=%fused_computation.7 | loop fusion | flops 131072 | bytes 1310724 | tf_op jit(solution)/shard_map/convert_element_type | solution.py:144
  13.2 0.0 collective-permute-start.2
  13.2 8.5 %collective-permute-done.1.refs_4_ = bf16[2,128,512]{2,1,0:T(8,128)(2,1)S(1)} collective-permute-done((bf16[2,128,512]{2,1,0:T(8,128)(2,1)S(1)}, bf16[2,128,512]{2,1,0:T(8,128)(2,1)S(1)}, u32[]{:S(2)}, u32[]{:S(2)}) %collective-permute-start.1) | collective-permute-done | bytes 262176 | tf_op jit(solution)/shard_map/ppermute | solution.py:134
  21.7 0.0 collective-permute-start.3
  21.7 0.0 all-to-all-done.refs_1_
  21.7 0.0 copy-start.2
  21.7 0.5 collective-permute-start
  22.2 0.7 %stack.45.refs_0_ = s32[9]{0:T(128)} concatenate(s32[1]{0:T(128)} %bitcast.1, s32[1]{0:T(128)} %bitcast.2, s32[1]{0:T(128)} %bitcast.3, s32[1]{0:T(128)} %bitcast.4, s32[1]{0:T(128)} %bitcast.5, s32[1]{0:T(128)} %bitcast.6, s32[1]{0:T(128)} %bitcast.7, s32[1]{0:T(128)} %bitcast.8, s32[1]{0:T(128)} %bitcast.4), dimensions={0} | concatenate | bytes 72 | tf_op jit(solution)/shard_map/stack | solution.py:168
  22.9 0.0 collective-permute-done.2.refs_5_
  22.9 0.3 collective-permute-done.3.refs_6_
  23.2 0.4 collective-permute-done.refs_2_
  23.6 0.0 copy-done.1
  23.6 0.0 copy-done.5
  23.6 0.0 copy-done.2
  23.6 0.0 copy-done.6
  23.6 0.3 copy-done.7
  23.9 0.4 copy-done.8
  24.3 8.2 %shard_map.60 = (bf16[32,32,128]{2,1,0:T(8,128)(2,1)}, bf16[1,2,128,512]{3,2,1,0:T(8,128)(2,1)}, f32[2,128,512]{2,1,0:T(8,128)}) custom-call(s32[9]{0:T(128)} %stack.45.refs_0_, bf16[32,32,128]{2,1,0:T(8,128)(2,1)} %copy-done.2, bf16[32,32,128]{2,1,0:T(8,128)(2,1)} %copy-done.8, bf16[2,128,512]{2,1,0:T(8,128)(2,1)} %copy-done.1, ...), custom_call_target="tpu_custom_call" | custom-call | tf_op jit(solution)/shard_map/pallas_call | solution.py:176
  32.5 1.3 %collective-permute-start.4 = (bf16[2,128,512]{2,1,0:T(8,128)(2,1)}, bf16[2,128,512]{2,1,0:T(8,128)(2,1)S(1)}, u32[]{:S(2)}, u32[]{:S(2)}) collective-permute-start(bf16[2,128,512]{2,1,0:T(8,128)(2,1)} %bitcast.31), channel_id=1, source_target_pairs={{0,2},{1,3},{2,0},{3,1},{4,6},{5,7},{6,4},{7,5},{8,10},{9,11},{10,... | collective-permute-start | bytes 786440 | tf_op jit(solution)/shard_map/ppermute | solution.py:134
  33.8 4.8 %all-to-all-start.1 = ((bf16[32,32,128]{2,1,0:T(8,128)(2,1)}), bf16[32,32,128]{2,1,0:T(8,128)(2,1)S(1)}, u32[]{:S(2)}, u32[]{:S(2)}) async-start(bf16[32,32,128]{2,1,0:T(8,128)(2,1)} %get-tuple-element.5), calls=%async_computation.1 | async-start | bytes 524288 | tf_op jit(solution)/shard_map/all_to_all | solution.py:217
  38.6 2.5 %collective-permute-done.4 = bf16[2,128,512]{2,1,0:T(8,128)(2,1)S(1)} collective-permute-done((bf16[2,128,512]{2,1,0:T(8,128)(2,1)}, bf16[2,128,512]{2,1,0:T(8,128)(2,1)S(1)}, u32[]{:S(2)}, u32[]{:S(2)}) %collective-permute-start.4) | collective-permute-done | bytes 262176 | tf_op jit(solution)/shard_map/ppermute | solution.py:134
  41.1 0.0 copy-done.4
  41.1 0.2 select_bitcast_fusion.1
  41.3 1.0 %pad_maximum_fusion = f32[2,2,128,512]{3,2,1,0:T(8,128)} fusion(f32[1,2,128,512]{3,2,1,0:T(8,128)S(1)} %get-tuple-element.11, f32[1,2,128,512]{3,2,1,0:T(8,128)S(1)} %get-tuple-element.10), kind=kLoop, calls=%fused_computation | loop fusion | flops 262144 | bytes 2097152 | tf_op jit(solution)/shard_map/stack | solution.py:211
  42.3 6.8 %all-to-all-done.1 = bf16[32,32,128]{2,1,0:T(8,128)(2,1)S(1)} async-done(((bf16[32,32,128]{2,1,0:T(8,128)(2,1)}), bf16[32,32,128]{2,1,0:T(8,128)(2,1)S(1)}, u32[]{:S(2)}, u32[]{:S(2)}) %all-to-all-start.1) | async-done | bytes 262176 | tf_op jit(solution)/shard_map/all_to_all | solution.py:217
  49.2 0.7 %copy-done.3 = bf16[32,32,128]{2,1,0:T(8,128)(2,1)} copy-done((bf16[32,32,128]{2,1,0:T(8,128)(2,1)}, bf16[32,32,128]{2,1,0:T(8,128)(2,1)S(1)}, u32[]{:S(2)}) %copy-start.3) | copy-done | bytes 262168
  49.9 1.7 %shard_map.61 = bf16[16,64,128]{2,1,0:T(8,128)(2,1)} custom-call(s32[2,8]{1,0:T(2,128)} %bitcast.30, s32[1]{0:T(128)S(6)} %copy.6.rot_ref, bf16[16,64,128]{2,1,0:T(8,128)(2,1)} %bitcast.28), custom_call_target="tpu_custom_call" | custom-call | tf_op jit(solution)/shard_map/pallas_call | solution.py:218
  (8 shorter events, 0.1 us)
Async XLA Ops:
  0.6 9.8 %copy-start = (f32[2,2,128,512]{3,2,1,0:T(8,128)S(1)}, f32[2,2,128,512]{3,2,1,0:T(8,128)}, u32[]{:S(2)}) copy-start(f32[2,2,128,512]{3,2,1,0:T(8,128)} %param.5) | copy-start | bytes 3145732
  3.1 18.6 %all-to-all-start = ((bf16[32,32,128]{2,1,0:T(8,128)(2,1)}), bf16[32,32,128]{2,1,0:T(8,128)(2,1)S(1)}, u32[]{:S(2)}, u32[]{:S(2)}) async-start(bf16[32,32,128]{2,1,0:T(8,128)(2,1)} %bitcast.27), calls=%async_computation | async-start | bytes 524288 | tf_op jit(solution)/shard_map/all_to_all | solution.py:161
  10.5 11.2 %collective-permute-start.1 = (bf16[2,128,512]{2,1,0:T(8,128)(2,1)S(1)}, bf16[2,128,512]{2,1,0:T(8,128)(2,1)S(1)}, u32[]{:S(2)}, u32[]{:S(2)}) collective-permute-start(bf16[2,128,512]{2,1,0:T(8,128)(2,1)S(1)} %fusion), channel_id=1, source_target_pairs={{0,2},{1,3},{2,0},{3,1},{4,6},{5,7},{6,4},{7,5},{8,10},{9,11},{10,... | collective-permute-start | bytes 786440 | tf_op jit(solution)/shard_map/ppermute | solution.py:134
  13.2 10.4 %copy-start.1 = (bf16[2,128,512]{2,1,0:T(8,128)(2,1)}, bf16[2,128,512]{2,1,0:T(8,128)(2,1)S(1)}, u32[]{:S(2)}) copy-start(bf16[2,128,512]{2,1,0:T(8,128)(2,1)S(1)} %get-tuple-element.8.refs_3_) | copy-start | bytes 786436
  13.2 9.7 %collective-permute-start.2 = (bf16[2,128,512]{2,1,0:T(8,128)(2,1)S(1)}, bf16[2,128,512]{2,1,0:T(8,128)(2,1)S(1)}, u32[]{:S(2)}, u32[]{:S(2)}) collective-permute-start(bf16[2,128,512]{2,1,0:T(8,128)(2,1)S(1)} %get-tuple-element.8.refs_3_), channel_id=1, source_target_pairs={{0,1},{1,0},{2,3},{3,2},{4,5},{5,4},{6,7},{7,6},{8,9},{9,8},{10,11... | collective-permute-start | bytes 786440 | tf_op jit(solution)/shard_map/ppermute | solution.py:137
  21.7 1.9 %copy-start.5 = (bf16[2,128,512]{2,1,0:T(8,128)(2,1)}, bf16[2,128,512]{2,1,0:T(8,128)(2,1)S(1)}, u32[]{:S(2)}) copy-start(bf16[2,128,512]{2,1,0:T(8,128)(2,1)S(1)} %collective-permute-done.1.refs_4_) | copy-start | bytes 786436
  21.7 1.5 %collective-permute-start.3 = (bf16[2,128,512]{2,1,0:T(8,128)(2,1)S(1)}, bf16[2,128,512]{2,1,0:T(8,128)(2,1)S(1)}, u32[]{:S(2)}, u32[]{:S(2)}) collective-permute-start(bf16[2,128,512]{2,1,0:T(8,128)(2,1)S(1)} %collective-permute-done.1.refs_4_), channel_id=1, source_target_pairs={{0,1},{1,0},{2,3},{3,2},{4,5},{5,4},{6,7},{7,6},{8,9},{9,8},{10,11... | collective-permute-start | bytes 786440 | tf_op jit(solution)/shard_map/ppermute | solution.py:137
  21.7 1.9 %copy-start.2 = (bf16[32,32,128]{2,1,0:T(8,128)(2,1)}, bf16[32,32,128]{2,1,0:T(8,128)(2,1)S(1)}, u32[]{:S(2)}) copy-start(bf16[32,32,128]{2,1,0:T(8,128)(2,1)S(1)} %all-to-all-done.refs_1_) | copy-start | bytes 786436
  21.7 1.9 %collective-permute-start = (bf16[32,32,128]{2,1,0:T(8,128)(2,1)S(1)}, bf16[32,32,128]{2,1,0:T(8,128)(2,1)S(1)}, u32[]{:S(2)}, u32[]{:S(2)}) collective-permute-start(bf16[32,32,128]{2,1,0:T(8,128)(2,1)S(1)} %all-to-all-done.refs_1_), channel_id=1, source_target_pairs={{0,1},{1,0},{2,3},{3,2},{4,5},{5,4},{6,7},{7,6},{8,9},{9,8},{10,11... | collective-permute-start | bytes 786440 | tf_op jit(solution)/shard_map/ppermute | solution.py:137
  22.9 0.7 %copy-start.6 = (bf16[2,128,512]{2,1,0:T(8,128)(2,1)}, bf16[2,128,512]{2,1,0:T(8,128)(2,1)S(1)}, u32[]{:S(2)}) copy-start(bf16[2,128,512]{2,1,0:T(8,128)(2,1)S(1)} %collective-permute-done.2.refs_5_) | copy-start | bytes 786436
  23.2 0.7 %copy-start.7 = (bf16[2,128,512]{2,1,0:T(8,128)(2,1)}, bf16[2,128,512]{2,1,0:T(8,128)(2,1)S(1)}, u32[]{:S(2)}) copy-start(bf16[2,128,512]{2,1,0:T(8,128)(2,1)S(1)} %collective-permute-done.3.refs_6_) | copy-start | bytes 786436
  23.6 0.7 %copy-start.8 = (bf16[32,32,128]{2,1,0:T(8,128)(2,1)}, bf16[32,32,128]{2,1,0:T(8,128)(2,1)S(1)}, u32[]{:S(2)}) copy-start(bf16[32,32,128]{2,1,0:T(8,128)(2,1)S(1)} %collective-permute-done.refs_2_) | copy-start | bytes 786436
  32.5 8.6 %copy-start.4 = (f32[2,128,512]{2,1,0:T(8,128)S(1)}, f32[2,128,512]{2,1,0:T(8,128)}, u32[]{:S(2)}) copy-start(f32[2,128,512]{2,1,0:T(8,128)} %get-tuple-element.6) | copy-start | bytes 1572868
  32.5 8.6 %collective-permute-start.4 = (bf16[2,128,512]{2,1,0:T(8,128)(2,1)}, bf16[2,128,512]{2,1,0:T(8,128)(2,1)S(1)}, u32[]{:S(2)}, u32[]{:S(2)}) collective-permute-start(bf16[2,128,512]{2,1,0:T(8,128)(2,1)} %bitcast.31), channel_id=1, source_target_pairs={{0,2},{1,3},{2,0},{3,1},{4,6},{5,7},{6,4},{7,5},{8,10},{9,11},{10,... | collective-permute-start | bytes 786440 | tf_op jit(solution)/shard_map/ppermute | solution.py:134
  33.8 15.4 %all-to-all-start.1 = ((bf16[32,32,128]{2,1,0:T(8,128)(2,1)}), bf16[32,32,128]{2,1,0:T(8,128)(2,1)S(1)}, u32[]{:S(2)}, u32[]{:S(2)}) async-start(bf16[32,32,128]{2,1,0:T(8,128)(2,1)} %get-tuple-element.5), calls=%async_computation.1 | async-start | bytes 524288 | tf_op jit(solution)/shard_map/all_to_all | solution.py:217
  49.2 0.7 %copy-start.3 = (bf16[32,32,128]{2,1,0:T(8,128)(2,1)}, bf16[32,32,128]{2,1,0:T(8,128)(2,1)S(1)}, u32[]{:S(2)}) copy-start(bf16[32,32,128]{2,1,0:T(8,128)(2,1)S(1)} %all-to-all-done.1) | copy-start | bytes 786436

commit v2 on v1

v2 whole, which is shorter than its diff:
```python
import functools

import jax
import jax.numpy as jnp
from jax import lax
from jax.experimental import pallas as pl
from jax.experimental.pallas import tpu as pltpu
from jax.sharding import PartitionSpec as P

ITERS = 2


decay_rate = 0.9
damping = 1.0
bf16 = jnp.bfloat16
f32 = jnp.float32

VMEM = pl.BlockSpec(memory_space=pltpu.VMEM)
SMEM = pl.BlockSpec(memory_space=pltpu.SMEM)


def owner_of(owners_ref, rot, o, s, dp_count):
    row = o - rot
    return owners_ref[s, jnp.where(row < 0, row + dp_count, row)]


def pick_kernel(owners_ref, rot_ref, tiles_ref, out_ref, *, dp_count, slots):
    rot = rot_ref[0]

    def one(j, carry):
        out_ref[j] = tiles_ref[owner_of(owners_ref, rot, j // slots, j % slots, dp_count)]
        return carry

    lax.fori_loop(0, dp_count * slots, one, 0, unroll=dp_count * slots <= 16)


def place_kernel(owners_ref, rot_ref, in_ref, out_ref, *, dp_count, slots):
    rot = rot_ref[0]

    def one(j, carry):
        out_ref[owner_of(owners_ref, rot, j // slots, j % slots, dp_count)] = in_ref[j]
        return carry

    lax.fori_loop(0, dp_count * slots, one, 0, unroll=dp_count * slots <= 16)


def dot(a, b, dims=(((1,), (0,)), ((), ()))):
    return lax.dot_general(a, b, dims, preferred_element_type=f32)


def newton_root(factor, eye5):
    norm = jnp.sum(jnp.square(factor.astype(f32)))
    moment = (2.5 / jnp.sqrt(norm) * factor.astype(f32)).astype(bf16)
    current = None
    for newton_step in range(ITERS):
        step_t = ((eye5 - moment.astype(f32)) * 0.25).astype(bf16)
        current = step_t if newton_step == 0 else dot(current, step_t).astype(bf16)
        if newton_step + 1 < ITERS:
            square = dot(step_t, step_t).astype(bf16)
            partial_m = dot(square, moment).astype(bf16)
            moment = dot(square, partial_m).astype(bf16)
    return current


def gather_grad(g_refs, g_scr, part, *, dp_count, mp_count, parts, piece_rows, tile_cols):
    for k, g_ref in enumerate(g_refs):
        piece = part - k
        at = pl.multiple_of(jnp.where(piece < 0, piece + parts, piece) * piece_rows, piece_rows)
        for o in range(dp_count):
            for m in range(mp_count):
                rows = pl.ds(o * parts * piece_rows + at, piece_rows)
                g_scr[rows, m * tile_cols : (m + 1) * tile_cols] = g_ref[o * mp_count + m]


def owner_kernel(*refs, n_g, split, sizes):
    g_refs, refs = refs[:n_g], refs[n_g:]
    s_refs, (out_ref, g_scr, s_scr, res_scr) = refs[:-4], refs[-4:]
    dp_count, mp_count, parts = sizes["dp_count"], sizes["mp_count"], sizes["parts"]
    piece_rows, tile_cols = sizes["piece_rows"], sizes["tile_cols"]
    slots = mp_count // parts
    order = g_scr.shape[0]
    rows = s_refs[0].shape[1]
    my_index = lax.axis_index("mp")
    slot, part = my_index // parts, my_index % parts
    if split:
        gather_grad(g_refs, g_scr, part, **sizes)
    else:
        g_scr[...] = g_refs[0][...]
    for k in range(parts):
        for j in range(slots):
            chunk = (slot - j + slots) % slots * parts + (part - k + parts) % parts
            s_scr[:, pl.ds(pl.multiple_of(chunk * rows, rows), rows), :] = s_refs[k * slots + j][...]
    ids = lax.broadcasted_iota(jnp.int32, (order, order), 0)
    eye = ids == lax.broadcasted_iota(jnp.int32, (order, order), 1)
    grad = g_scr[...]
    roots = []
    for side in range(2):
        across = 1 - side
        gram = dot(grad, grad, (((across,), (across,)), ((), ())))
        updated = decay_rate * s_scr[side].astype(f32) + (1.0 - decay_rate) * gram
        factor = (updated + jnp.where(eye, damping, 0.0)).astype(bf16)
        roots.append(newton_root(factor, jnp.where(eye, 5.0, 0.0)))
    right_applied = dot(grad, roots[1]).astype(bf16)
    result = dot(roots[0], right_applied).astype(bf16).astype(f32)
    grad_norm = jnp.sqrt(jnp.sum(jnp.square(grad.astype(f32))))
    result_norm = jnp.sqrt(jnp.sum(jnp.square(result)))
    res_scr[...] = (result * (grad_norm / (result_norm + 1e-06))).astype(bf16)
    if split:
        at = pl.multiple_of(part * piece_rows, piece_rows)
        for o in range(dp_count):
            for m in range(mp_count):
                from_rows = pl.ds(o * parts * piece_rows + at, piece_rows)
                out_ref[o * mp_count + m] = res_scr[from_rows, m * tile_cols : (m + 1) * tile_cols]
    else:
        out_ref[...] = res_scr[...]


def stats_kernel(*refs, sizes):
    g_refs, (old_ref, new_ref, g_scr) = refs[:-3], refs[-3:]
    parts = sizes["parts"]
    slots = sizes["mp_count"] // parts
    rows = old_ref.shape[2]
    my_index = lax.axis_index("mp")
    at = pl.multiple_of(my_index * rows, rows)
    for j in range(slots):
        gather_grad(g_refs[j * parts : (j + 1) * parts], g_scr.at[j], my_index % parts, **sizes)
        slot = (my_index // parts - j + slots) % slots
        left = dot(g_scr[j, pl.ds(at, rows), :], g_scr[j], (((1,), (1,)), ((), ())))
        right = dot(g_scr[j, :, pl.ds(at, rows)], g_scr[j], (((0,), (0,)), ((), ())))
        new_ref[slot, 0] = decay_rate * old_ref[slot, 0] + (1.0 - decay_rate) * left
        new_ref[slot, 1] = decay_rate * old_ref[slot, 1] + (1.0 - decay_rate) * right


def call(kernel, out_shape, in_specs, scratch=(), vmem=16, flops=0):
    return pl.pallas_call(
        kernel,
        out_shape=out_shape,
        in_specs=in_specs,
        out_specs=VMEM,
        scratch_shapes=list(scratch),
        compiler_params=pltpu.CompilerParams(vmem_limit_bytes=vmem * 2**20),
        cost_estimate=pl.CostEstimate(flops=flops, transcendentals=0, bytes_accessed=0) if flops else None,
    )


def body(grad_tiles, factor_stats, owner_blocks, rotation):
    dp_count = lax.axis_size("dp")
    mp_count = lax.axis_size("mp")
    tile_rows, tile_cols = grad_tiles.shape[1:]
    slots = owner_blocks.shape[1]
    rows, order = factor_stats.shape[2:]
    parts = mp_count // slots
    piece_rows = tile_rows // parts
    split = piece_rows % 16 == 0 and tile_cols % 128 == 0 and rows == tile_cols
    my_index = lax.axis_index("mp")
    my_slot = my_index // parts
    my_part = my_index % parts
    owners = owner_blocks.T
    where = dict(dp_count=dp_count, slots=slots)
    sizes = dict(
        dp_count=dp_count, mp_count=mp_count, parts=parts, piece_rows=piece_rows, tile_cols=tile_cols
    )

    def to_slot(x, ahead):
        return lax.ppermute(x, "mp", [(i, (i + ahead * parts) % mp_count) for i in range(mp_count)])

    def to_part(x, ahead):
        return lax.ppermute(
            x, "mp", [(i, i // parts * parts + (i + ahead) % parts) for i in range(mp_count)]
        )

    def all_pieces(x):
        return [x] + [to_part(x, ahead) for ahead in range(1, parts)]

    def whole_grad(pieces):
        held = jnp.take(jnp.stack(pieces), (my_part - jnp.arange(parts)) % parts, axis=0)
        held = held.reshape(parts, dp_count, mp_count, piece_rows, tile_cols)
        return held.transpose(1, 0, 3, 2, 4).reshape(order, order)

    chunks = []
    for ahead in range(slots):
        old = lax.dynamic_index_in_dim(factor_stats, (my_slot + ahead) % slots, 0, keepdims=False)
        chunks.append(to_slot(old.astype(bf16), ahead) if ahead else old.astype(bf16))
    chunks += [to_part(chunk, ahead) for ahead in range(1, parts) for chunk in chunks]

    picked = call(
        functools.partial(pick_kernel, **where),
        jax.ShapeDtypeStruct(grad_tiles.shape, bf16),
        [SMEM, SMEM, VMEM],
    )(owners, rotation, grad_tiles)
    outgoing = picked.reshape(dp_count * mp_count, piece_rows, tile_cols)
    arrived = lax.all_to_all(outgoing, ("dp", "mp"), split_axis=0, concat_axis=0, tiled=True)
    pieces = all_pieces(arrived)
    theirs = [to_slot(arrived, ahead) for ahead in range(1, slots)]

    own_grad = pieces if split else [whole_grad(pieces)]
    result = call(
        functools.partial(owner_kernel, n_g=len(own_grad), split=split, sizes=sizes),
        jax.ShapeDtypeStruct(arrived.shape if split else (order, order), bf16),
        [VMEM] * (len(own_grad) + len(chunks)),
        [
            pltpu.VMEM((order, order), bf16),
            pltpu.VMEM((2, order, order), bf16),
            pltpu.VMEM((order, order), bf16),
        ],
        vmem=32,
        flops=24 * order**3,
    )(*own_grad, *chunks)
    if not split:
        result = result.reshape(dp_count, parts, piece_rows, mp_count, tile_cols)
        result = lax.dynamic_index_in_dim(result, my_part, 1, keepdims=False)
        result = result.transpose(0, 2, 1, 3).reshape(dp_count * mp_count, piece_rows, tile_cols)
    returned = lax.all_to_all(result, ("dp", "mp"), split_axis=0, concat_axis=0, tiled=True)

    grads = [pieces] + [all_pieces(x) for x in theirs]
    if split:
        new_stats = call(
            functools.partial(stats_kernel, sizes=sizes),
            jax.ShapeDtypeStruct(factor_stats.shape, f32),
            [VMEM] * (slots * parts + 1),
            [pltpu.VMEM((slots, order, order), bf16)],
            flops=4 * slots * rows * order**2,
        )(*[x for slot_pieces in grads for x in slot_pieces], factor_stats)
    else:
        blocks = jnp.stack([whole_grad(x) for x in grads])
        blocks = jnp.take(blocks, (my_slot - jnp.arange(slots)) % slots, axis=0)
        row_part = lax.dynamic_slice_in_dim(blocks, my_index * rows, rows, 1)
        col_part = lax.dynamic_slice_in_dim(blocks, my_index * rows, rows, 2)
        left = jnp.einsum("kij,klj->kil", row_part, blocks, preferred_element_type=f32)
        right = jnp.einsum("kji,kjl->kil", col_part, blocks, preferred_element_type=f32)
        new_stats = decay_rate * factor_stats + (1.0 - decay_rate) * jnp.stack([left, right], axis=1)

    preconditioned = call(
        functools.partial(place_kernel, **where),
        jax.ShapeDtypeStruct(grad_tiles.shape, bf16),
        [SMEM, SMEM, VMEM],
    )(owners, rotation, returned.reshape(grad_tiles.shape))
    return (preconditioned, new_stats)


def solution(mesh):
    return jax.shard_map(
        body,
        mesh=mesh,
        in_specs=(P(None, "dp", "mp"), P("dp", None, "mp", None), P(), P()),
        out_specs=(P(None, "dp", "mp"), P("dp", None, "mp", None)),
        check_vma=False,
    )
```

time: 51.9 us -> 48.2 us (0.929)
  other arithmetic: 2.08 us -> 0 us
  Pallas kernels: 11.6 us -> 11 us
    ppermute x2, waiting for transfers between devices: 11 us -> 9.33 us  [to_slot(): lax.ppermute(x, 'mp', [(i, (i + ahead * parts) % mp_count) for i in range...]
    another operation x2 -> x0, other arithmetic: 1.21 us -> none  [body(): jnp.stack([jnp.where(my_slot == s, stats_rows[0], stats_rows[1]) for s in...]
    convert_element_type x1 -> x0, other arithmetic: 0.87 us -> none  [body(): chunks = [slot_stats(0).astype(bf16)]]
    ppermute x3 -> x4, waiting for transfers between devices: 0.71 us -> 1.44 us  [to_part(): lax.ppermute(x, 'mp', [(i, i // parts * parts + (i + ahead) % parts) for...]
    another operation x1 -> x0, local copies, waits for them, and re-layouts: 0.68 us -> none  [body(): jnp.stack([my_part] + [(my_part - k) % parts * piece_rows for k in range(...]
    pallas_call x3 -> x4, Pallas kernels: 11.6 us -> 11 us  [the longest x1 6.63 us: body(): call(functools.partial(owner_kernel, n_g=len(own_grad), split=split, size...]
    unnamed x18 -> x8, local copies, waits for them, and re-layouts: 1.42 us -> 1.63 us
  transfers between devices with their start and end apart: 7 -> 8, of which waited for: 5 -> 4; matrix products, arithmetic and copies ran while one was open for 5% -> 0% of each run, Pallas kernels for 0% -> 18%
where the time goes in v2:
time: 48.2 us; the launch traced here: 47.9 us
  waiting for transfers between devices  18 us (37%)
  starting transfers between devices  15.8 us (33%)
  Pallas kernels  11 us (23%)
  local copies, waits for them, and re-layouts  1.7 us (4%)
  between operations  1.48 us (3%)
    ppermute x2, waiting for transfers between devices, to_slot(): lax.ppermute(x, 'mp', [(i, (i + ahead * parts) % mp_count) for i in range...  9.33 us
    all_to_all x1, starting transfers between devices, body(): lax.all_to_all(outgoing, ('dp', 'mp'), split_axis=0, concat_axis=0, tiled...  7.33 us
    all_to_all x1, waiting for transfers between devices, body(): lax.all_to_all(result, ('dp', 'mp'), split_axis=0, concat_axis=0, tiled=T...  7.19 us
    pallas_call x1, Pallas kernels, body(): call(functools.partial(owner_kernel, n_g=len(own_grad), split=split, size...  6.63 us
    all_to_all x1, starting transfers between devices, body(): lax.all_to_all(result, ('dp', 'mp'), split_axis=0, concat_axis=0, tiled=T...  4.59 us
    ppermute x2, starting transfers between devices, to_slot(): lax.ppermute(x, 'mp', [(i, (i + ahead * parts) % mp_count) for i in range...  3.07 us
    pallas_call x1, Pallas kernels, body(): call(functools.partial(stats_kernel, sizes=sizes), jax.ShapeDtypeStruct(f...  1.77 us
    unnamed x8, local copies, waits for them, and re-layouts  1.63 us
  transfers between devices with their start and end apart: 8, of which 4 were waited for; matrix products, arithmetic and copies ran while one was open for 0% of the time, Pallas kernels for 18%

profile of v2, /device:TPU:0, one launch (start us, length us, event | category | flops | bytes accessed | tf_op | source)
XLA Modules:
  0.0 47.9 jit_solution(5867767666954008154)
XLA Ops:
  0.6 0.0 copy-start
  1.4 0.0 copy-start.1
  1.4 0.9 %copy-done.1 = bf16[16,64,128]{2,1,0:T(8,128)(2,1)S(1)} copy-done((bf16[16,64,128]{2,1,0:T(8,128)(2,1)S(1)}, bf16[16,64,128]{2,1,0:T(8,128)(2,1)}, u32[]{:S(2)}) %copy-start.1) | copy-done | bytes 262168
  2.3 0.0 copy-start.2
  2.3 0.7 %copy-done.2 = s32[8,2]{0,1:T(2,128)S(1)} copy-done((s32[8,2]{0,1:T(2,128)S(1)}, s32[8,2]{0,1:T(2,128)}, u32[]{:S(2)}) %copy-start.2) | copy-done | bytes 88
  3.0 1.3 %shard_map.59 = bf16[16,64,128]{2,1,0:T(8,128)(2,1)} custom-call(s32[2,8]{1,0:T(2,128)S(1)} %bitcast.8, s32[1]{0:T(128)S(6)} %copy.6.rot_ref, bf16[16,64,128]{2,1,0:T(8,128)(2,1)S(1)} %copy-done.1), custom_call_target="tpu_custom_call" | custom-call | tf_op jit(solution)/shard_map/pallas_call | solution.py:186
  4.3 7.3 %all-to-all-start = ((bf16[32,32,128]{2,1,0:T(8,128)(2,1)}), bf16[32,32,128]{2,1,0:T(8,128)(2,1)S(1)}, u32[]{:S(2)}, u32[]{:S(2)}) async-start(bf16[32,32,128]{2,1,0:T(8,128)(2,1)} %bitcast.1), calls=%async_computation | async-start | bytes 524288 | tf_op jit(solution)/shard_map/all_to_all | solution.py:192
  11.7 0.0 copy-done
  11.7 0.1 fusion.1
  11.8 1.8 %collective-permute-start.1 = (bf16[2,128,512]{2,1,0:T(8,128)(2,1)S(1)}, bf16[2,128,512]{2,1,0:T(8,128)(2,1)S(1)}, u32[]{:S(2)}, u32[]{:S(2)}) collective-permute-start(bf16[2,128,512]{2,1,0:T(8,128)(2,1)S(1)} %get-tuple-element.2), channel_id=1, source_target_pairs={{0,2},{1,3},{2,0},{3,1},{4,6},{5,7},{6,4},{7,5},{8,10},{9,11},{10,... | collective-permute-start | bytes 786440 | tf_op jit(solution)/shard_map/ppermute | solution.py:165
  13.6 0.0 collective-permute-start.2
  13.6 9.3 %collective-permute-done.1.refs_3_ = bf16[2,128,512]{2,1,0:T(8,128)(2,1)S(1)} collective-permute-done((bf16[2,128,512]{2,1,0:T(8,128)(2,1)S(1)}, bf16[2,128,512]{2,1,0:T(8,128)(2,1)S(1)}, u32[]{:S(2)}, u32[]{:S(2)}) %collective-permute-start.1) | collective-permute-done | bytes 262176 | tf_op jit(solution)/shard_map/ppermute | solution.py:165
  22.9 0.0 collective-permute-start.3
  22.9 0.0 all-to-all-done.refs_0_
  22.9 0.5 %collective-permute-start = (bf16[32,32,128]{2,1,0:T(8,128)(2,1)S(1)}, bf16[32,32,128]{2,1,0:T(8,128)(2,1)S(1)}, u32[]{:S(2)}, u32[]{:S(2)}) collective-permute-start(bf16[32,32,128]{2,1,0:T(8,128)(2,1)S(1)} %all-to-all-done.refs_0_), channel_id=1, source_target_pairs={{0,1},{1,0},{2,3},{3,2},{4,5},{5,4},{6,7},{7,6},{8,9},{9,8},{10,11... | collective-permute-start | bytes 786440 | tf_op jit(solution)/shard_map/ppermute | solution.py:168
  23.4 1.2 %collective-permute-start.4 = (bf16[32,32,128]{2,1,0:T(8,128)(2,1)S(1)}, bf16[32,32,128]{2,1,0:T(8,128)(2,1)S(1)}, u32[]{:S(2)}, u32[]{:S(2)}) collective-permute-start(bf16[32,32,128]{2,1,0:T(8,128)(2,1)S(1)} %all-to-all-done.refs_0_), channel_id=1, source_target_pairs={{0,2},{1,3},{2,0},{3,1},{4,6},{5,7},{6,4},{7,5},{8,10},{9,11},{10,... | collective-permute-start | bytes 786440 | tf_op jit(solution)/shard_map/ppermute | solution.py:165
  24.7 0.0 collective-permute-done.2.refs_4_
  24.7 0.0 collective-permute-done.3.refs_5_
  24.7 0.1 collective-permute-done.refs_1_
  24.8 6.6 %shard_map.60 = bf16[32,32,128]{2,1,0:T(8,128)(2,1)} custom-call(bf16[32,32,128]{2,1,0:T(8,128)(2,1)S(1)} %all-to-all-done.refs_0_, bf16[32,32,128]{2,1,0:T(8,128)(2,1)S(1)} %collective-permute-done.refs_1_, bf16[2,128,512]{2,1,0:T(8,128)(2,1)S(1)} %get-tuple-element.3.refs_2_, bf16[2,128,512]{2,1,0:T(8,128)(2,1)S(1)} %collective-permute-done.1.refs_3_, ...), custom_call_target="tpu_custom_call" | custom-call | flops 3221225472 | tf_op jit(solution)/shard_map/pallas_call | solution.py:197
  31.5 4.6 %all-to-all-start.1 = ((bf16[32,32,128]{2,1,0:T(8,128)(2,1)}), bf16[32,32,128]{2,1,0:T(8,128)(2,1)S(1)}, u32[]{:S(2)}, u32[]{:S(2)}) async-start(bf16[32,32,128]{2,1,0:T(8,128)(2,1)} %shard_map.60), calls=%async_computation.1 | async-start | bytes 524288 | tf_op jit(solution)/shard_map/all_to_all | solution.py:213
  36.1 0.0 collective-permute-done.4.refs_2_
  36.1 0.3 collective-permute-start.5
  36.4 1.3 %collective-permute-done.5.refs_3_ = bf16[32,32,128]{2,1,0:T(8,128)(2,1)S(1)} collective-permute-done((bf16[32,32,128]{2,1,0:T(8,128)(2,1)S(1)}, bf16[32,32,128]{2,1,0:T(8,128)(2,1)S(1)}, u32[]{:S(2)}, u32[]{:S(2)}) %collective-permute-start.5) | collective-permute-done | bytes 262176 | tf_op jit(solution)/shard_map/ppermute | solution.py:168
  37.7 1.8 %shard_map.62 = f32[2,2,128,512]{3,2,1,0:T(8,128)} custom-call(bf16[32,32,128]{2,1,0:T(8,128)(2,1)S(1)} %all-to-all-done.refs_0_, bf16[32,32,128]{2,1,0:T(8,128)(2,1)S(1)} %collective-permute-done.refs_1_, bf16[32,32,128]{2,1,0:T(8,128)(2,1)S(1)} %collective-permute-done.4.refs_2_, bf16[32,32,128]{2,1,0:T(8,128)(2,1)S(1)} %collective-permute-done.5.refs_3_, ...), custom_call_target="tpu_custom_call" | custom-call | flops 268435456 | tf_op jit(solution)/shard_map/pallas_call | solution.py:217
  39.4 0.0 copy-start.3
  39.4 7.2 %all-to-all-done.1 = bf16[32,32,128]{2,1,0:T(8,128)(2,1)S(1)} async-done(((bf16[32,32,128]{2,1,0:T(8,128)(2,1)}), bf16[32,32,128]{2,1,0:T(8,128)(2,1)S(1)}, u32[]{:S(2)}, u32[]{:S(2)}) %all-to-all-start.1) | async-done | bytes 262176 | tf_op jit(solution)/shard_map/all_to_all | solution.py:213
  46.6 0.0 copy-done.3
  46.6 1.3 %shard_map.61 = bf16[16,64,128]{2,1,0:T(8,128)(2,1)} custom-call(s32[2,8]{1,0:T(2,128)S(1)} %bitcast.9, s32[1]{0:T(128)S(6)} %copy.6.rot_ref, bf16[16,64,128]{2,1,0:T(8,128)(2,1)S(1)} %bitcast.7), custom_call_target="tpu_custom_call" | custom-call | tf_op jit(solution)/shard_map/pallas_call | solution.py:233
Async XLA Ops:
  0.6 11.0 %copy-start = (f32[2,2,128,512]{3,2,1,0:T(8,128)S(1)}, f32[2,2,128,512]{3,2,1,0:T(8,128)}, u32[]{:S(2)}) copy-start(f32[2,2,128,512]{3,2,1,0:T(8,128)} %refs_4_.1) | copy-start | bytes 3145732
  1.4 1.0 %copy-start.1 = (bf16[16,64,128]{2,1,0:T(8,128)(2,1)S(1)}, bf16[16,64,128]{2,1,0:T(8,128)(2,1)}, u32[]{:S(2)}) copy-start(bf16[16,64,128]{2,1,0:T(8,128)(2,1)} %tiles_ref.1) | copy-start | bytes 786436
  2.3 0.7 %copy-start.2 = (s32[8,2]{0,1:T(2,128)S(1)}, s32[8,2]{0,1:T(2,128)}, u32[]{:S(2)}) copy-start(s32[8,2]{0,1:T(2,128)} %param.6) | copy-start | bytes 196
  4.3 18.6 %all-to-all-start = ((bf16[32,32,128]{2,1,0:T(8,128)(2,1)}), bf16[32,32,128]{2,1,0:T(8,128)(2,1)S(1)}, u32[]{:S(2)}, u32[]{:S(2)}) async-start(bf16[32,32,128]{2,1,0:T(8,128)(2,1)} %bitcast.1), calls=%async_computation | async-start | bytes 524288 | tf_op jit(solution)/shard_map/all_to_all | solution.py:192
  11.8 11.2 %collective-permute-start.1 = (bf16[2,128,512]{2,1,0:T(8,128)(2,1)S(1)}, bf16[2,128,512]{2,1,0:T(8,128)(2,1)S(1)}, u32[]{:S(2)}, u32[]{:S(2)}) collective-permute-start(bf16[2,128,512]{2,1,0:T(8,128)(2,1)S(1)} %get-tuple-element.2), channel_id=1, source_target_pairs={{0,2},{1,3},{2,0},{3,1},{4,6},{5,7},{6,4},{7,5},{8,10},{9,11},{10,... | collective-permute-start | bytes 786440 | tf_op jit(solution)/shard_map/ppermute | solution.py:165
  13.6 11.1 %collective-permute-start.2 = (bf16[2,128,512]{2,1,0:T(8,128)(2,1)S(1)}, bf16[2,128,512]{2,1,0:T(8,128)(2,1)S(1)}, u32[]{:S(2)}, u32[]{:S(2)}) collective-permute-start(bf16[2,128,512]{2,1,0:T(8,128)(2,1)S(1)} %get-tuple-element.3.refs_2_), channel_id=1, source_target_pairs={{0,1},{1,0},{2,3},{3,2},{4,5},{5,4},{6,7},{7,6},{8,9},{9,8},{10,11... | collective-permute-start | bytes 786440 | tf_op jit(solution)/shard_map/ppermute | solution.py:168
  22.9 1.8 %collective-permute-start.3 = (bf16[2,128,512]{2,1,0:T(8,128)(2,1)S(1)}, bf16[2,128,512]{2,1,0:T(8,128)(2,1)S(1)}, u32[]{:S(2)}, u32[]{:S(2)}) collective-permute-start(bf16[2,128,512]{2,1,0:T(8,128)(2,1)S(1)} %collective-permute-done.1.refs_3_), channel_id=1, source_target_pairs={{0,1},{1,0},{2,3},{3,2},{4,5},{5,4},{6,7},{7,6},{8,9},{9,8},{10,11... | collective-permute-start | bytes 786440 | tf_op jit(solution)/shard_map/ppermute | solution.py:168
  22.9 1.9 %collective-permute-start = (bf16[32,32,128]{2,1,0:T(8,128)(2,1)S(1)}, bf16[32,32,128]{2,1,0:T(8,128)(2,1)S(1)}, u32[]{:S(2)}, u32[]{:S(2)}) collective-permute-start(bf16[32,32,128]{2,1,0:T(8,128)(2,1)S(1)} %all-to-all-done.refs_0_), channel_id=1, source_target_pairs={{0,1},{1,0},{2,3},{3,2},{4,5},{5,4},{6,7},{7,6},{8,9},{9,8},{10,11... | collective-permute-start | bytes 786440 | tf_op jit(solution)/shard_map/ppermute | solution.py:168
  23.4 12.6 %collective-permute-start.4 = (bf16[32,32,128]{2,1,0:T(8,128)(2,1)S(1)}, bf16[32,32,128]{2,1,0:T(8,128)(2,1)S(1)}, u32[]{:S(2)}, u32[]{:S(2)}) collective-permute-start(bf16[32,32,128]{2,1,0:T(8,128)(2,1)S(1)} %all-to-all-done.refs_0_), channel_id=1, source_target_pairs={{0,2},{1,3},{2,0},{3,1},{4,6},{5,7},{6,4},{7,5},{8,10},{9,11},{10,... | collective-permute-start | bytes 786440 | tf_op jit(solution)/shard_map/ppermute | solution.py:165
  31.5 15.2 %all-to-all-start.1 = ((bf16[32,32,128]{2,1,0:T(8,128)(2,1)}), bf16[32,32,128]{2,1,0:T(8,128)(2,1)S(1)}, u32[]{:S(2)}, u32[]{:S(2)}) async-start(bf16[32,32,128]{2,1,0:T(8,128)(2,1)} %shard_map.60), calls=%async_computation.1 | async-start | bytes 524288 | tf_op jit(solution)/shard_map/all_to_all | solution.py:213
  36.1 1.6 %collective-permute-start.5 = (bf16[32,32,128]{2,1,0:T(8,128)(2,1)S(1)}, bf16[32,32,128]{2,1,0:T(8,128)(2,1)S(1)}, u32[]{:S(2)}, u32[]{:S(2)}) collective-permute-start(bf16[32,32,128]{2,1,0:T(8,128)(2,1)S(1)} %collective-permute-done.4.refs_2_), channel_id=1, source_target_pairs={{0,1},{1,0},{2,3},{3,2},{4,5},{5,4},{6,7},{7,6},{8,9},{9,8},{10,11... | collective-permute-start | bytes 786440 | tf_op jit(solution)/shard_map/ppermute | solution.py:168
  39.4 7.2 %copy-start.3 = (s32[8,2]{0,1:T(2,128)S(1)}, s32[8,2]{0,1:T(2,128)}, u32[]{:S(2)}) copy-start(s32[8,2]{0,1:T(2,128)} %param.6) | copy-start | bytes 196

commit v3 on v2

v3 whole, which is shorter than its diff:
```python
import functools

import jax
import jax.numpy as jnp
from jax import lax
from jax.experimental import pallas as pl
from jax.experimental.pallas import tpu as pltpu
from jax.sharding import PartitionSpec as P


ITERS = 2


decay_rate = 0.9
damping = 1.0
bf16 = jnp.bfloat16
f32 = jnp.float32


def owner_of(owners_ref, rot, o, s, dp_count):
    row = o - rot
    return owners_ref[s, jnp.where(row < 0, row + dp_count, row)]


def pick_kernel(owners_hbm, rot_ref, tiles_hbm, out_ref, owners_ref, tiles_ref, sems, *, dp_count, slots):
    pairs = ((owners_hbm, owners_ref), (tiles_hbm, tiles_ref))
    copies = [pltpu.make_async_copy(a, b, sems.at[i]) for i, (a, b) in enumerate(pairs)]
    for copy in copies:
        copy.start()
    for copy in copies:
        copy.wait()
    rot = rot_ref[0]

    def one(j, carry):
        out_ref[j] = tiles_ref[owner_of(owners_ref, rot, j // slots, j % slots, dp_count)]
        return carry

    lax.fori_loop(0, dp_count * slots, one, 0, unroll=dp_count * slots <= 16)


def place_kernel(owners_ref, rot_ref, in_ref, out_hbm, sems, *, dp_count, slots):
    rot = rot_ref[0]

    def copy(j):
        block = owner_of(owners_ref, rot, j // slots, j % slots, dp_count)
        return pltpu.make_async_copy(in_ref.at[j], out_hbm.at[block], sems.at[j])

    def start(j, carry):
        copy(j).start()
        return carry

    def wait(j, carry):
        copy(j).wait()
        return carry

    count = dp_count * slots
    lax.fori_loop(0, count, start, 0, unroll=count <= 16)
    lax.fori_loop(0, count, wait, 0, unroll=count <= 16)


def dot(a, b, dims=(((1,), (0,)), ((), ()))):
    return lax.dot_general(a, b, dims, preferred_element_type=f32)


def newton_root(factor, eye5):
    norm = jnp.sum(jnp.square(factor.astype(f32)))
    moment = (2.5 / jnp.sqrt(norm) * factor.astype(f32)).astype(bf16)
    current = None
    for newton_step in range(ITERS):
        step_t = ((eye5 - moment.astype(f32)) * 0.25).astype(bf16)
        current = step_t if newton_step == 0 else dot(current, step_t).astype(bf16)
        if newton_step + 1 < ITERS:
            square = dot(step_t, step_t).astype(bf16)
            partial_m = dot(square, moment).astype(bf16)
            moment = dot(square, partial_m).astype(bf16)
    return current


def gather_grad(g_refs, g_scr, part, *, dp_count, mp_count, parts, piece_rows, tile_cols):
    for k, g_ref in enumerate(g_refs):
        piece = part - k
        at = pl.multiple_of(jnp.where(piece < 0, piece + parts, piece) * piece_rows, piece_rows)
        for o in range(dp_count):
            for m in range(mp_count):
                rows = pl.ds(o * parts * piece_rows + at, piece_rows)
                g_scr[rows, m * tile_cols : (m + 1) * tile_cols] = g_ref[o * mp_count + m]


def base_kernel(*refs, parts):
    s_refs, (out_ref, s_scr) = refs[:-2], refs[-2:]
    order = out_ref.shape[0]
    rows = s_refs[0].shape[0]
    my_index = lax.axis_index("mp")
    half = rows * parts
    for k, s_ref in enumerate(s_refs):
        at = pl.multiple_of((my_index ^ k) * rows, rows)
        if s_ref.shape[1] == order:
            s_scr[pl.ds(at, rows), :] = s_ref[...]
            continue
        for slot in range(2):

            @pl.when(my_index // parts == slot)
            def _():
                s_scr[pl.ds(at, rows), (1 - slot) * half : (2 - slot) * half] = s_ref[...]

    if s_refs[-1].shape[1] != order:
        for slot in range(2):

            @pl.when(my_index // parts == slot)
            def _():
                mine = slice(slot * half, (slot + 1) * half)
                other = slice((1 - slot) * half, (2 - slot) * half)
                s_scr[other, mine] = s_scr[mine, other].astype(f32).T.astype(bf16)

    ids = lax.broadcasted_iota(jnp.int32, (order, order), 0)
    eye = ids == lax.broadcasted_iota(jnp.int32, (order, order), 1)
    out_ref[...] = decay_rate * s_scr[...].astype(f32) + jnp.where(eye, damping, 0.0)


def root_kernel(*refs, n_g, split, sizes):
    g_refs, (base_ref, root_ref, grad_ref, gram_scr) = refs[:n_g], refs[n_g:]
    order = grad_ref.shape[0]
    part = lax.axis_index("mp") % sizes["parts"]
    if split:
        gather_grad(g_refs, grad_ref, part, **sizes)
    else:
        grad_ref[...] = g_refs[0][...]
    for side in range(2):

        @pl.when(part % 2 == side)
        def _():
            across = 1 - side
            gram_scr[...] = dot(grad_ref[...], grad_ref[...], (((across,), (across,)), ((), ())))

    ids = lax.broadcasted_iota(jnp.int32, (order, order), 0)
    eye = ids == lax.broadcasted_iota(jnp.int32, (order, order), 1)
    factor = (base_ref[...] + (1.0 - decay_rate) * gram_scr[...]).astype(bf16)
    root_ref[...] = newton_root(factor, jnp.where(eye, 5.0, 0.0))


def half_kernel(root_ref, grad_ref, out_ref, norm_ref, *, parts):
    for side in range(2):

        @pl.when(lax.axis_index("mp") % parts % 2 == side)
        def _():
            a, b = (root_ref, grad_ref) if side == 0 else (grad_ref, root_ref)
            out_ref[...] = dot(a[...], b[...]).astype(bf16)

    squares = jnp.sum(jnp.square(grad_ref[...].astype(f32)))
    norm_ref[...] = jnp.full(norm_ref.shape, jnp.sqrt(squares), f32)


def result_kernel(half_ref, root_ref, norm_ref, out_ref, res_scr, *, split, sizes):
    dp_count, mp_count, parts = sizes["dp_count"], sizes["mp_count"], sizes["parts"]
    piece_rows, tile_cols = sizes["piece_rows"], sizes["tile_cols"]
    part = lax.axis_index("mp") % parts
    for side in range(2):

        @pl.when(part % 2 == side)
        def _():
            a, b = (half_ref, root_ref) if side == 0 else (root_ref, half_ref)
            res_scr[...] = dot(a[...], b[...]).astype(bf16)

    scale = norm_ref[0, 0] / (jnp.sqrt(jnp.sum(jnp.square(res_scr[...].astype(f32)))) + 1e-06)
    if not split:
        out_ref[...] = (res_scr[...].astype(f32) * scale).astype(bf16)
        return
    at = pl.multiple_of(part * piece_rows, piece_rows)
    for o in range(dp_count):
        for m in range(mp_count):
            piece = res_scr[pl.ds(o * parts * piece_rows + at, piece_rows), m * tile_cols : (m + 1) * tile_cols]
            out_ref[o * mp_count + m] = (piece.astype(f32) * scale).astype(bf16)


def stats_kernel(*refs, sizes):
    g_refs, (old_ref, new_ref, g_scr) = refs[:-3], refs[-3:]
    parts = sizes["parts"]
    slots = sizes["mp_count"] // parts
    rows = old_ref.shape[2]
    my_index = lax.axis_index("mp")
    at = pl.multiple_of(my_index * rows, rows)
    for j in range(slots):
        gather_grad(g_refs[j * parts : (j + 1) * parts], g_scr.at[j], my_index % parts, **sizes)
        slot = (my_index // parts - j + slots) % slots
        left = dot(g_scr[j, pl.ds(at, rows), :], g_scr[j], (((1,), (1,)), ((), ())))
        right = dot(g_scr[j, :, pl.ds(at, rows)], g_scr[j], (((0,), (0,)), ((), ())))
        new_ref[slot, 0] = decay_rate * old_ref[slot, 0] + (1.0 - decay_rate) * left
        new_ref[slot, 1] = decay_rate * old_ref[slot, 1] + (1.0 - decay_rate) * right


VMEM = pl.BlockSpec(memory_space=pltpu.VMEM)
SMEM = pl.BlockSpec(memory_space=pltpu.SMEM)
HBM = pl.BlockSpec(memory_space=pltpu.HBM)


def in_hbm(x):
    return pltpu.with_memory_space_constraint(x, pltpu.HBM)


def call(kernel, out_shape, in_specs, scratch=(), out_specs=VMEM, vmem=8, flops=0):
    return pl.pallas_call(
        kernel,
        out_shape=out_shape,
        in_specs=in_specs,
        out_specs=(VMEM,) * len(out_shape) if isinstance(out_shape, tuple) else out_specs,
        scratch_shapes=list(scratch),
        compiler_params=pltpu.CompilerParams(vmem_limit_bytes=vmem * 2**20),
        cost_estimate=pl.CostEstimate(flops=flops, transcendentals=0, bytes_accessed=0) if flops else None,
    )


def step(grad_tiles, factor_stats, owner_blocks, rotation):
    dp_count = lax.axis_size("dp")
    mp_count = lax.axis_size("mp")
    tile_rows, tile_cols = grad_tiles.shape[1:]
    slots = owner_blocks.shape[1]
    rows, order = factor_stats.shape[2:]
    parts = mp_count // slots
    assert parts % 2 == 0 and mp_count & (mp_count - 1) == 0
    piece_rows = tile_rows // parts
    split = piece_rows % 16 == 0 and tile_cols % 128 == 0 and rows == tile_cols
    my_index = lax.axis_index("mp")
    my_slot = my_index // parts
    my_part = my_index % parts
    owners = owner_blocks.T
    where = dict(dp_count=dp_count, slots=slots)
    sizes = dict(
        dp_count=dp_count, mp_count=mp_count, parts=parts, piece_rows=piece_rows, tile_cols=tile_cols
    )
    table = pltpu.SMEM(owners.shape, jnp.int32)

    def to_slot(x, ahead):
        return lax.ppermute(x, "mp", [(i, (i + ahead * parts) % mp_count) for i in range(mp_count)])

    def to_part(x, ahead):
        return lax.ppermute(
            x, "mp", [(i, i // parts * parts + (i + ahead) % parts) for i in range(mp_count)]
        )

    def to_flip(x, flip):
        return lax.ppermute(x, "mp", [(i, i ^ flip) for i in range(mp_count)])

    def all_pieces(x):
        return [x] + [to_part(x, ahead) for ahead in range(1, parts)]

    def whole_grad(pieces):
        held = jnp.take(jnp.stack(pieces), (my_part - jnp.arange(parts)) % parts, axis=0)
        held = held.reshape(parts, dp_count, mp_count, piece_rows, tile_cols)
        return held.transpose(1, 0, 3, 2, 4).reshape(order, order)

    square = pltpu.VMEM((order, order), bf16)
    square_f32 = pltpu.VMEM((order, order), f32)
    chunks = []
    for flip in range(mp_count):
        dest = my_index ^ flip
        across = flip >= parts and slots == 2
        at = (dest // parts, dest % parts % 2, 0, my_slot * rows * parts if across else 0)
        old = lax.dynamic_slice(factor_stats, at, (1, 1, rows, rows * parts if across else order))
        old = old.reshape(old.shape[2:]).astype(bf16)
        chunks.append(to_flip(old, flip) if flip else old)
    base = call(
        functools.partial(base_kernel, parts=parts),
        square_f32,
        [VMEM] * len(chunks),
        [square],
        flops=order**2,
    )(*chunks)

    picked = call(
        functools.partial(pick_kernel, **where),
        jax.ShapeDtypeStruct(grad_tiles.shape, bf16),
        [HBM, SMEM, HBM],
        [table, pltpu.VMEM(grad_tiles.shape, bf16), pltpu.SemaphoreType.DMA((2,))],
    )(in_hbm(owners), rotation, in_hbm(grad_tiles))
    outgoing = picked.reshape(dp_count * mp_count, piece_rows, tile_cols)
    arrived = lax.all_to_all(outgoing, ("dp", "mp"), split_axis=0, concat_axis=0, tiled=True)
    pieces = all_pieces(arrived)
    theirs = [to_slot(arrived, ahead) for ahead in range(1, slots)]

    own_grad = pieces if split else [whole_grad(pieces)]
    root, grad = call(
        functools.partial(root_kernel, n_g=len(own_grad), split=split, sizes=sizes),
        (square, square),
        [VMEM] * (len(own_grad) + 1),
        [square_f32],
        vmem=16,
        flops=10 * order**3,
    )(*own_grad, base)
    other_root = to_flip(root, 1)
    half, norm = call(
        functools.partial(half_kernel, parts=parts),
        (square, pltpu.VMEM((8, 128), f32)),
        [VMEM, VMEM],
        flops=2 * order**3,
    )(root, grad)
    result = call(
        functools.partial(result_kernel, split=split, sizes=sizes),
        pltpu.VMEM(arrived.shape if split else (order, order), bf16),
        [VMEM, VMEM, VMEM],
        [square],
        flops=2 * order**3,
    )(half, other_root, norm)
    if not split:
        result = result.reshape(dp_count, parts, piece_rows, mp_count, tile_cols)
        result = lax.dynamic_index_in_dim(result, my_part, 1, keepdims=False)
        result = result.transpose(0, 2, 1, 3).reshape(dp_count * mp_count, piece_rows, tile_cols)
    returned = lax.all_to_all(result, ("dp", "mp"), split_axis=0, concat_axis=0, tiled=True)

    grads = [pieces] + [all_pieces(x) for x in theirs]
    if split:
        new_stats = call(
            functools.partial(stats_kernel, sizes=sizes),
            jax.ShapeDtypeStruct(factor_stats.shape, f32),
            [VMEM] * (slots * parts + 1),
            [pltpu.VMEM((slots, order, order), bf16)],
            vmem=16,
            flops=4 * slots * rows * order**2,
        )(*[x for slot_pieces in grads for x in slot_pieces], factor_stats)
    else:
        blocks = jnp.stack([whole_grad(x) for x in grads])
        blocks = jnp.take(blocks, (my_slot - jnp.arange(slots)) % slots, axis=0)
        row_part = lax.dynamic_slice_in_dim(blocks, my_index * rows, rows, 1)
        col_part = lax.dynamic_slice_in_dim(blocks, my_index * rows, rows, 2)
        left = jnp.einsum("kij,klj->kil", row_part, blocks, preferred_element_type=f32)
        right = jnp.einsum("kji,kjl->kil", col_part, blocks, preferred_element_type=f32)
        new_stats = decay_rate * factor_stats + (1.0 - decay_rate) * jnp.stack([left, right], axis=1)

    preconditioned = call(
        functools.partial(place_kernel, **where),
        jax.ShapeDtypeStruct(grad_tiles.shape, bf16),
        [SMEM, SMEM, VMEM],
        [pltpu.SemaphoreType.DMA((dp_count * slots,))],
        out_specs=HBM,
    )(owners, rotation, returned.reshape(grad_tiles.shape))
    return (preconditioned, new_stats)


def solution(mesh):
    return placed(mesh)


def placed(mesh):
    return jax.shard_map(
        step,
        mesh=mesh,
        in_specs=(P(None, "dp", "mp"), P("dp", None, "mp", None), P(), P()),
        out_specs=(P(None, "dp", "mp"), P("dp", None, "mp", None)),
        check_vma=False,
    )
```

time: 48.2 us -> 48.5 us (level)
  waiting for transfers between devices: 18 us -> 22.6 us
  starting transfers between devices: 15.8 us -> 13.7 us
  local copies, waits for them, and re-layouts: 1.7 us -> 0.06 us
  Pallas kernels: 11 us -> 10.1 us
    all_to_all x2, waiting for transfers between devices: 7.19 us -> 15.7 us  [the longest x1 10.5 us: step(): lax.all_to_all(outgoing, ('dp', 'mp'), split_axis=0, concat_axis=0, tiled...]
    ppermute x2 -> x1, waiting for transfers between devices: 9.33 us -> 2.03 us  [to_slot(): lax.ppermute(x, 'mp', [(i, (i + ahead * parts) % mp_count) for i in range...]
    ppermute x0 -> x4, waiting for transfers between devices: none -> 3.36 us  [to_flip(): return lax.ppermute(x, 'mp', [(i, i ^ flip) for i in range(mp_count)])]
    ppermute x0 -> x4, starting transfers between devices: none -> 2.71 us  [to_flip(): return lax.ppermute(x, 'mp', [(i, i ^ flip) for i in range(mp_count)])]
    all_to_all x2, starting transfers between devices: 11.9 us -> 9.92 us  [the longest x1 7.33 us: step(): lax.all_to_all(outgoing, ('dp', 'mp'), split_axis=0, concat_axis=0, tiled...]
    ppermute x2 -> x1, starting transfers between devices: 3.07 us -> 1.12 us  [to_slot(): lax.ppermute(x, 'mp', [(i, (i + ahead * parts) % mp_count) for i in range...]
    unnamed x8 -> x4, local copies, waits for them, and re-layouts: 1.63 us -> 0.01 us
    pallas_call x4 -> x7, Pallas kernels: 11 us -> 10.1 us  [the longest x1 2.5 us: step(): call(functools.partial(root_kernel, n_g=len(own_grad), split=split, sizes...]
  transfers between devices with their start and end apart: 8 -> 9, of which waited for: 4 -> 5; matrix products, arithmetic and copies ran while one was open for 0% -> 0% of each run, Pallas kernels for 18% -> 9%
where the time goes in v3:
time: 48.5 us; the launch traced here: 48.1 us
  waiting for transfers between devices  22.6 us (47%)
  starting transfers between devices  13.7 us (28%)
  Pallas kernels  10.1 us (21%)
  between operations  1.55 us (3%)
    all_to_all x1, waiting for transfers between devices, step(): lax.all_to_all(outgoing, ('dp', 'mp'), split_axis=0, concat_axis=0, tiled...  10.5 us
    all_to_all x1, starting transfers between devices, step(): lax.all_to_all(outgoing, ('dp', 'mp'), split_axis=0, concat_axis=0, tiled...  7.33 us
    all_to_all x1, waiting for transfers between devices, step(): lax.all_to_all(result, ('dp', 'mp'), split_axis=0, concat_axis=0, tiled=T...  5.24 us
    ppermute x4, waiting for transfers between devices, to_flip(): return lax.ppermute(x, 'mp', [(i, i ^ flip) for i in range(mp_count)])  3.36 us
    ppermute x4, starting transfers between devices, to_flip(): return lax.ppermute(x, 'mp', [(i, i ^ flip) for i in range(mp_count)])  2.71 us
    all_to_all x1, starting transfers between devices, step(): lax.all_to_all(result, ('dp', 'mp'), split_axis=0, concat_axis=0, tiled=T...  2.59 us
    pallas_call x1, Pallas kernels, step(): call(functools.partial(root_kernel, n_g=len(own_grad), split=split, sizes...  2.5 us
    ppermute x1, waiting for transfers between devices, to_slot(): lax.ppermute(x, 'mp', [(i, (i + ahead * parts) % mp_count) for i in range...  2.03 us
  transfers between devices with their start and end apart: 9, of which 5 were waited for; matrix products, arithmetic and copies ran while one was open for 0% of the time, Pallas kernels for 9%

profile of v3, /device:TPU:0, one launch (start us, length us, event | category | flops | bytes accessed | tf_op | source)
XLA Modules:
  0.0 48.1 jit_solution(5030839984428178605)
XLA Ops:
  0.6 0.0 copy-start
  1.4 1.7 %shard_map.59 = bf16[16,64,128]{2,1,0:T(8,128)(2,1)} custom-call(s32[2,8]{1,0:T(2,128)} %bitcast.12, s32[1]{0:T(128)S(6)} %copy.6.rot_ref, bf16[16,64,128]{2,1,0:T(8,128)(2,1)} %tiles_hbm.1), custom_call_target="tpu_custom_call" | custom-call | tf_op jit(solution)/shard_map/pallas_call | solution.py:269
  3.1 7.3 %all-to-all-start = ((bf16[32,32,128]{2,1,0:T(8,128)(2,1)}), bf16[32,32,128]{2,1,0:T(8,128)(2,1)S(1)}, u32[]{:S(2)}, u32[]{:S(2)}) async-start(bf16[32,32,128]{2,1,0:T(8,128)(2,1)} %bitcast.1), calls=%async_computation | async-start | bytes 524288 | tf_op jit(solution)/shard_map/all_to_all | solution.py:276
  10.5 10.5 %all-to-all-done.refs_0_ = bf16[32,32,128]{2,1,0:T(8,128)(2,1)S(1)} async-done(((bf16[32,32,128]{2,1,0:T(8,128)(2,1)}), bf16[32,32,128]{2,1,0:T(8,128)(2,1)S(1)}, u32[]{:S(2)}, u32[]{:S(2)}) %all-to-all-start) | async-done | bytes 262176 | tf_op jit(solution)/shard_map/all_to_all | solution.py:276
  21.0 0.0 collective-permute-start
  21.0 0.0 copy-done
  21.0 0.6 %collective-permute-start.1 = (bf16[128,512]{1,0:T(8,128)(2,1)S(1)}, bf16[128,512]{1,0:T(8,128)(2,1)S(1)}, u32[]{:S(2)}, u32[]{:S(2)}) collective-permute-start(bf16[128,512]{1,0:T(8,128)(2,1)S(1)} %get-tuple-element.12), channel_id=1, source_target_pairs={{0,1},{1,0},{2,3},{3,2},{4,5},{5,4},{6,7},{7,6},{8,9},{9,8},{10,11... | collective-permute-start | bytes 393224 | tf_op jit(solution)/shard_map/ppermute | solution.py:241
  21.6 0.5 %collective-permute-start.2 = (bf16[128,256]{1,0:T(8,128)(2,1)S(1)}, bf16[128,256]{1,0:T(8,128)(2,1)S(1)}, u32[]{:S(2)}, u32[]{:S(2)}) collective-permute-start(bf16[128,256]{1,0:T(8,128)(2,1)S(1)} %get-tuple-element.11), channel_id=1, source_target_pairs={{0,2},{1,3},{2,0},{3,1},{4,6},{5,7},{6,4},{7,5},{8,10},{9,11},{10,... | collective-permute-start | bytes 196616 | tf_op jit(solution)/shard_map/ppermute | solution.py:241
  22.1 1.0 %collective-permute-start.3 = (bf16[128,256]{1,0:T(8,128)(2,1)S(1)}, bf16[128,256]{1,0:T(8,128)(2,1)S(1)}, u32[]{:S(2)}, u32[]{:S(2)}) collective-permute-start(bf16[128,256]{1,0:T(8,128)(2,1)S(1)} %get-tuple-element.10), channel_id=1, source_target_pairs={{0,3},{1,2},{2,1},{3,0},{4,7},{5,6},{6,5},{7,4},{8,11},{9,10},{10,... | collective-permute-start | bytes 196616 | tf_op jit(solution)/shard_map/ppermute | solution.py:241
  23.2 3.4 %collective-permute-done.2.refs_2_ = bf16[128,256]{1,0:T(8,128)(2,1)S(1)} collective-permute-done((bf16[128,256]{1,0:T(8,128)(2,1)S(1)}, bf16[128,256]{1,0:T(8,128)(2,1)S(1)}, u32[]{:S(2)}, u32[]{:S(2)}) %collective-permute-start.2) | collective-permute-done | bytes 65568 | tf_op jit(solution)/shard_map/ppermute | solution.py:241
  26.5 0.0 collective-permute-done.3.refs_3_
  26.5 0.0 collective-permute-done.1.refs_1_
  26.5 0.3 shard_map.60.refs_2_
  26.8 0.0 collective-permute-done.refs_1_
  26.8 2.5 %shard_map.61 = (bf16[512,512]{1,0:T(8,128)(2,1)S(1)}, bf16[512,512]{1,0:T(8,128)(2,1)S(1)}) custom-call(bf16[32,32,128]{2,1,0:T(8,128)(2,1)S(1)} %all-to-all-done.refs_0_, bf16[32,32,128]{2,1,0:T(8,128)(2,1)S(1)} %collective-permute-done.refs_1_, f32[512,512]{1,0:T(8,128)S(1)} %shard_map.60.refs_2_), custom_call_target="tpu_custom_call" | custom-call | flops 1342177280 | tf_op jit(solution)/shard_map/pallas_call | solution.py:281
  29.3 0.6 %collective-permute-start.4 = (bf16[512,512]{1,0:T(8,128)(2,1)S(1)}, bf16[512,512]{1,0:T(8,128)(2,1)S(1)}, u32[]{:S(2)}, u32[]{:S(2)}) collective-permute-start(bf16[512,512]{1,0:T(8,128)(2,1)S(1)} %get-tuple-element.6.root_ref), channel_id=1, source_target_pairs={{0,1},{1,0},{2,3},{3,2},{4,5},{5,4},{6,7},{7,6},{8,9},{9,8},{10,11... | collective-permute-start | bytes 1572872 | tf_op jit(solution)/shard_map/ppermute | solution.py:241
  29.9 1.1 %collective-permute-start.5 = (bf16[32,32,128]{2,1,0:T(8,128)(2,1)S(1)}, bf16[32,32,128]{2,1,0:T(8,128)(2,1)S(1)}, u32[]{:S(2)}, u32[]{:S(2)}) collective-permute-start(bf16[32,32,128]{2,1,0:T(8,128)(2,1)S(1)} %all-to-all-done.refs_0_), channel_id=1, source_target_pairs={{0,2},{1,3},{2,0},{3,1},{4,6},{5,7},{6,4},{7,5},{8,10},{9,11},{10,... | collective-permute-start | bytes 786440 | tf_op jit(solution)/shard_map/ppermute | solution.py:233
  31.0 0.9 %shard_map.62 = (bf16[512,512]{1,0:T(8,128)(2,1)S(1)}, f32[8,128]{1,0:T(8,128)S(1)}) custom-call(bf16[512,512]{1,0:T(8,128)(2,1)S(1)} %get-tuple-element.6.root_ref, bf16[512,512]{1,0:T(8,128)(2,1)S(1)} %get-tuple-element.7.grad_ref), custom_call_target="tpu_custom_call" | custom-call | flops 268435456 | tf_op jit(solution)/shard_map/pallas_call | solution.py:290
  31.9 0.0 collective-permute-done.4.root_ref
  31.9 1.7 %shard_map.63 = bf16[32,32,128]{2,1,0:T(8,128)(2,1)} custom-call(bf16[512,512]{1,0:T(8,128)(2,1)S(1)} %get-tuple-element.8.half_ref, bf16[512,512]{1,0:T(8,128)(2,1)S(1)} %collective-permute-done.4.root_ref, f32[8,128]{1,0:T(8,128)S(1)} %get-tuple-element.9.norm_ref), custom_call_target="tpu_custom_call" | custom-call | flops 268435456 | tf_op jit(solution)/shard_map/pallas_call | solution.py:296
  33.6 2.6 %all-to-all-start.1 = ((bf16[32,32,128]{2,1,0:T(8,128)(2,1)}), bf16[32,32,128]{2,1,0:T(8,128)(2,1)S(1)}, u32[]{:S(2)}, u32[]{:S(2)}) async-start(bf16[32,32,128]{2,1,0:T(8,128)(2,1)} %shard_map.63), calls=%async_computation.1 | async-start | bytes 524288 | tf_op jit(solution)/shard_map/all_to_all | solution.py:307
  36.2 2.0 %collective-permute-done.5.refs_2_ = bf16[32,32,128]{2,1,0:T(8,128)(2,1)S(1)} collective-permute-done((bf16[32,32,128]{2,1,0:T(8,128)(2,1)S(1)}, bf16[32,32,128]{2,1,0:T(8,128)(2,1)S(1)}, u32[]{:S(2)}, u32[]{:S(2)}) %collective-permute-start.5) | collective-permute-done | bytes 262176 | tf_op jit(solution)/shard_map/ppermute | solution.py:233
  38.2 0.0 collective-permute-start.6
  38.2 1.5 %collective-permute-done.6.refs_3_ = bf16[32,32,128]{2,1,0:T(8,128)(2,1)S(1)} collective-permute-done((bf16[32,32,128]{2,1,0:T(8,128)(2,1)S(1)}, bf16[32,32,128]{2,1,0:T(8,128)(2,1)S(1)}, u32[]{:S(2)}, u32[]{:S(2)}) %collective-permute-start.6) | collective-permute-done | bytes 262176 | tf_op jit(solution)/shard_map/ppermute | solution.py:236
  39.7 1.8 %shard_map.65 = f32[2,2,128,512]{3,2,1,0:T(8,128)} custom-call(bf16[32,32,128]{2,1,0:T(8,128)(2,1)S(1)} %all-to-all-done.refs_0_, bf16[32,32,128]{2,1,0:T(8,128)(2,1)S(1)} %collective-permute-done.refs_1_, bf16[32,32,128]{2,1,0:T(8,128)(2,1)S(1)} %collective-permute-done.5.refs_2_, bf16[32,32,128]{2,1,0:T(8,128)(2,1)S(1)} %collective-permute-done.6.refs_3_, ...), custom_call_target="tpu_custom_call" | custom-call | flops 268435456 | tf_op jit(solution)/shard_map/pallas_call | solution.py:311
  41.5 0.0 copy-start.1
  41.5 5.2 %all-to-all-done.1 = bf16[32,32,128]{2,1,0:T(8,128)(2,1)S(1)} async-done(((bf16[32,32,128]{2,1,0:T(8,128)(2,1)}), bf16[32,32,128]{2,1,0:T(8,128)(2,1)S(1)}, u32[]{:S(2)}, u32[]{:S(2)}) %all-to-all-start.1) | async-done | bytes 262176 | tf_op jit(solution)/shard_map/all_to_all | solution.py:307
  46.7 0.0 copy-done.1
  46.7 1.4 %shard_map.64 = bf16[16,64,128]{2,1,0:T(8,128)(2,1)} custom-call(s32[2,8]{1,0:T(2,128)S(1)} %bitcast.13, s32[1]{0:T(128)S(6)} %copy.6.rot_ref, bf16[16,64,128]{2,1,0:T(8,128)(2,1)S(1)} %bitcast.11), custom_call_target="tpu_custom_call" | custom-call | tf_op jit(solution)/shard_map/pallas_call | solution.py:328
  (2 shorter events, 0.1 us)
Async XLA Ops:
  0.6 20.4 %copy-start = (f32[2,2,128,512]{3,2,1,0:T(8,128)S(1)}, f32[2,2,128,512]{3,2,1,0:T(8,128)}, u32[]{:S(2)}) copy-start(f32[2,2,128,512]{3,2,1,0:T(8,128)} %refs_4_.1) | copy-start | bytes 3145732
  3.1 17.9 %all-to-all-start = ((bf16[32,32,128]{2,1,0:T(8,128)(2,1)}), bf16[32,32,128]{2,1,0:T(8,128)(2,1)S(1)}, u32[]{:S(2)}, u32[]{:S(2)}) async-start(bf16[32,32,128]{2,1,0:T(8,128)(2,1)} %bitcast.1), calls=%async_computation | async-start | bytes 524288 | tf_op jit(solution)/shard_map/all_to_all | solution.py:276
  21.0 5.8 %collective-permute-start = (bf16[32,32,128]{2,1,0:T(8,128)(2,1)S(1)}, bf16[32,32,128]{2,1,0:T(8,128)(2,1)S(1)}, u32[]{:S(2)}, u32[]{:S(2)}) collective-permute-start(bf16[32,32,128]{2,1,0:T(8,128)(2,1)S(1)} %all-to-all-done.refs_0_), channel_id=1, source_target_pairs={{0,1},{1,0},{2,3},{3,2},{4,5},{5,4},{6,7},{7,6},{8,9},{9,8},{10,11... | collective-permute-start | bytes 786440 | tf_op jit(solution)/shard_map/ppermute | solution.py:236
  21.0 5.5 %collective-permute-start.1 = (bf16[128,512]{1,0:T(8,128)(2,1)S(1)}, bf16[128,512]{1,0:T(8,128)(2,1)S(1)}, u32[]{:S(2)}, u32[]{:S(2)}) collective-permute-start(bf16[128,512]{1,0:T(8,128)(2,1)S(1)} %get-tuple-element.12), channel_id=1, source_target_pairs={{0,1},{1,0},{2,3},{3,2},{4,5},{5,4},{6,7},{7,6},{8,9},{9,8},{10,11... | collective-permute-start | bytes 393224 | tf_op jit(solution)/shard_map/ppermute | solution.py:241
  21.6 4.9 %collective-permute-start.2 = (bf16[128,256]{1,0:T(8,128)(2,1)S(1)}, bf16[128,256]{1,0:T(8,128)(2,1)S(1)}, u32[]{:S(2)}, u32[]{:S(2)}) collective-permute-start(bf16[128,256]{1,0:T(8,128)(2,1)S(1)} %get-tuple-element.11), channel_id=1, source_target_pairs={{0,2},{1,3},{2,0},{3,1},{4,6},{5,7},{6,4},{7,5},{8,10},{9,11},{10,... | collective-permute-start | bytes 196616 | tf_op jit(solution)/shard_map/ppermute | solution.py:241
  22.1 4.4 %collective-permute-start.3 = (bf16[128,256]{1,0:T(8,128)(2,1)S(1)}, bf16[128,256]{1,0:T(8,128)(2,1)S(1)}, u32[]{:S(2)}, u32[]{:S(2)}) collective-permute-start(bf16[128,256]{1,0:T(8,128)(2,1)S(1)} %get-tuple-element.10), channel_id=1, source_target_pairs={{0,3},{1,2},{2,1},{3,0},{4,7},{5,6},{6,5},{7,4},{8,11},{9,10},{10,... | collective-permute-start | bytes 196616 | tf_op jit(solution)/shard_map/ppermute | solution.py:241
  29.3 2.6 %collective-permute-start.4 = (bf16[512,512]{1,0:T(8,128)(2,1)S(1)}, bf16[512,512]{1,0:T(8,128)(2,1)S(1)}, u32[]{:S(2)}, u32[]{:S(2)}) collective-permute-start(bf16[512,512]{1,0:T(8,128)(2,1)S(1)} %get-tuple-element.6.root_ref), channel_id=1, source_target_pairs={{0,1},{1,0},{2,3},{3,2},{4,5},{5,4},{6,7},{7,6},{8,9},{9,8},{10,11... | collective-permute-start | bytes 1572872 | tf_op jit(solution)/shard_map/ppermute | solution.py:241
  29.9 8.3 %collective-permute-start.5 = (bf16[32,32,128]{2,1,0:T(8,128)(2,1)S(1)}, bf16[32,32,128]{2,1,0:T(8,128)(2,1)S(1)}, u32[]{:S(2)}, u32[]{:S(2)}) collective-permute-start(bf16[32,32,128]{2,1,0:T(8,128)(2,1)S(1)} %all-to-all-done.refs_0_), channel_id=1, source_target_pairs={{0,2},{1,3},{2,0},{3,1},{4,6},{5,7},{6,4},{7,5},{8,10},{9,11},{10,... | collective-permute-start | bytes 786440 | tf_op jit(solution)/shard_map/ppermute | solution.py:233
  33.6 13.2 %all-to-all-start.1 = ((bf16[32,32,128]{2,1,0:T(8,128)(2,1)}), bf16[32,32,128]{2,1,0:T(8,128)(2,1)S(1)}, u32[]{:S(2)}, u32[]{:S(2)}) async-start(bf16[32,32,128]{2,1,0:T(8,128)(2,1)} %shard_map.63), calls=%async_computation.1 | async-start | bytes 524288 | tf_op jit(solution)/shard_map/all_to_all | solution.py:307
  38.2 1.5 %collective-permute-start.6 = (bf16[32,32,128]{2,1,0:T(8,128)(2,1)S(1)}, bf16[32,32,128]{2,1,0:T(8,128)(2,1)S(1)}, u32[]{:S(2)}, u32[]{:S(2)}) collective-permute-start(bf16[32,32,128]{2,1,0:T(8,128)(2,1)S(1)} %collective-permute-done.5.refs_2_), channel_id=1, source_target_pairs={{0,1},{1,0},{2,3},{3,2},{4,5},{5,4},{6,7},{7,6},{8,9},{9,8},{10,11... | collective-permute-start | bytes 786440 | tf_op jit(solution)/shard_map/ppermute | solution.py:236
  41.5 5.2 %copy-start.1 = (s32[8,2]{0,1:T(2,128)S(1)}, s32[8,2]{0,1:T(2,128)}, u32[]{:S(2)}) copy-start(s32[8,2]{0,1:T(2,128)} %param.6) | copy-start | bytes 196

commit v4 on v2

v4 whole, which is shorter than its diff:
```python
import functools

import jax
import jax.numpy as jnp
from jax import lax
from jax.experimental import pallas as pl
from jax.experimental.pallas import tpu as pltpu
from jax.sharding import PartitionSpec as P


ITERS = 2


decay_rate = 0.9
damping = 1.0
bf16 = jnp.bfloat16
f32 = jnp.float32


def owner_of(owners_ref, rot, o, s, dp_count):
    row = o - rot
    return owners_ref[s, jnp.where(row < 0, row + dp_count, row)]


def each(count, one):
    lax.fori_loop(0, count, lambda j, carry: (one(j), carry)[1], 0, unroll=count <= 16)


def pick_kernel(
    owners_hbm, rot_ref, tiles_hbm, stats_hbm, out_ref, far_ref, near_ref, owners_ref, tiles_ref, far_scr, near_scr, sems,
    *, dp_count, parts
):
    slots = owners_ref.shape[0]
    half = far_scr.shape[2]
    slot = lax.axis_index("mp") // parts
    columns = pl.ds(pl.multiple_of(slot * half, half), half)
    pairs = (
        (owners_hbm, owners_ref),
        (tiles_hbm, tiles_ref),
        (stats_hbm.at[1 - slot, :, :, columns], far_scr),
        (stats_hbm.at[slot], near_scr),
    )
    copies = [pltpu.make_async_copy(a, b, sems.at[i]) for i, (a, b) in enumerate(pairs)]
    for copy in copies:
        copy.start()
    rot = rot_ref[0]
    copies[0].wait()
    copies[1].wait()

    def move(j):
        out_ref[j] = tiles_ref[owner_of(owners_ref, rot, j // slots, j % slots, dp_count)]

    each(dp_count * slots, move)
    copies[2].wait()
    far_ref[...] = far_scr[...].astype(bf16)
    copies[3].wait()
    near_ref[...] = near_scr[...].astype(bf16)


def place_kernel(owners_ref, rot_ref, in_ref, out_hbm, sems, *, dp_count, slots):
    rot = rot_ref[0]

    def copy(j):
        block = owner_of(owners_ref, rot, j // slots, j % slots, dp_count)
        return pltpu.make_async_copy(in_ref.at[j], out_hbm.at[block], sems.at[j])

    each(dp_count * slots, lambda j: copy(j).start())
    each(dp_count * slots, lambda j: copy(j).wait())


def dot(a, b, dims=(((1,), (0,)), ((), ()))):
    return lax.dot_general(a, b, dims, preferred_element_type=f32)


def gather_grad(g_refs, g_scr, part, *, dp_count, mp_count, parts, piece_rows, tile_cols):
    for k, g_ref in enumerate(g_refs):
        piece = part - k
        at = pl.multiple_of(jnp.where(piece < 0, piece + parts, piece) * piece_rows, piece_rows)
        for o in range(dp_count):
            for m in range(mp_count):
                rows = pl.ds(o * parts * piece_rows + at, piece_rows)
                g_scr[rows, m * tile_cols : (m + 1) * tile_cols] = g_ref[o * mp_count + m]


def base_kernel(*refs, parts, slots):
    s_refs, (out_ref, s_scr) = refs[:-2], refs[-2:]
    order = out_ref.shape[1]
    rows = s_refs[0].shape[1]
    half = rows * parts
    my_index = lax.axis_index("mp")
    slot, part = my_index // parts, my_index % parts
    for i, s_ref in enumerate(s_refs):
        k, j = i // slots, i % slots
        source = (slot - j + slots) % slots * parts + (part - k + parts) % parts
        at = pl.multiple_of(source * rows, rows)
        if s_ref.shape[2] == order:
            s_scr[:, pl.ds(at, rows), :] = s_ref[...]
            continue
        for g in range(2):

            @pl.when(slot == g)
            def _():
                s_scr[:, pl.ds(at, rows), (1 - g) * half : (2 - g) * half] = s_ref[...]

    if slots == 2:
        for g in range(2):

            @pl.when(slot == g)
            def _():
                mine = slice(g * half, (g + 1) * half)
                other = slice((1 - g) * half, (2 - g) * half)
                for side in range(2):
                    s_scr[side, other, mine] = s_scr[side, mine, other].astype(f32).T.astype(bf16)

    ids = lax.broadcasted_iota(jnp.int32, (order, order), 0)
    eye = ids == lax.broadcasted_iota(jnp.int32, (order, order), 1)
    for side in range(2):
        out_ref[side] = decay_rate * s_scr[side].astype(f32) + jnp.where(eye, damping, 0.0)


def owner_kernel(*refs, n_g, split, sizes):
    g_refs, (base_ref, out_ref, g_scr, res_scr) = refs[:n_g], refs[n_g:]
    dp_count, mp_count, parts = sizes["dp_count"], sizes["mp_count"], sizes["parts"]
    piece_rows, tile_cols = sizes["piece_rows"], sizes["tile_cols"]
    order = g_scr.shape[0]
    part = lax.axis_index("mp") % parts
    if split:
        gather_grad(g_refs, g_scr, part, **sizes)
    else:
        g_scr[...] = g_refs[0][...]
    ids = lax.broadcasted_iota(jnp.int32, (order, order), 0)
    eye5 = jnp.where(ids == lax.broadcasted_iota(jnp.int32, (order, order), 1), 5.0, 0.0)
    grad = g_scr[...]

    def gram_of(side):
        return dot(grad, grad, (((1 - side,), (1 - side,)), ((), ())))

    def moment_of(side, gram):
        factor = (base_ref[side] + (1.0 - decay_rate) * gram).astype(bf16)
        norm = jnp.sum(jnp.square(factor.astype(f32)))
        return (2.5 / jnp.sqrt(norm) * factor.astype(f32)).astype(bf16)

    def step_of(moment):
        return ((eye5 - moment.astype(f32)) * 0.25).astype(bf16)

    def product(a, b):
        return dot(a, b).astype(bf16)

    grams = {1: gram_of(1), 0: gram_of(0)}
    moment = {1: moment_of(1, grams[1])}
    root = {1: step_of(moment[1])}
    for newton_step in range(ITERS - 1):
        step_t = {1: root[1] if newton_step == 0 else step_of(moment[1])}
        square = {1: product(step_t[1], step_t[1])}
        if newton_step == 0:
            moment[0] = moment_of(0, grams[0])
            root[0] = step_of(moment[0])
        else:
            root[1] = product(root[1], step_t[1])
        step_t[0] = root[0] if newton_step == 0 else step_of(moment[0])
        partial_m = {1: product(square[1], moment[1])}
        square[0] = product(step_t[0], step_t[0])
        if newton_step:
            root[0] = product(root[0], step_t[0])
        moment[1] = product(square[1], partial_m[1])
        partial_m[0] = product(square[0], moment[0])
        last = step_of(moment[1])
        moment[0] = product(square[0], partial_m[0])
    root[1] = product(root[1], last)
    last = step_of(moment[0])
    right_applied = product(grad, root[1])
    root[0] = product(root[0], last)
    res_scr[...] = dot(root[0], right_applied).astype(bf16)
    grad_norm = jnp.sqrt(jnp.sum(jnp.square(grad.astype(f32))))
    scale = grad_norm / (jnp.sqrt(jnp.sum(jnp.square(res_scr[...].astype(f32)))) + 1e-06)
    if not split:
        out_ref[...] = (res_scr[...].astype(f32) * scale).astype(bf16)
        return
    at = pl.multiple_of(part * piece_rows, piece_rows)
    for o in range(dp_count):
        for m in range(mp_count):
            from_rows = pl.ds(o * parts * piece_rows + at, piece_rows)
            piece = res_scr[from_rows, m * tile_cols : (m + 1) * tile_cols].astype(f32)
            out_ref[o * mp_count + m] = (piece * scale).astype(bf16)


def stats_kernel(*refs, sizes):
    g_refs, (old_hbm, new_ref, g_scr, old_ref, sem) = refs[:-5], refs[-5:]
    parts = sizes["parts"]
    slots = sizes["mp_count"] // parts
    rows = old_ref.shape[2]
    old = pltpu.make_async_copy(old_hbm, old_ref, sem)
    old.start()
    my_index = lax.axis_index("mp")
    at = pl.multiple_of(my_index * rows, rows)
    for j in range(slots):
        gather_grad(g_refs[j * parts : (j + 1) * parts], g_scr.at[j], my_index % parts, **sizes)
        slot = (my_index // parts - j + slots) % slots
        left = dot(g_scr[j, pl.ds(at, rows), :], g_scr[j], (((1,), (1,)), ((), ())))
        right = dot(g_scr[j, :, pl.ds(at, rows)], g_scr[j], (((0,), (0,)), ((), ())))
        if j == 0:
            old.wait()
        new_ref[slot, 0] = decay_rate * old_ref[slot, 0] + (1.0 - decay_rate) * left
        new_ref[slot, 1] = decay_rate * old_ref[slot, 1] + (1.0 - decay_rate) * right


VMEM = pl.BlockSpec(memory_space=pltpu.VMEM)
SMEM = pl.BlockSpec(memory_space=pltpu.SMEM)
HBM = pl.BlockSpec(memory_space=pltpu.HBM)


def in_hbm(x):
    return pltpu.with_memory_space_constraint(x, pltpu.HBM)


def call(kernel, out_shape, in_specs, scratch=(), out_specs=VMEM, vmem=8, flops=0):
    return pl.pallas_call(
        kernel,
        out_shape=out_shape,
        in_specs=in_specs,
        out_specs=out_specs,
        scratch_shapes=list(scratch),
        compiler_params=pltpu.CompilerParams(vmem_limit_bytes=vmem * 2**20),
        cost_estimate=pl.CostEstimate(flops=flops, transcendentals=0, bytes_accessed=0) if flops else None,
    )


def step(grad_tiles, factor_stats, owner_blocks, rotation):
    dp_count = lax.axis_size("dp")
    mp_count = lax.axis_size("mp")
    tile_rows, tile_cols = grad_tiles.shape[1:]
    slots = owner_blocks.shape[1]
    rows, order = factor_stats.shape[2:]
    parts = mp_count // slots
    piece_rows = tile_rows // parts
    split = piece_rows % 16 == 0 and tile_cols % 128 == 0 and rows == tile_cols
    my_index = lax.axis_index("mp")
    my_slot = my_index // parts
    my_part = my_index % parts
    owners = owner_blocks.T
    where = dict(dp_count=dp_count, slots=slots)
    sizes = dict(
        dp_count=dp_count, mp_count=mp_count, parts=parts, piece_rows=piece_rows, tile_cols=tile_cols
    )
    table = pltpu.SMEM(owners.shape, jnp.int32)

    def to_slot(x, ahead):
        return lax.ppermute(x, "mp", [(i, (i + ahead * parts) % mp_count) for i in range(mp_count)])

    def to_part(x, ahead):
        return lax.ppermute(
            x, "mp", [(i, i // parts * parts + (i + ahead) % parts) for i in range(mp_count)]
        )

    def all_pieces(x):
        return [x] + [to_part(x, ahead) for ahead in range(1, parts)]

    def whole_grad(pieces):
        held = jnp.take(jnp.stack(pieces), (my_part - jnp.arange(parts)) % parts, axis=0)
        held = held.reshape(parts, dp_count, mp_count, piece_rows, tile_cols)
        return held.transpose(1, 0, 3, 2, 4).reshape(order, order)

    assert slots == 2
    half = rows * parts
    picked, far, near, table = call(
        functools.partial(pick_kernel, dp_count=dp_count, parts=parts),
        (
            pltpu.VMEM(grad_tiles.shape, bf16),
            pltpu.VMEM((2, rows, half), bf16),
            pltpu.VMEM((2, rows, order), bf16),
            pltpu.SMEM(owners.shape, jnp.int32),
        ),
        [HBM, SMEM, HBM, HBM],
        [
            pltpu.VMEM(grad_tiles.shape, bf16),
            pltpu.VMEM((2, rows, half), f32),
            pltpu.VMEM((2, rows, order), f32),
            pltpu.SemaphoreType.DMA((4,)),
        ],
        out_specs=(VMEM, VMEM, VMEM, SMEM),
    )(in_hbm(owners), rotation, in_hbm(grad_tiles), in_hbm(factor_stats))
    chunks = [near, to_slot(far, 1)]
    for ahead in range(1, parts):
        chunks.append(to_part(near, ahead))
        chunks.append(to_part(chunks[1], ahead))
    base = call(
        functools.partial(base_kernel, parts=parts, slots=slots),
        pltpu.VMEM((2, order, order), f32),
        [VMEM] * len(chunks),
        [pltpu.VMEM((2, order, order), bf16)],
        flops=order**2,
    )(*chunks)

    outgoing = picked.reshape(dp_count * mp_count, piece_rows, tile_cols)
    arrived = lax.all_to_all(outgoing, ("dp", "mp"), split_axis=0, concat_axis=0, tiled=True)
    pieces = all_pieces(arrived)
    theirs = [to_slot(arrived, ahead) for ahead in range(1, slots)]

    own_grad = pieces if split else [whole_grad(pieces)]
    result = call(
        functools.partial(owner_kernel, n_g=len(own_grad), split=split, sizes=sizes),
        pltpu.HBM(arrived.shape if split else (order, order), bf16),
        [VMEM] * (len(own_grad) + 1),
        [pltpu.VMEM((order, order), bf16), pltpu.VMEM((order, order), bf16)],
        vmem=24,
        flops=24 * order**3,
    )(*own_grad, base)
    if not split:
        result = result.reshape(dp_count, parts, piece_rows, mp_count, tile_cols)
        result = lax.dynamic_index_in_dim(result, my_part, 1, keepdims=False)
        result = result.transpose(0, 2, 1, 3).reshape(dp_count * mp_count, piece_rows, tile_cols)
    returned = lax.all_to_all(result, ("dp", "mp"), split_axis=0, concat_axis=0, tiled=True)

    grads = [pieces] + [all_pieces(x) for x in theirs]
    if split:
        new_stats = call(
            functools.partial(stats_kernel, sizes=sizes),
            jax.ShapeDtypeStruct(factor_stats.shape, f32),
            [VMEM] * (slots * parts) + [HBM],
            [
                pltpu.VMEM((slots, order, order), bf16),
                pltpu.VMEM(factor_stats.shape, f32),
                pltpu.SemaphoreType.DMA,
            ],
            vmem=16,
            flops=4 * slots * rows * order**2,
        )(*[x for slot_pieces in grads for x in slot_pieces], in_hbm(factor_stats))
    else:
        blocks = jnp.stack([whole_grad(x) for x in grads])
        blocks = jnp.take(blocks, (my_slot - jnp.arange(slots)) % slots, axis=0)
        row_part = lax.dynamic_slice_in_dim(blocks, my_index * rows, rows, 1)
        col_part = lax.dynamic_slice_in_dim(blocks, my_index * rows, rows, 2)
        left = jnp.einsum("kij,klj->kil", row_part, blocks, preferred_element_type=f32)
        right = jnp.einsum("kji,kjl->kil", col_part, blocks, preferred_element_type=f32)
        new_stats = decay_rate * factor_stats + (1.0 - decay_rate) * jnp.stack([left, right], axis=1)

    preconditioned = call(
        functools.partial(place_kernel, **where),
        jax.ShapeDtypeStruct(grad_tiles.shape, bf16),
        [SMEM, SMEM, VMEM],
        [pltpu.SemaphoreType.DMA((dp_count * slots,))],
        out_specs=HBM,
    )(table, rotation, returned.reshape(grad_tiles.shape))
    return (preconditioned, new_stats)


def solution(mesh):
    return placed(mesh)


def placed(mesh):
    return jax.shard_map(
        step,
        mesh=mesh,
        in_specs=(P(None, "dp", "mp"), P("dp", None, "mp", None), P(), P()),
        out_specs=(P(None, "dp", "mp"), P("dp", None, "mp", None)),
        check_vma=False,
    )
```

time: 48.2 us -> 44 us (0.913)
  starting transfers between devices: 15.8 us -> 13.6 us
  local copies, waits for them, and re-layouts: 1.7 us -> 0 us
  waiting for transfers between devices: 18 us -> 17.3 us
    ppermute x2, waiting for transfers between devices: 9.33 us -> 0.01 us  [to_slot(): lax.ppermute(x, 'mp', [(i, (i + ahead * parts) % mp_count) for i in range...]
    all_to_all x2, waiting for transfers between devices: 7.19 us -> 14.8 us  [the longest x1 8.74 us: step(): lax.all_to_all(outgoing, ('dp', 'mp'), split_axis=0, concat_axis=0, tiled...]
    unnamed x8 -> x0, local copies, waits for them, and re-layouts: 1.63 us -> none
    all_to_all x2, starting transfers between devices: 11.9 us -> 10.4 us  [the longest x1 7.33 us: step(): lax.all_to_all(outgoing, ('dp', 'mp'), split_axis=0, concat_axis=0, tiled...]
    ppermute x4, waiting for transfers between devices: 1.44 us -> 2.5 us  [to_part(): lax.ppermute(x, 'mp', [(i, i // parts * parts + (i + ahead) % parts) for...]
    ppermute x2, starting transfers between devices: 3.07 us -> 2.35 us  [to_slot(): lax.ppermute(x, 'mp', [(i, (i + ahead * parts) % mp_count) for i in range...]
    pallas_call x4 -> x5, Pallas kernels: 11 us -> 11.4 us  [the longest x1 5.4 us: step(): call(functools.partial(owner_kernel, n_g=len(own_grad), split=split, size...]
  transfers between devices with their start and end apart: 8 -> 8, of which waited for: 4 -> 4; matrix products, arithmetic and copies ran while one was open for 0% -> 0% of each run, Pallas kernels for 18% -> 20%
where the time goes in v4:
time: 44 us; the launch traced here: 43.7 us
  waiting for transfers between devices  17.3 us (39%)
  starting transfers between devices  13.6 us (31%)
  Pallas kernels  11.4 us (26%)
  between operations  1.33 us (3%)
    all_to_all x1, waiting for transfers between devices, step(): lax.all_to_all(outgoing, ('dp', 'mp'), split_axis=0, concat_axis=0, tiled...  8.74 us
    all_to_all x1, starting transfers between devices, step(): lax.all_to_all(outgoing, ('dp', 'mp'), split_axis=0, concat_axis=0, tiled...  7.33 us
    all_to_all x1, waiting for transfers between devices, step(): lax.all_to_all(result, ('dp', 'mp'), split_axis=0, concat_axis=0, tiled=T...  6.09 us
    pallas_call x1, Pallas kernels, step(): call(functools.partial(owner_kernel, n_g=len(own_grad), split=split, size...  5.4 us
    all_to_all x1, starting transfers between devices, step(): lax.all_to_all(result, ('dp', 'mp'), split_axis=0, concat_axis=0, tiled=T...  3.1 us
    pallas_call x1, Pallas kernels, step(): call(functools.partial(stats_kernel, sizes=sizes), jax.ShapeDtypeStruct(f...  2.87 us
    ppermute x4, waiting for transfers between devices, to_part(): lax.ppermute(x, 'mp', [(i, i // parts * parts + (i + ahead) % parts) for...  2.5 us
    ppermute x2, starting transfers between devices, to_slot(): lax.ppermute(x, 'mp', [(i, (i + ahead * parts) % mp_count) for i in range...  2.35 us
  transfers between devices with their start and end apart: 8, of which 4 were waited for; matrix products, arithmetic and copies ran while one was open for 0% of the time, Pallas kernels for 20%

profile of v4, /device:TPU:0, one launch (start us, length us, event | category | flops | bytes accessed | tf_op | source)
XLA Modules:
  0.0 43.7 jit_solution(6136955853613915667)
XLA Ops:
  1.3 1.9 %shard_map.59 = (bf16[16,64,128]{2,1,0:T(8,128)(2,1)}, bf16[2,128,256]{2,1,0:T(8,128)(2,1)S(1)}, bf16[2,128,512]{2,1,0:T(8,128)(2,1)S(1)}, s32[2,8]{1,0:T(2,128)S(4)}) custom-call(s32[2,8]{1,0:T(2,128)} %bitcast.4, s32[1]{0:T(128)S(6)} %copy.6.rot_ref, bf16[16,64,128]{2,1,0:T(8,128)(2,1)} %tiles_hbm.1, f32[2,2,128,512]{3,2,1,0:T(8,128)} %refs_4_.1), custom_call_target="tpu_custom_call" | custom-call | tf_op jit(solution)/shard_map/pallas_call | solution.py:265
  3.2 7.3 %all-to-all-start = ((bf16[32,32,128]{2,1,0:T(8,128)(2,1)}), bf16[32,32,128]{2,1,0:T(8,128)(2,1)S(1)}, u32[]{:S(2)}, u32[]{:S(2)}) async-start(bf16[32,32,128]{2,1,0:T(8,128)(2,1)} %bitcast.1), calls=%async_computation | async-start | bytes 524288 | tf_op jit(solution)/shard_map/all_to_all | solution.py:295
  10.6 1.8 %collective-permute-start.1 = (bf16[2,128,256]{2,1,0:T(8,128)(2,1)S(1)}, bf16[2,128,256]{2,1,0:T(8,128)(2,1)S(1)}, u32[]{:S(2)}, u32[]{:S(2)}) collective-permute-start(bf16[2,128,256]{2,1,0:T(8,128)(2,1)S(1)} %get-tuple-element.9), channel_id=1, source_target_pairs={{0,2},{1,3},{2,0},{3,1},{4,6},{5,7},{6,4},{7,5},{8,10},{9,11},{10,... | collective-permute-start | bytes 393224 | tf_op jit(solution)/shard_map/ppermute | solution.py:248
  12.4 0.0 collective-permute-start.2
  12.4 8.7 %all-to-all-done.refs_0_ = bf16[32,32,128]{2,1,0:T(8,128)(2,1)S(1)} async-done(((bf16[32,32,128]{2,1,0:T(8,128)(2,1)}), bf16[32,32,128]{2,1,0:T(8,128)(2,1)S(1)}, u32[]{:S(2)}, u32[]{:S(2)}) %all-to-all-start) | async-done | bytes 262176 | tf_op jit(solution)/shard_map/all_to_all | solution.py:295
  21.1 0.0 collective-permute-start
  21.1 0.0 collective-permute-done.1.refs_1_
  21.1 0.5 %collective-permute-start.3 = (bf16[2,128,256]{2,1,0:T(8,128)(2,1)S(1)}, bf16[2,128,256]{2,1,0:T(8,128)(2,1)S(1)}, u32[]{:S(2)}, u32[]{:S(2)}) collective-permute-start(bf16[2,128,256]{2,1,0:T(8,128)(2,1)S(1)} %collective-permute-done.1.refs_1_), channel_id=1, source_target_pairs={{0,1},{1,0},{2,3},{3,2},{4,5},{5,4},{6,7},{7,6},{8,9},{9,8},{10,11... | collective-permute-start | bytes 393224 | tf_op jit(solution)/shard_map/ppermute | solution.py:251
  21.7 1.2 %collective-permute-done.3.refs_3_ = bf16[2,128,256]{2,1,0:T(8,128)(2,1)S(1)} collective-permute-done((bf16[2,128,256]{2,1,0:T(8,128)(2,1)S(1)}, bf16[2,128,256]{2,1,0:T(8,128)(2,1)S(1)}, u32[]{:S(2)}, u32[]{:S(2)}) %collective-permute-start.3) | collective-permute-done | bytes 131104 | tf_op jit(solution)/shard_map/ppermute | solution.py:251
  22.9 0.0 collective-permute-done.2.refs_2_
  22.9 0.4 shard_map.60.refs_2_
  23.3 0.5 %collective-permute-start.4 = (bf16[32,32,128]{2,1,0:T(8,128)(2,1)S(1)}, bf16[32,32,128]{2,1,0:T(8,128)(2,1)S(1)}, u32[]{:S(2)}, u32[]{:S(2)}) collective-permute-start(bf16[32,32,128]{2,1,0:T(8,128)(2,1)S(1)} %all-to-all-done.refs_0_), channel_id=1, source_target_pairs={{0,2},{1,3},{2,0},{3,1},{4,6},{5,7},{6,4},{7,5},{8,10},{9,11},{10,... | collective-permute-start | bytes 786440 | tf_op jit(solution)/shard_map/ppermute | solution.py:248
  23.8 0.0 collective-permute-done.refs_1_
  23.8 5.4 %shard_map.61 = bf16[32,32,128]{2,1,0:T(8,128)(2,1)} custom-call(bf16[32,32,128]{2,1,0:T(8,128)(2,1)S(1)} %all-to-all-done.refs_0_, bf16[32,32,128]{2,1,0:T(8,128)(2,1)S(1)} %collective-permute-done.refs_1_, f32[2,512,512]{2,1,0:T(8,128)S(1)} %shard_map.60.refs_2_), custom_call_target="tpu_custom_call" | custom-call | flops 3221225472 | tf_op jit(solution)/shard_map/pallas_call | solution.py:300
  29.2 3.1 %all-to-all-start.1 = ((bf16[32,32,128]{2,1,0:T(8,128)(2,1)}), bf16[32,32,128]{2,1,0:T(8,128)(2,1)S(1)}, u32[]{:S(2)}, u32[]{:S(2)}) async-start(bf16[32,32,128]{2,1,0:T(8,128)(2,1)} %shard_map.61), calls=%async_computation.1 | async-start | bytes 524288 | tf_op jit(solution)/shard_map/all_to_all | solution.py:312
  32.3 0.0 collective-permute-done.4.refs_2_
  32.3 0.3 collective-permute-start.5
  32.6 1.3 %collective-permute-done.5.refs_3_ = bf16[32,32,128]{2,1,0:T(8,128)(2,1)S(1)} collective-permute-done((bf16[32,32,128]{2,1,0:T(8,128)(2,1)S(1)}, bf16[32,32,128]{2,1,0:T(8,128)(2,1)S(1)}, u32[]{:S(2)}, u32[]{:S(2)}) %collective-permute-start.5) | collective-permute-done | bytes 262176 | tf_op jit(solution)/shard_map/ppermute | solution.py:251
  33.9 2.9 %shard_map.63 = f32[2,2,128,512]{3,2,1,0:T(8,128)} custom-call(bf16[32,32,128]{2,1,0:T(8,128)(2,1)S(1)} %all-to-all-done.refs_0_, bf16[32,32,128]{2,1,0:T(8,128)(2,1)S(1)} %collective-permute-done.refs_1_, bf16[32,32,128]{2,1,0:T(8,128)(2,1)S(1)} %collective-permute-done.4.refs_2_, bf16[32,32,128]{2,1,0:T(8,128)(2,1)S(1)} %collective-permute-done.5.refs_3_, ...), custom_call_target="tpu_custom_call" | custom-call | flops 268435456 | tf_op jit(solution)/shard_map/pallas_call | solution.py:316
  36.8 6.1 %all-to-all-done.1 = bf16[32,32,128]{2,1,0:T(8,128)(2,1)S(1)} async-done(((bf16[32,32,128]{2,1,0:T(8,128)(2,1)}), bf16[32,32,128]{2,1,0:T(8,128)(2,1)S(1)}, u32[]{:S(2)}, u32[]{:S(2)}) %all-to-all-start.1) | async-done | bytes 262176 | tf_op jit(solution)/shard_map/all_to_all | solution.py:312
  42.9 0.8 %shard_map.62 = bf16[16,64,128]{2,1,0:T(8,128)(2,1)} custom-call(s32[2,8]{1,0:T(2,128)S(4)} %get-tuple-element.6.owners_ref, s32[1]{0:T(128)S(6)} %copy.6.rot_ref, bf16[16,64,128]{2,1,0:T(8,128)(2,1)S(1)} %bitcast.3), custom_call_target="tpu_custom_call" | custom-call | tf_op jit(solution)/shard_map/pallas_call | solution.py:337
Async XLA Ops:
  3.2 17.9 %all-to-all-start = ((bf16[32,32,128]{2,1,0:T(8,128)(2,1)}), bf16[32,32,128]{2,1,0:T(8,128)(2,1)S(1)}, u32[]{:S(2)}, u32[]{:S(2)}) async-start(bf16[32,32,128]{2,1,0:T(8,128)(2,1)} %bitcast.1), calls=%async_computation | async-start | bytes 524288 | tf_op jit(solution)/shard_map/all_to_all | solution.py:295
  10.6 10.6 %collective-permute-start.1 = (bf16[2,128,256]{2,1,0:T(8,128)(2,1)S(1)}, bf16[2,128,256]{2,1,0:T(8,128)(2,1)S(1)}, u32[]{:S(2)}, u32[]{:S(2)}) collective-permute-start(bf16[2,128,256]{2,1,0:T(8,128)(2,1)S(1)} %get-tuple-element.9), channel_id=1, source_target_pairs={{0,2},{1,3},{2,0},{3,1},{4,6},{5,7},{6,4},{7,5},{8,10},{9,11},{10,... | collective-permute-start | bytes 393224 | tf_op jit(solution)/shard_map/ppermute | solution.py:248
  12.4 10.5 %collective-permute-start.2 = (bf16[2,128,512]{2,1,0:T(8,128)(2,1)S(1)}, bf16[2,128,512]{2,1,0:T(8,128)(2,1)S(1)}, u32[]{:S(2)}, u32[]{:S(2)}) collective-permute-start(bf16[2,128,512]{2,1,0:T(8,128)(2,1)S(1)} %get-tuple-element.8.refs_0_), channel_id=1, source_target_pairs={{0,1},{1,0},{2,3},{3,2},{4,5},{5,4},{6,7},{7,6},{8,9},{9,8},{10,11... | collective-permute-start | bytes 786440 | tf_op jit(solution)/shard_map/ppermute | solution.py:251
  21.1 2.7 %collective-permute-start = (bf16[32,32,128]{2,1,0:T(8,128)(2,1)S(1)}, bf16[32,32,128]{2,1,0:T(8,128)(2,1)S(1)}, u32[]{:S(2)}, u32[]{:S(2)}) collective-permute-start(bf16[32,32,128]{2,1,0:T(8,128)(2,1)S(1)} %all-to-all-done.refs_0_), channel_id=1, source_target_pairs={{0,1},{1,0},{2,3},{3,2},{4,5},{5,4},{6,7},{7,6},{8,9},{9,8},{10,11... | collective-permute-start | bytes 786440 | tf_op jit(solution)/shard_map/ppermute | solution.py:251
  21.1 1.7 %collective-permute-start.3 = (bf16[2,128,256]{2,1,0:T(8,128)(2,1)S(1)}, bf16[2,128,256]{2,1,0:T(8,128)(2,1)S(1)}, u32[]{:S(2)}, u32[]{:S(2)}) collective-permute-start(bf16[2,128,256]{2,1,0:T(8,128)(2,1)S(1)} %collective-permute-done.1.refs_1_), channel_id=1, source_target_pairs={{0,1},{1,0},{2,3},{3,2},{4,5},{5,4},{6,7},{7,6},{8,9},{9,8},{10,11... | collective-permute-start | bytes 393224 | tf_op jit(solution)/shard_map/ppermute | solution.py:251
  23.3 9.0 %collective-permute-start.4 = (bf16[32,32,128]{2,1,0:T(8,128)(2,1)S(1)}, bf16[32,32,128]{2,1,0:T(8,128)(2,1)S(1)}, u32[]{:S(2)}, u32[]{:S(2)}) collective-permute-start(bf16[32,32,128]{2,1,0:T(8,128)(2,1)S(1)} %all-to-all-done.refs_0_), channel_id=1, source_target_pairs={{0,2},{1,3},{2,0},{3,1},{4,6},{5,7},{6,4},{7,5},{8,10},{9,11},{10,... | collective-permute-start | bytes 786440 | tf_op jit(solution)/shard_map/ppermute | solution.py:248
  29.2 13.7 %all-to-all-start.1 = ((bf16[32,32,128]{2,1,0:T(8,128)(2,1)}), bf16[32,32,128]{2,1,0:T(8,128)(2,1)S(1)}, u32[]{:S(2)}, u32[]{:S(2)}) async-start(bf16[32,32,128]{2,1,0:T(8,128)(2,1)} %shard_map.61), calls=%async_computation.1 | async-start | bytes 524288 | tf_op jit(solution)/shard_map/all_to_all | solution.py:312
  32.3 1.6 %collective-permute-start.5 = (bf16[32,32,128]{2,1,0:T(8,128)(2,1)S(1)}, bf16[32,32,128]{2,1,0:T(8,128)(2,1)S(1)}, u32[]{:S(2)}, u32[]{:S(2)}) collective-permute-start(bf16[32,32,128]{2,1,0:T(8,128)(2,1)S(1)} %collective-permute-done.4.refs_2_), channel_id=1, source_target_pairs={{0,1},{1,0},{2,3},{3,2},{4,5},{5,4},{6,7},{7,6},{8,9},{9,8},{10,11... | collective-permute-start | bytes 786440 | tf_op jit(solution)/shard_map/ppermute | solution.py:251

commit v5 on v4

--- a/solution.py
+++ b/solution.py
@@ -82,40 +82,48 @@
                 g_scr[rows, m * tile_cols : (m + 1) * tile_cols] = g_ref[o * mp_count + m]
 
 
-def base_kernel(*refs, parts, slots):
+def diagonal(shape, value):
+    ids = lax.broadcasted_iota(jnp.int32, shape, 0)
+    return jnp.where(ids == lax.broadcasted_iota(jnp.int32, shape, 1), value, 0.0)
+
+
+def near_base_kernel(*refs, parts):
     s_refs, (out_ref, s_scr) = refs[:-2], refs[-2:]
-    order = out_ref.shape[1]
     rows = s_refs[0].shape[1]
     half = rows * parts
-    my_index = lax.axis_index("mp")
-    slot, part = my_index // parts, my_index % parts
-    for i, s_ref in enumerate(s_refs):
-        k, j = i // slots, i % slots
-        source = (slot - j + slots) % slots * parts + (part - k + parts) % parts
-        at = pl.multiple_of(source * rows, rows)
-        if s_ref.shape[2] == order:
-            s_scr[:, pl.ds(at, rows), :] = s_ref[...]
-            continue
-        for g in range(2):
-
-            @pl.when(slot == g)
-            def _():
-                s_scr[:, pl.ds(at, rows), (1 - g) * half : (2 - g) * half] = s_ref[...]
-
-    if slots == 2:
-        for g in range(2):
-
-            @pl.when(slot == g)
-            def _():
-                mine = slice(g * half, (g + 1) * half)
-                other = slice((1 - g) * half, (2 - g) * half)
-                for side in range(2):
-                    s_scr[side, other, mine] = s_scr[side, mine, other].astype(f32).T.astype(bf16)
-
-    ids = lax.broadcasted_iota(jnp.int32, (order, order), 0)
-    eye = ids == lax.broadcasted_iota(jnp.int32, (order, order), 1)
-    for side in range(2):
-        out_ref[side] = decay_rate * s_scr[side].astype(f32) + jnp.where(eye, damping, 0.0)
+    slot, part = lax.axis_index("mp") // parts, lax.axis_index("mp") % parts
+    for k, s_ref in enumerate(s_refs):
+        at = pl.multiple_of((part - k + parts) % parts * rows, rows)
+        s_scr[:, pl.ds(at, rows), :] = s_ref[...]
+    for g in range(2):
+
+        @pl.when(slot == g)
+        def _():
+            mine = slice(g * half, (g + 1) * half)
+            other = slice((1 - g) * half, (2 - g) * half)
+            for side in range(2):
+                square = decay_rate * s_scr[side, :, mine].astype(f32)
+                out_ref[side, mine, mine] = square + diagonal((half, half), damping)
+                across = decay_rate * s_scr[side, :, other].astype(f32)
+                out_ref[side, mine, other] = across
+                out_ref[side, other, mine] = across.T
+
+
+def far_base_kernel(base_ref, *refs, parts):
+    s_refs, (out_ref, s_scr) = refs[:-2], refs[-2:]
+    rows, half = s_refs[0].shape[1:]
+    slot, part = lax.axis_index("mp") // parts, lax.axis_index("mp") % parts
+    for k, s_ref in enumerate(s_refs):
+        at = pl.multiple_of((part - k + parts) % parts * rows, rows)
+        s_scr[:, pl.ds(at, rows), :] = s_ref[...]
+    for g in range(2):
+
+        @pl.when(slot == g)
+        def _():
+            other = slice((1 - g) * half, (2 - g) * half)
+            for side in range(2):
+                square = decay_rate * s_scr[side].astype(f32)
+                out_ref[side, other, other] = square + diagonal((half, half), damping)
 
 
 def owner_kernel(*refs, n_g, split, sizes):
@@ -128,8 +136,7 @@
         gather_grad(g_refs, g_scr, part, **sizes)
     else:
         g_scr[...] = g_refs[0][...]
-    ids = lax.broadcasted_iota(jnp.int32, (order, order), 0)
-    eye5 = jnp.where(ids == lax.broadcasted_iota(jnp.int32, (order, order), 1), 5.0, 0.0)
+    eye5 = diagonal((order, order), 5.0)
     grad = g_scr[...]
 
     def gram_of(side):
@@ -167,11 +174,11 @@
         last = step_of(moment[1])
         moment[0] = product(square[0], partial_m[0])
     root[1] = product(root[1], last)
+    grad_norm = jnp.sqrt(jnp.sum(jnp.square(grad.astype(f32))))
     last = step_of(moment[0])
     right_applied = product(grad, root[1])
     root[0] = product(root[0], last)
     res_scr[...] = dot(root[0], right_applied).astype(bf16)
-    grad_norm = jnp.sqrt(jnp.sum(jnp.square(grad.astype(f32))))
     scale = grad_norm / (jnp.sqrt(jnp.sum(jnp.square(res_scr[...].astype(f32)))) + 1e-06)
     if not split:
         out_ref[...] = (res_scr[...].astype(f32) * scale).astype(bf16)
@@ -213,13 +220,14 @@
     return pltpu.with_memory_space_constraint(x, pltpu.HBM)
 
 
-def call(kernel, out_shape, in_specs, scratch=(), out_specs=VMEM, vmem=8, flops=0):
+def call(kernel, out_shape, in_specs, scratch=(), out_specs=VMEM, vmem=8, flops=0, aliases=None):
     return pl.pallas_call(
         kernel,
         out_shape=out_shape,
         in_specs=in_specs,
         out_specs=out_specs,
         scratch_shapes=list(scratch),
+        input_output_aliases=aliases or {},
         compiler_params=pltpu.CompilerParams(vmem_limit_bytes=vmem * 2**20),
         cost_estimate=pl.CostEstimate(flops=flops, transcendentals=0, bytes_accessed=0) if flops else None,
     )
@@ -283,13 +291,22 @@
     for ahead in range(1, parts):
         chunks.append(to_part(near, ahead))
         chunks.append(to_part(chunks[1], ahead))
+    base_type = pltpu.VMEM((2, order, order), f32)
     base = call(
-        functools.partial(base_kernel, parts=parts, slots=slots),
-        pltpu.VMEM((2, order, order), f32),
-        [VMEM] * len(chunks),
-        [pltpu.VMEM((2, order, order), bf16)],
+        functools.partial(near_base_kernel, parts=parts),
+        base_type,
+        [VMEM] * parts,
+        [pltpu.VMEM((2, half, order), bf16)],
         flops=order**2,
-    )(*chunks)
+    )(*chunks[0::2])
+    base = call(
+        functools.partial(far_base_kernel, parts=parts),
+        base_type,
+        [VMEM] * (parts + 1),
+        [pltpu.VMEM((2, half, half), bf16)],
+        flops=order**2,
+        aliases={0: 0},
+    )(base, *chunks[1::2])
 
     outgoing = picked.reshape(dp_count * mp_count, piece_rows, tile_cols)
     arrived = lax.all_to_all(outgoing, ("dp", "mp"), split_axis=0, concat_axis=0, tiled=True)

time: 44 us -> 43.8 us (level)
  no operation moved by 1% of the time
where the time goes in v5:
time: 43.8 us; the launch traced here: 43.5 us
  waiting for transfers between devices  16.9 us (39%)
  starting transfers between devices  13.8 us (32%)
  Pallas kernels  11.4 us (26%)
  between operations  1.34 us (3%)
    all_to_all x1, waiting for transfers between devices, step(): lax.all_to_all(outgoing, ('dp', 'mp'), split_axis=0, concat_axis=0, tiled...  8.62 us
    all_to_all x1, starting transfers between devices, step(): lax.all_to_all(outgoing, ('dp', 'mp'), split_axis=0, concat_axis=0, tiled...  7.33 us
    all_to_all x1, waiting for transfers between devices, step(): lax.all_to_all(result, ('dp', 'mp'), split_axis=0, concat_axis=0, tiled=T...  6.09 us
    pallas_call x1, Pallas kernels, step(): call(functools.partial(owner_kernel, n_g=len(own_grad), split=split, size...  5.41 us
    all_to_all x1, starting transfers between devices, step(): lax.all_to_all(result, ('dp', 'mp'), split_axis=0, concat_axis=0, tiled=T...  3.22 us
    pallas_call x1, Pallas kernels, step(): call(functools.partial(stats_kernel, sizes=sizes), jax.ShapeDtypeStruct(f...  2.87 us
    ppermute x4, waiting for transfers between devices, to_part(): lax.ppermute(x, 'mp', [(i, i // parts * parts + (i + ahead) % parts) for...  2.19 us
    ppermute x2, starting transfers between devices, to_slot(): lax.ppermute(x, 'mp', [(i, (i + ahead * parts) % mp_count) for i in range...  2.15 us
  transfers between devices with their start and end apart: 8, of which 4 were waited for; matrix products, arithmetic and copies ran while one was open for 0% of the time, Pallas kernels for 20%

profile of v5, /device:TPU:0, one launch (start us, length us, event | category | flops | bytes accessed | tf_op | source)
XLA Modules:
  0.0 43.5 jit_solution(8748779294112328278)
XLA Ops:
  1.3 1.9 %shard_map.59 = (bf16[16,64,128]{2,1,0:T(8,128)(2,1)}, bf16[2,128,256]{2,1,0:T(8,128)(2,1)S(1)}, bf16[2,128,512]{2,1,0:T(8,128)(2,1)S(1)}, s32[2,8]{1,0:T(2,128)S(4)}) custom-call(s32[2,8]{1,0:T(2,128)} %bitcast.4, s32[1]{0:T(128)S(6)} %copy.8.rot_ref, bf16[16,64,128]{2,1,0:T(8,128)(2,1)} %tiles_hbm.1, f32[2,2,128,512]{3,2,1,0:T(8,128)} %refs_4_.1), custom_call_target="tpu_custom_call" | custom-call | tf_op jit(solution)/shard_map/pallas_call | solution.py:273
  3.2 7.3 %all-to-all-start = ((bf16[32,32,128]{2,1,0:T(8,128)(2,1)}), bf16[32,32,128]{2,1,0:T(8,128)(2,1)S(1)}, u32[]{:S(2)}, u32[]{:S(2)}) async-start(bf16[32,32,128]{2,1,0:T(8,128)(2,1)} %bitcast.1), calls=%async_computation | async-start | bytes 524288 | tf_op jit(solution)/shard_map/all_to_all | solution.py:312
  10.6 0.3 collective-permute-start.1
  10.9 1.6 %collective-permute-start.2 = (bf16[2,128,256]{2,1,0:T(8,128)(2,1)S(1)}, bf16[2,128,256]{2,1,0:T(8,128)(2,1)S(1)}, u32[]{:S(2)}, u32[]{:S(2)}) collective-permute-start(bf16[2,128,256]{2,1,0:T(8,128)(2,1)S(1)} %get-tuple-element.9), channel_id=1, source_target_pairs={{0,2},{1,3},{2,0},{3,1},{4,6},{5,7},{6,4},{7,5},{8,10},{9,11},{10,... | collective-permute-start | bytes 393224 | tf_op jit(solution)/shard_map/ppermute | solution.py:256
  12.5 8.6 %all-to-all-done.refs_0_ = bf16[32,32,128]{2,1,0:T(8,128)(2,1)S(1)} async-done(((bf16[32,32,128]{2,1,0:T(8,128)(2,1)}), bf16[32,32,128]{2,1,0:T(8,128)(2,1)S(1)}, u32[]{:S(2)}, u32[]{:S(2)}) %all-to-all-start) | async-done | bytes 262176 | tf_op jit(solution)/shard_map/all_to_all | solution.py:312
  21.1 0.0 collective-permute-start
  21.1 0.0 collective-permute-done.2.refs_0_
  21.1 0.5 %collective-permute-start.3 = (bf16[2,128,256]{2,1,0:T(8,128)(2,1)S(1)}, bf16[2,128,256]{2,1,0:T(8,128)(2,1)S(1)}, u32[]{:S(2)}, u32[]{:S(2)}) collective-permute-start(bf16[2,128,256]{2,1,0:T(8,128)(2,1)S(1)} %collective-permute-done.2.refs_0_), channel_id=1, source_target_pairs={{0,1},{1,0},{2,3},{3,2},{4,5},{5,4},{6,7},{7,6},{8,9},{9,8},{10,11... | collective-permute-start | bytes 393224 | tf_op jit(solution)/shard_map/ppermute | solution.py:259
  21.7 0.0 collective-permute-done.1.refs_1_
  21.7 0.3 shard_map.60.base_ref
  22.0 0.9 %collective-permute-done.3.refs_1_ = bf16[2,128,256]{2,1,0:T(8,128)(2,1)S(1)} collective-permute-done((bf16[2,128,256]{2,1,0:T(8,128)(2,1)S(1)}, bf16[2,128,256]{2,1,0:T(8,128)(2,1)S(1)}, u32[]{:S(2)}, u32[]{:S(2)}) %collective-permute-start.3) | collective-permute-done | bytes 131104 | tf_op jit(solution)/shard_map/ppermute | solution.py:259
  22.9 0.1 shard_map.61.refs_2_
  23.0 0.5 %collective-permute-start.4 = (bf16[32,32,128]{2,1,0:T(8,128)(2,1)S(1)}, bf16[32,32,128]{2,1,0:T(8,128)(2,1)S(1)}, u32[]{:S(2)}, u32[]{:S(2)}) collective-permute-start(bf16[32,32,128]{2,1,0:T(8,128)(2,1)S(1)} %all-to-all-done.refs_0_), channel_id=1, source_target_pairs={{0,2},{1,3},{2,0},{3,1},{4,6},{5,7},{6,4},{7,5},{8,10},{9,11},{10,... | collective-permute-start | bytes 786440 | tf_op jit(solution)/shard_map/ppermute | solution.py:256
  23.5 0.0 collective-permute-done.refs_1_
  23.5 5.4 %shard_map.62 = bf16[32,32,128]{2,1,0:T(8,128)(2,1)} custom-call(bf16[32,32,128]{2,1,0:T(8,128)(2,1)S(1)} %all-to-all-done.refs_0_, bf16[32,32,128]{2,1,0:T(8,128)(2,1)S(1)} %collective-permute-done.refs_1_, f32[2,512,512]{2,1,0:T(8,128)S(1)} %shard_map.61.refs_2_), custom_call_target="tpu_custom_call" | custom-call | flops 3221225472 | tf_op jit(solution)/shard_map/pallas_call | solution.py:317
  28.9 3.2 %all-to-all-start.1 = ((bf16[32,32,128]{2,1,0:T(8,128)(2,1)}), bf16[32,32,128]{2,1,0:T(8,128)(2,1)S(1)}, u32[]{:S(2)}, u32[]{:S(2)}) async-start(bf16[32,32,128]{2,1,0:T(8,128)(2,1)} %shard_map.62), calls=%async_computation.1 | async-start | bytes 524288 | tf_op jit(solution)/shard_map/all_to_all | solution.py:329
  32.1 0.0 collective-permute-done.4.refs_2_
  32.1 0.3 collective-permute-start.5
  32.4 1.3 %collective-permute-done.5.refs_3_ = bf16[32,32,128]{2,1,0:T(8,128)(2,1)S(1)} collective-permute-done((bf16[32,32,128]{2,1,0:T(8,128)(2,1)S(1)}, bf16[32,32,128]{2,1,0:T(8,128)(2,1)S(1)}, u32[]{:S(2)}, u32[]{:S(2)}) %collective-permute-start.5) | collective-permute-done | bytes 262176 | tf_op jit(solution)/shard_map/ppermute | solution.py:259
  33.7 2.9 %shard_map.64 = f32[2,2,128,512]{3,2,1,0:T(8,128)} custom-call(bf16[32,32,128]{2,1,0:T(8,128)(2,1)S(1)} %all-to-all-done.refs_0_, bf16[32,32,128]{2,1,0:T(8,128)(2,1)S(1)} %collective-permute-done.refs_1_, bf16[32,32,128]{2,1,0:T(8,128)(2,1)S(1)} %collective-permute-done.4.refs_2_, bf16[32,32,128]{2,1,0:T(8,128)(2,1)S(1)} %collective-permute-done.5.refs_3_, ...), custom_call_target="tpu_custom_call" | custom-call | flops 268435456 | tf_op jit(solution)/shard_map/pallas_call | solution.py:333
  36.6 6.1 %all-to-all-done.1 = bf16[32,32,128]{2,1,0:T(8,128)(2,1)S(1)} async-done(((bf16[32,32,128]{2,1,0:T(8,128)(2,1)}), bf16[32,32,128]{2,1,0:T(8,128)(2,1)S(1)}, u32[]{:S(2)}, u32[]{:S(2)}) %all-to-all-start.1) | async-done | bytes 262176 | tf_op jit(solution)/shard_map/all_to_all | solution.py:329
  42.7 0.8 %shard_map.63 = bf16[16,64,128]{2,1,0:T(8,128)(2,1)} custom-call(s32[2,8]{1,0:T(2,128)S(4)} %get-tuple-element.6.owners_ref, s32[1]{0:T(128)S(6)} %copy.8.rot_ref, bf16[16,64,128]{2,1,0:T(8,128)(2,1)S(1)} %bitcast.3), custom_call_target="tpu_custom_call" | custom-call | tf_op jit(solution)/shard_map/pallas_call | solution.py:354
Async XLA Ops:
  3.2 17.9 %all-to-all-start = ((bf16[32,32,128]{2,1,0:T(8,128)(2,1)}), bf16[32,32,128]{2,1,0:T(8,128)(2,1)S(1)}, u32[]{:S(2)}, u32[]{:S(2)}) async-start(bf16[32,32,128]{2,1,0:T(8,128)(2,1)} %bitcast.1), calls=%async_computation | async-start | bytes 524288 | tf_op jit(solution)/shard_map/all_to_all | solution.py:312
  10.6 11.1 %collective-permute-start.1 = (bf16[2,128,512]{2,1,0:T(8,128)(2,1)S(1)}, bf16[2,128,512]{2,1,0:T(8,128)(2,1)S(1)}, u32[]{:S(2)}, u32[]{:S(2)}) collective-permute-start(bf16[2,128,512]{2,1,0:T(8,128)(2,1)S(1)} %get-tuple-element.8.refs_0_), channel_id=1, source_target_pairs={{0,1},{1,0},{2,3},{3,2},{4,5},{5,4},{6,7},{7,6},{8,9},{9,8},{10,11... | collective-permute-start | bytes 786440 | tf_op jit(solution)/shard_map/ppermute | solution.py:259
  10.9 10.3 %collective-permute-start.2 = (bf16[2,128,256]{2,1,0:T(8,128)(2,1)S(1)}, bf16[2,128,256]{2,1,0:T(8,128)(2,1)S(1)}, u32[]{:S(2)}, u32[]{:S(2)}) collective-permute-start(bf16[2,128,256]{2,1,0:T(8,128)(2,1)S(1)} %get-tuple-element.9), channel_id=1, source_target_pairs={{0,2},{1,3},{2,0},{3,1},{4,6},{5,7},{6,4},{7,5},{8,10},{9,11},{10,... | collective-permute-start | bytes 393224 | tf_op jit(solution)/shard_map/ppermute | solution.py:256
  21.1 2.3 %collective-permute-start = (bf16[32,32,128]{2,1,0:T(8,128)(2,1)S(1)}, bf16[32,32,128]{2,1,0:T(8,128)(2,1)S(1)}, u32[]{:S(2)}, u32[]{:S(2)}) collective-permute-start(bf16[32,32,128]{2,1,0:T(8,128)(2,1)S(1)} %all-to-all-done.refs_0_), channel_id=1, source_target_pairs={{0,1},{1,0},{2,3},{3,2},{4,5},{5,4},{6,7},{7,6},{8,9},{9,8},{10,11... | collective-permute-start | bytes 786440 | tf_op jit(solution)/shard_map/ppermute | solution.py:259
  21.1 1.7 %collective-permute-start.3 = (bf16[2,128,256]{2,1,0:T(8,128)(2,1)S(1)}, bf16[2,128,256]{2,1,0:T(8,128)(2,1)S(1)}, u32[]{:S(2)}, u32[]{:S(2)}) collective-permute-start(bf16[2,128,256]{2,1,0:T(8,128)(2,1)S(1)} %collective-permute-done.2.refs_0_), channel_id=1, source_target_pairs={{0,1},{1,0},{2,3},{3,2},{4,5},{5,4},{6,7},{7,6},{8,9},{9,8},{10,11... | collective-permute-start | bytes 393224 | tf_op jit(solution)/shard_map/ppermute | solution.py:259
  23.0 9.2 %collective-permute-start.4 = (bf16[32,32,128]{2,1,0:T(8,128)(2,1)S(1)}, bf16[32,32,128]{2,1,0:T(8,128)(2,1)S(1)}, u32[]{:S(2)}, u32[]{:S(2)}) collective-permute-start(bf16[32,32,128]{2,1,0:T(8,128)(2,1)S(1)} %all-to-all-done.refs_0_), channel_id=1, source_target_pairs={{0,2},{1,3},{2,0},{3,1},{4,6},{5,7},{6,4},{7,5},{8,10},{9,11},{10,... | collective-permute-start | bytes 786440 | tf_op jit(solution)/shard_map/ppermute | solution.py:256
  28.9 13.8 %all-to-all-start.1 = ((bf16[32,32,128]{2,1,0:T(8,128)(2,1)}), bf16[32,32,128]{2,1,0:T(8,128)(2,1)S(1)}, u32[]{:S(2)}, u32[]{:S(2)}) async-start(bf16[32,32,128]{2,1,0:T(8,128)(2,1)} %shard_map.62), calls=%async_computation.1 | async-start | bytes 524288 | tf_op jit(solution)/shard_map/all_to_all | solution.py:329
  32.1 1.6 %collective-permute-start.5 = (bf16[32,32,128]{2,1,0:T(8,128)(2,1)S(1)}, bf16[32,32,128]{2,1,0:T(8,128)(2,1)S(1)}, u32[]{:S(2)}, u32[]{:S(2)}) collective-permute-start(bf16[32,32,128]{2,1,0:T(8,128)(2,1)S(1)} %collective-permute-done.4.refs_2_), channel_id=1, source_target_pairs={{0,1},{1,0},{2,3},{3,2},{4,5},{5,4},{6,7},{7,6},{8,9},{9,8},{10,11... | collective-permute-start | bytes 786440 | tf_op jit(solution)/shard_map/ppermute | solution.py:259

commit v6 on v5

--- a/solution.py
+++ b/solution.py
@@ -6,9 +6,6 @@
 from jax.experimental import pallas as pl
 from jax.experimental.pallas import tpu as pltpu
 from jax.sharding import PartitionSpec as P
-
-
-ITERS = 2
 
 
 decay_rate = 0.9
@@ -138,46 +135,63 @@
         g_scr[...] = g_refs[0][...]
     eye5 = diagonal((order, order), 5.0)
     grad = g_scr[...]
-
-    def gram_of(side):
-        return dot(grad, grad, (((1 - side,), (1 - side,)), ((), ())))
-
-    def moment_of(side, gram):
-        factor = (base_ref[side] + (1.0 - decay_rate) * gram).astype(bf16)
+    bands = [slice(i, i + order // 2) for i in range(0, order, order // 2)]
+
+    def factor_of(side):
+        across = (((1 - side,), (1 - side,)), ((), ()))
+        parts_of = []
+        for at in bands:
+            gram = dot(grad, grad[at] if side == 0 else grad[:, at], across)
+            parts_of.append((base_ref[side, :, at] + (1.0 - decay_rate) * gram).astype(bf16))
+        return jnp.concatenate(parts_of, axis=1)
+
+    def moment_of(factor):
         norm = jnp.sum(jnp.square(factor.astype(f32)))
         return (2.5 / jnp.sqrt(norm) * factor.astype(f32)).astype(bf16)
 
     def step_of(moment):
-        return ((eye5 - moment.astype(f32)) * 0.25).astype(bf16)
+        step = ((eye5 - moment.astype(f32)) * 0.25).astype(bf16)
+        added = []
+        for i in range(0, order, 128):
+            block = slice(i, i + 128)
+            exact = (diagonal((128, 128), 5.0) - moment[block, block].astype(f32)) * 0.25
+            added.append(jnp.sum(step[block, block].astype(f32) - exact, axis=0, keepdims=True))
+        return step, jnp.concatenate(added, axis=1)
+
+    def partial_of(square, step, added):
+        cube, partial_m, more = [], [], []
+        for at in bands:
+            power = dot(square, step[:, at])
+            cube.append(power.astype(bf16))
+            piece = square[:, at].astype(f32)
+            partial_m.append((piece * (5.0 + 4.0 * added[:, at]) - 4.0 * power).astype(bf16))
+            moment = jnp.sum(piece * partial_m[-1].astype(f32), axis=0, keepdims=True)
+            rounded = ((5.0 - moment.astype(bf16).astype(f32)) * 0.25).astype(bf16)
+            more.append(rounded.astype(f32) - (5.0 - moment) * 0.25)
+        return [jnp.concatenate(x, axis=1) for x in (cube, partial_m, more)]
+
+    def root_of(step, added, cube, partial_m):
+        pieces = []
+        for at in bands:
+            last = dot(cube, partial_m[:, at])
+            pieces.append((step[:, at].astype(f32) * (1.25 + added[:, at]) - 0.25 * last).astype(bf16))
+        return jnp.concatenate(pieces, axis=1)
 
     def product(a, b):
         return dot(a, b).astype(bf16)
 
-    grams = {1: gram_of(1), 0: gram_of(0)}
-    moment = {1: moment_of(1, grams[1])}
-    root = {1: step_of(moment[1])}
-    for newton_step in range(ITERS - 1):
-        step_t = {1: root[1] if newton_step == 0 else step_of(moment[1])}
-        square = {1: product(step_t[1], step_t[1])}
-        if newton_step == 0:
-            moment[0] = moment_of(0, grams[0])
-            root[0] = step_of(moment[0])
-        else:
-            root[1] = product(root[1], step_t[1])
-        step_t[0] = root[0] if newton_step == 0 else step_of(moment[0])
-        partial_m = {1: product(square[1], moment[1])}
-        square[0] = product(step_t[0], step_t[0])
-        if newton_step:
-            root[0] = product(root[0], step_t[0])
-        moment[1] = product(square[1], partial_m[1])
-        partial_m[0] = product(square[0], moment[0])
-        last = step_of(moment[1])
-        moment[0] = product(square[0], partial_m[0])
-    root[1] = product(root[1], last)
+    factor = {1: factor_of(1), 0: factor_of(0)}
+    step, added, square, cube, partial_m, root = {}, {}, {}, {}, {}, {}
+    step[1], added[1] = step_of(moment_of(factor[1]))
+    square[1] = product(step[1], step[1])
+    step[0], added[0] = step_of(moment_of(factor[0]))
+    cube[1], partial_m[1], added[1] = partial_of(square[1], step[1], added[1])
+    square[0] = product(step[0], step[0])
+    root[1] = root_of(step[1], added[1], cube[1], partial_m[1])
+    cube[0], partial_m[0], added[0] = partial_of(square[0], step[0], added[0])
     grad_norm = jnp.sqrt(jnp.sum(jnp.square(grad.astype(f32))))
-    last = step_of(moment[0])
     right_applied = product(grad, root[1])
-    root[0] = product(root[0], last)
+    root[0] = root_of(step[0], added[0], cube[0], partial_m[0])
     res_scr[...] = dot(root[0], right_applied).astype(bf16)
     scale = grad_norm / (jnp.sqrt(jnp.sum(jnp.square(res_scr[...].astype(f32)))) + 1e-06)
     if not split:

time: 43.8 us -> 43.4 us (level)
  transfers between devices with their start and end apart: 8 -> 8, of which waited for: 4 -> 4; matrix products, arithmetic and copies ran while one was open for 0% -> 0% of each run, Pallas kernels for 20% -> 19%
where the time goes in v6:
time: 43.4 us; the launch traced here: 43.1 us
  waiting for transfers between devices  16.9 us (39%)
  starting transfers between devices  13.8 us (32%)
  Pallas kernels  11 us (25%)
  between operations  1.34 us (3%)
    all_to_all x1, waiting for transfers between devices, step(): lax.all_to_all(outgoing, ('dp', 'mp'), split_axis=0, concat_axis=0, tiled...  8.62 us
    all_to_all x1, starting transfers between devices, step(): lax.all_to_all(outgoing, ('dp', 'mp'), split_axis=0, concat_axis=0, tiled...  7.33 us
    all_to_all x1, waiting for transfers between devices, step(): lax.all_to_all(result, ('dp', 'mp'), split_axis=0, concat_axis=0, tiled=T...  6.09 us
    pallas_call x1, Pallas kernels, step(): call(functools.partial(owner_kernel, n_g=len(own_grad), split=split, size...  5.01 us
    all_to_all x1, starting transfers between devices, step(): lax.all_to_all(result, ('dp', 'mp'), split_axis=0, concat_axis=0, tiled=T...  3.22 us
    pallas_call x1, Pallas kernels, step(): call(functools.partial(stats_kernel, sizes=sizes), jax.ShapeDtypeStruct(f...  2.86 us
    ppermute x4, waiting for transfers between devices, to_part(): lax.ppermute(x, 'mp', [(i, i // parts * parts + (i + ahead) % parts) for...  2.19 us
    ppermute x2, starting transfers between devices, to_slot(): lax.ppermute(x, 'mp', [(i, (i + ahead * parts) % mp_count) for i in range...  2.15 us
  transfers between devices with their start and end apart: 8, of which 4 were waited for; matrix products, arithmetic and copies ran while one was open for 0% of the time, Pallas kernels for 19%

profile of v6, /device:TPU:0, one launch (start us, length us, event | category | flops | bytes accessed | tf_op | source)
XLA Modules:
  0.0 43.1 jit_solution(1584555457307022456)
XLA Ops:
  1.3 1.9 %shard_map.59 = (bf16[16,64,128]{2,1,0:T(8,128)(2,1)}, bf16[2,128,256]{2,1,0:T(8,128)(2,1)S(1)}, bf16[2,128,512]{2,1,0:T(8,128)(2,1)S(1)}, s32[2,8]{1,0:T(2,128)S(4)}) custom-call(s32[2,8]{1,0:T(2,128)} %bitcast.4, s32[1]{0:T(128)S(6)} %copy.8.rot_ref, bf16[16,64,128]{2,1,0:T(8,128)(2,1)} %tiles_hbm.1, f32[2,2,128,512]{3,2,1,0:T(8,128)} %refs_4_.1), custom_call_target="tpu_custom_call" | custom-call | tf_op jit(solution)/shard_map/pallas_call | solution.py:287
  3.2 7.3 %all-to-all-start = ((bf16[32,32,128]{2,1,0:T(8,128)(2,1)}), bf16[32,32,128]{2,1,0:T(8,128)(2,1)S(1)}, u32[]{:S(2)}, u32[]{:S(2)}) async-start(bf16[32,32,128]{2,1,0:T(8,128)(2,1)} %bitcast.1), calls=%async_computation | async-start | bytes 524288 | tf_op jit(solution)/shard_map/all_to_all | solution.py:326
  10.6 0.3 collective-permute-start.1
  10.9 1.6 %collective-permute-start.2 = (bf16[2,128,256]{2,1,0:T(8,128)(2,1)S(1)}, bf16[2,128,256]{2,1,0:T(8,128)(2,1)S(1)}, u32[]{:S(2)}, u32[]{:S(2)}) collective-permute-start(bf16[2,128,256]{2,1,0:T(8,128)(2,1)S(1)} %get-tuple-element.9), channel_id=1, source_target_pairs={{0,2},{1,3},{2,0},{3,1},{4,6},{5,7},{6,4},{7,5},{8,10},{9,11},{10,... | collective-permute-start | bytes 393224 | tf_op jit(solution)/shard_map/ppermute | solution.py:270
  12.5 8.6 %all-to-all-done.refs_0_ = bf16[32,32,128]{2,1,0:T(8,128)(2,1)S(1)} async-done(((bf16[32,32,128]{2,1,0:T(8,128)(2,1)}), bf16[32,32,128]{2,1,0:T(8,128)(2,1)S(1)}, u32[]{:S(2)}, u32[]{:S(2)}) %all-to-all-start) | async-done | bytes 262176 | tf_op jit(solution)/shard_map/all_to_all | solution.py:326
  21.1 0.0 collective-permute-start
  21.1 0.0 collective-permute-done.2.refs_0_
  21.1 0.5 %collective-permute-start.3 = (bf16[2,128,256]{2,1,0:T(8,128)(2,1)S(1)}, bf16[2,128,256]{2,1,0:T(8,128)(2,1)S(1)}, u32[]{:S(2)}, u32[]{:S(2)}) collective-permute-start(bf16[2,128,256]{2,1,0:T(8,128)(2,1)S(1)} %collective-permute-done.2.refs_0_), channel_id=1, source_target_pairs={{0,1},{1,0},{2,3},{3,2},{4,5},{5,4},{6,7},{7,6},{8,9},{9,8},{10,11... | collective-permute-start | bytes 393224 | tf_op jit(solution)/shard_map/ppermute | solution.py:273
  21.7 0.0 collective-permute-done.1.refs_1_
  21.7 0.3 shard_map.60.base_ref
  22.0 0.9 %collective-permute-done.3.refs_1_ = bf16[2,128,256]{2,1,0:T(8,128)(2,1)S(1)} collective-permute-done((bf16[2,128,256]{2,1,0:T(8,128)(2,1)S(1)}, bf16[2,128,256]{2,1,0:T(8,128)(2,1)S(1)}, u32[]{:S(2)}, u32[]{:S(2)}) %collective-permute-start.3) | collective-permute-done | bytes 131104 | tf_op jit(solution)/shard_map/ppermute | solution.py:273
  22.9 0.1 shard_map.61.refs_2_
  23.0 0.5 %collective-permute-start.4 = (bf16[32,32,128]{2,1,0:T(8,128)(2,1)S(1)}, bf16[32,32,128]{2,1,0:T(8,128)(2,1)S(1)}, u32[]{:S(2)}, u32[]{:S(2)}) collective-permute-start(bf16[32,32,128]{2,1,0:T(8,128)(2,1)S(1)} %all-to-all-done.refs_0_), channel_id=1, source_target_pairs={{0,2},{1,3},{2,0},{3,1},{4,6},{5,7},{6,4},{7,5},{8,10},{9,11},{10,... | collective-permute-start | bytes 786440 | tf_op jit(solution)/shard_map/ppermute | solution.py:270
  23.5 0.0 collective-permute-done.refs_1_
  23.5 5.0 %shard_map.62 = bf16[32,32,128]{2,1,0:T(8,128)(2,1)} custom-call(bf16[32,32,128]{2,1,0:T(8,128)(2,1)S(1)} %all-to-all-done.refs_0_, bf16[32,32,128]{2,1,0:T(8,128)(2,1)S(1)} %collective-permute-done.refs_1_, f32[2,512,512]{2,1,0:T(8,128)S(1)} %shard_map.61.refs_2_), custom_call_target="tpu_custom_call" | custom-call | flops 3221225472 | tf_op jit(solution)/shard_map/pallas_call | solution.py:331
  28.5 3.2 %all-to-all-start.1 = ((bf16[32,32,128]{2,1,0:T(8,128)(2,1)}), bf16[32,32,128]{2,1,0:T(8,128)(2,1)S(1)}, u32[]{:S(2)}, u32[]{:S(2)}) async-start(bf16[32,32,128]{2,1,0:T(8,128)(2,1)} %shard_map.62), calls=%async_computation.1 | async-start | bytes 524288 | tf_op jit(solution)/shard_map/all_to_all | solution.py:343
  31.7 0.0 collective-permute-done.4.refs_2_
  31.7 0.3 collective-permute-start.5
  32.1 1.3 %collective-permute-done.5.refs_3_ = bf16[32,32,128]{2,1,0:T(8,128)(2,1)S(1)} collective-permute-done((bf16[32,32,128]{2,1,0:T(8,128)(2,1)S(1)}, bf16[32,32,128]{2,1,0:T(8,128)(2,1)S(1)}, u32[]{:S(2)}, u32[]{:S(2)}) %collective-permute-start.5) | collective-permute-done | bytes 262176 | tf_op jit(solution)/shard_map/ppermute | solution.py:273
  33.3 2.9 %shard_map.64 = f32[2,2,128,512]{3,2,1,0:T(8,128)} custom-call(bf16[32,32,128]{2,1,0:T(8,128)(2,1)S(1)} %all-to-all-done.refs_0_, bf16[32,32,128]{2,1,0:T(8,128)(2,1)S(1)} %collective-permute-done.refs_1_, bf16[32,32,128]{2,1,0:T(8,128)(2,1)S(1)} %collective-permute-done.4.refs_2_, bf16[32,32,128]{2,1,0:T(8,128)(2,1)S(1)} %collective-permute-done.5.refs_3_, ...), custom_call_target="tpu_custom_call" | custom-call | flops 268435456 | tf_op jit(solution)/shard_map/pallas_call | solution.py:347
  36.2 6.1 %all-to-all-done.1 = bf16[32,32,128]{2,1,0:T(8,128)(2,1)S(1)} async-done(((bf16[32,32,128]{2,1,0:T(8,128)(2,1)}), bf16[32,32,128]{2,1,0:T(8,128)(2,1)S(1)}, u32[]{:S(2)}, u32[]{:S(2)}) %all-to-all-start.1) | async-done | bytes 262176 | tf_op jit(solution)/shard_map/all_to_all | solution.py:343
  42.3 0.8 %shard_map.63 = bf16[16,64,128]{2,1,0:T(8,128)(2,1)} custom-call(s32[2,8]{1,0:T(2,128)S(4)} %get-tuple-element.6.owners_ref, s32[1]{0:T(128)S(6)} %copy.8.rot_ref, bf16[16,64,128]{2,1,0:T(8,128)(2,1)S(1)} %bitcast.3), custom_call_target="tpu_custom_call" | custom-call | tf_op jit(solution)/shard_map/pallas_call | solution.py:368
Async XLA Ops:
  3.2 17.9 %all-to-all-start = ((bf16[32,32,128]{2,1,0:T(8,128)(2,1)}), bf16[32,32,128]{2,1,0:T(8,128)(2,1)S(1)}, u32[]{:S(2)}, u32[]{:S(2)}) async-start(bf16[32,32,128]{2,1,0:T(8,128)(2,1)} %bitcast.1), calls=%async_computation | async-start | bytes 524288 | tf_op jit(solution)/shard_map/all_to_all | solution.py:326
  10.6 11.1 %collective-permute-start.1 = (bf16[2,128,512]{2,1,0:T(8,128)(2,1)S(1)}, bf16[2,128,512]{2,1,0:T(8,128)(2,1)S(1)}, u32[]{:S(2)}, u32[]{:S(2)}) collective-permute-start(bf16[2,128,512]{2,1,0:T(8,128)(2,1)S(1)} %get-tuple-element.8.refs_0_), channel_id=1, source_target_pairs={{0,1},{1,0},{2,3},{3,2},{4,5},{5,4},{6,7},{7,6},{8,9},{9,8},{10,11... | collective-permute-start | bytes 786440 | tf_op jit(solution)/shard_map/ppermute | solution.py:273
  10.9 10.3 %collective-permute-start.2 = (bf16[2,128,256]{2,1,0:T(8,128)(2,1)S(1)}, bf16[2,128,256]{2,1,0:T(8,128)(2,1)S(1)}, u32[]{:S(2)}, u32[]{:S(2)}) collective-permute-start(bf16[2,128,256]{2,1,0:T(8,128)(2,1)S(1)} %get-tuple-element.9), channel_id=1, source_target_pairs={{0,2},{1,3},{2,0},{3,1},{4,6},{5,7},{6,4},{7,5},{8,10},{9,11},{10,... | collective-permute-start | bytes 393224 | tf_op jit(solution)/shard_map/ppermute | solution.py:270
  21.1 2.3 %collective-permute-start = (bf16[32,32,128]{2,1,0:T(8,128)(2,1)S(1)}, bf16[32,32,128]{2,1,0:T(8,128)(2,1)S(1)}, u32[]{:S(2)}, u32[]{:S(2)}) collective-permute-start(bf16[32,32,128]{2,1,0:T(8,128)(2,1)S(1)} %all-to-all-done.refs_0_), channel_id=1, source_target_pairs={{0,1},{1,0},{2,3},{3,2},{4,5},{5,4},{6,7},{7,6},{8,9},{9,8},{10,11... | collective-permute-start | bytes 786440 | tf_op jit(solution)/shard_map/ppermute | solution.py:273
  21.1 1.7 %collective-permute-start.3 = (bf16[2,128,256]{2,1,0:T(8,128)(2,1)S(1)}, bf16[2,128,256]{2,1,0:T(8,128)(2,1)S(1)}, u32[]{:S(2)}, u32[]{:S(2)}) collective-permute-start(bf16[2,128,256]{2,1,0:T(8,128)(2,1)S(1)} %collective-permute-done.2.refs_0_), channel_id=1, source_target_pairs={{0,1},{1,0},{2,3},{3,2},{4,5},{5,4},{6,7},{7,6},{8,9},{9,8},{10,11... | collective-permute-start | bytes 393224 | tf_op jit(solution)/shard_map/ppermute | solution.py:273
  23.0 8.8 %collective-permute-start.4 = (bf16[32,32,128]{2,1,0:T(8,128)(2,1)S(1)}, bf16[32,32,128]{2,1,0:T(8,128)(2,1)S(1)}, u32[]{:S(2)}, u32[]{:S(2)}) collective-permute-start(bf16[32,32,128]{2,1,0:T(8,128)(2,1)S(1)} %all-to-all-done.refs_0_), channel_id=1, source_target_pairs={{0,2},{1,3},{2,0},{3,1},{4,6},{5,7},{6,4},{7,5},{8,10},{9,11},{10,... | collective-permute-start | bytes 786440 | tf_op jit(solution)/shard_map/ppermute | solution.py:270
  28.5 13.8 %all-to-all-start.1 = ((bf16[32,32,128]{2,1,0:T(8,128)(2,1)}), bf16[32,32,128]{2,1,0:T(8,128)(2,1)S(1)}, u32[]{:S(2)}, u32[]{:S(2)}) async-start(bf16[32,32,128]{2,1,0:T(8,128)(2,1)} %shard_map.62), calls=%async_computation.1 | async-start | bytes 524288 | tf_op jit(solution)/shard_map/all_to_all | solution.py:343
  31.7 1.6 %collective-permute-start.5 = (bf16[32,32,128]{2,1,0:T(8,128)(2,1)S(1)}, bf16[32,32,128]{2,1,0:T(8,128)(2,1)S(1)}, u32[]{:S(2)}, u32[]{:S(2)}) collective-permute-start(bf16[32,32,128]{2,1,0:T(8,128)(2,1)S(1)} %collective-permute-done.4.refs_2_), channel_id=1, source_target_pairs={{0,1},{1,0},{2,3},{3,2},{4,5},{5,4},{6,7},{7,6},{8,9},{9,8},{10,11... | collective-permute-start | bytes 786440 | tf_op jit(solution)/shard_map/ppermute | solution.py:273

commit v7 on v6

--- a/solution.py
+++ b/solution.py
@@ -192,8 +192,12 @@
     grad_norm = jnp.sqrt(jnp.sum(jnp.square(grad.astype(f32))))
     right_applied = product(grad, root[1])
     root[0] = root_of(step[0], added[0], cube[0], partial_m[0])
-    res_scr[...] = dot(root[0], right_applied).astype(bf16)
-    scale = grad_norm / (jnp.sqrt(jnp.sum(jnp.square(res_scr[...].astype(f32)))) + 1e-06)
+    squares = jnp.zeros((1, order // 2), f32)
+    for at in bands:
+        piece = dot(root[0], right_applied[:, at]).astype(bf16)
+        res_scr[:, at] = piece
+        squares += jnp.sum(jnp.square(piece.astype(f32)), axis=0, keepdims=True)
+    scale = grad_norm / (jnp.sqrt(jnp.sum(squares)) + 1e-06)
     if not split:
         out_ref[...] = (res_scr[...].astype(f32) * scale).astype(bf16)
         return

time: 43.4 us -> 43.3 us (level)
  no operation moved by 1% of the time
where the time goes in v7:
time: 43.3 us; the launch traced here: 43 us
  waiting for transfers between devices  16.9 us (39%)
  starting transfers between devices  13.8 us (32%)
  Pallas kernels  10.9 us (25%)
  between operations  1.34 us (3%)
    all_to_all x1, waiting for transfers between devices, step(): lax.all_to_all(outgoing, ('dp', 'mp'), split_axis=0, concat_axis=0, tiled...  8.62 us
    all_to_all x1, starting transfers between devices, step(): lax.all_to_all(outgoing, ('dp', 'mp'), split_axis=0, concat_axis=0, tiled...  7.33 us
    all_to_all x1, waiting for transfers between devices, step(): lax.all_to_all(result, ('dp', 'mp'), split_axis=0, concat_axis=0, tiled=T...  6.09 us
    pallas_call x1, Pallas kernels, step(): call(functools.partial(owner_kernel, n_g=len(own_grad), split=split, size...  4.91 us
    all_to_all x1, starting transfers between devices, step(): lax.all_to_all(result, ('dp', 'mp'), split_axis=0, concat_axis=0, tiled=T...  3.22 us
    pallas_call x1, Pallas kernels, step(): call(functools.partial(stats_kernel, sizes=sizes), jax.ShapeDtypeStruct(f...  2.87 us
    ppermute x4, waiting for transfers between devices, to_part(): lax.ppermute(x, 'mp', [(i, i // parts * parts + (i + ahead) % parts) for...  2.19 us
    ppermute x2, starting transfers between devices, to_slot(): lax.ppermute(x, 'mp', [(i, (i + ahead * parts) % mp_count) for i in range...  2.15 us
  transfers between devices with their start and end apart: 8, of which 4 were waited for; matrix products, arithmetic and copies ran while one was open for 0% of the time, Pallas kernels for 19%

profile of v7, /device:TPU:0, one launch (start us, length us, event | category | flops | bytes accessed | tf_op | source)
XLA Modules:
  0.0 43.0 jit_solution(15118434962242660895)
XLA Ops:
  1.3 1.9 %shard_map.59 = (bf16[16,64,128]{2,1,0:T(8,128)(2,1)}, bf16[2,128,256]{2,1,0:T(8,128)(2,1)S(1)}, bf16[2,128,512]{2,1,0:T(8,128)(2,1)S(1)}, s32[2,8]{1,0:T(2,128)S(4)}) custom-call(s32[2,8]{1,0:T(2,128)} %bitcast.4, s32[1]{0:T(128)S(6)} %copy.8.rot_ref, bf16[16,64,128]{2,1,0:T(8,128)(2,1)} %tiles_hbm.1, f32[2,2,128,512]{3,2,1,0:T(8,128)} %refs_4_.1), custom_call_target="tpu_custom_call" | custom-call | tf_op jit(solution)/shard_map/pallas_call | solution.py:291
  3.2 7.3 %all-to-all-start = ((bf16[32,32,128]{2,1,0:T(8,128)(2,1)}), bf16[32,32,128]{2,1,0:T(8,128)(2,1)S(1)}, u32[]{:S(2)}, u32[]{:S(2)}) async-start(bf16[32,32,128]{2,1,0:T(8,128)(2,1)} %bitcast.1), calls=%async_computation | async-start | bytes 524288 | tf_op jit(solution)/shard_map/all_to_all | solution.py:330
  10.6 0.3 collective-permute-start.1
  10.9 1.6 %collective-permute-start.2 = (bf16[2,128,256]{2,1,0:T(8,128)(2,1)S(1)}, bf16[2,128,256]{2,1,0:T(8,128)(2,1)S(1)}, u32[]{:S(2)}, u32[]{:S(2)}) collective-permute-start(bf16[2,128,256]{2,1,0:T(8,128)(2,1)S(1)} %get-tuple-element.9), channel_id=1, source_target_pairs={{0,2},{1,3},{2,0},{3,1},{4,6},{5,7},{6,4},{7,5},{8,10},{9,11},{10,... | collective-permute-start | bytes 393224 | tf_op jit(solution)/shard_map/ppermute | solution.py:274
  12.5 8.6 %all-to-all-done.refs_0_ = bf16[32,32,128]{2,1,0:T(8,128)(2,1)S(1)} async-done(((bf16[32,32,128]{2,1,0:T(8,128)(2,1)}), bf16[32,32,128]{2,1,0:T(8,128)(2,1)S(1)}, u32[]{:S(2)}, u32[]{:S(2)}) %all-to-all-start) | async-done | bytes 262176 | tf_op jit(solution)/shard_map/all_to_all | solution.py:330
  21.1 0.0 collective-permute-start
  21.1 0.0 collective-permute-done.2.refs_0_
  21.1 0.5 %collective-permute-start.3 = (bf16[2,128,256]{2,1,0:T(8,128)(2,1)S(1)}, bf16[2,128,256]{2,1,0:T(8,128)(2,1)S(1)}, u32[]{:S(2)}, u32[]{:S(2)}) collective-permute-start(bf16[2,128,256]{2,1,0:T(8,128)(2,1)S(1)} %collective-permute-done.2.refs_0_), channel_id=1, source_target_pairs={{0,1},{1,0},{2,3},{3,2},{4,5},{5,4},{6,7},{7,6},{8,9},{9,8},{10,11... | collective-permute-start | bytes 393224 | tf_op jit(solution)/shard_map/ppermute | solution.py:277
  21.7 0.0 collective-permute-done.1.refs_1_
  21.7 0.3 shard_map.60.base_ref
  22.0 0.9 %collective-permute-done.3.refs_1_ = bf16[2,128,256]{2,1,0:T(8,128)(2,1)S(1)} collective-permute-done((bf16[2,128,256]{2,1,0:T(8,128)(2,1)S(1)}, bf16[2,128,256]{2,1,0:T(8,128)(2,1)S(1)}, u32[]{:S(2)}, u32[]{:S(2)}) %collective-permute-start.3) | collective-permute-done | bytes 131104 | tf_op jit(solution)/shard_map/ppermute | solution.py:277
  22.9 0.1 shard_map.61.refs_2_
  23.0 0.5 %collective-permute-start.4 = (bf16[32,32,128]{2,1,0:T(8,128)(2,1)S(1)}, bf16[32,32,128]{2,1,0:T(8,128)(2,1)S(1)}, u32[]{:S(2)}, u32[]{:S(2)}) collective-permute-start(bf16[32,32,128]{2,1,0:T(8,128)(2,1)S(1)} %all-to-all-done.refs_0_), channel_id=1, source_target_pairs={{0,2},{1,3},{2,0},{3,1},{4,6},{5,7},{6,4},{7,5},{8,10},{9,11},{10,... | collective-permute-start | bytes 786440 | tf_op jit(solution)/shard_map/ppermute | solution.py:274
  23.5 0.0 collective-permute-done.refs_1_
  23.5 4.9 %shard_map.62 = bf16[32,32,128]{2,1,0:T(8,128)(2,1)} custom-call(bf16[32,32,128]{2,1,0:T(8,128)(2,1)S(1)} %all-to-all-done.refs_0_, bf16[32,32,128]{2,1,0:T(8,128)(2,1)S(1)} %collective-permute-done.refs_1_, f32[2,512,512]{2,1,0:T(8,128)S(1)} %shard_map.61.refs_2_), custom_call_target="tpu_custom_call" | custom-call | flops 3221225472 | tf_op jit(solution)/shard_map/pallas_call | solution.py:335
  28.4 3.2 %all-to-all-start.1 = ((bf16[32,32,128]{2,1,0:T(8,128)(2,1)}), bf16[32,32,128]{2,1,0:T(8,128)(2,1)S(1)}, u32[]{:S(2)}, u32[]{:S(2)}) async-start(bf16[32,32,128]{2,1,0:T(8,128)(2,1)} %shard_map.62), calls=%async_computation.1 | async-start | bytes 524288 | tf_op jit(solution)/shard_map/all_to_all | solution.py:347
  31.6 0.0 collective-permute-done.4.refs_2_
  31.6 0.3 collective-permute-start.5
  31.9 1.3 %collective-permute-done.5.refs_3_ = bf16[32,32,128]{2,1,0:T(8,128)(2,1)S(1)} collective-permute-done((bf16[32,32,128]{2,1,0:T(8,128)(2,1)S(1)}, bf16[32,32,128]{2,1,0:T(8,128)(2,1)S(1)}, u32[]{:S(2)}, u32[]{:S(2)}) %collective-permute-start.5) | collective-permute-done | bytes 262176 | tf_op jit(solution)/shard_map/ppermute | solution.py:277
  33.2 2.9 %shard_map.64 = f32[2,2,128,512]{3,2,1,0:T(8,128)} custom-call(bf16[32,32,128]{2,1,0:T(8,128)(2,1)S(1)} %all-to-all-done.refs_0_, bf16[32,32,128]{2,1,0:T(8,128)(2,1)S(1)} %collective-permute-done.refs_1_, bf16[32,32,128]{2,1,0:T(8,128)(2,1)S(1)} %collective-permute-done.4.refs_2_, bf16[32,32,128]{2,1,0:T(8,128)(2,1)S(1)} %collective-permute-done.5.refs_3_, ...), custom_call_target="tpu_custom_call" | custom-call | flops 268435456 | tf_op jit(solution)/shard_map/pallas_call | solution.py:351
  36.1 6.1 %all-to-all-done.1 = bf16[32,32,128]{2,1,0:T(8,128)(2,1)S(1)} async-done(((bf16[32,32,128]{2,1,0:T(8,128)(2,1)}), bf16[32,32,128]{2,1,0:T(8,128)(2,1)S(1)}, u32[]{:S(2)}, u32[]{:S(2)}) %all-to-all-start.1) | async-done | bytes 262176 | tf_op jit(solution)/shard_map/all_to_all | solution.py:347
  42.2 0.8 %shard_map.63 = bf16[16,64,128]{2,1,0:T(8,128)(2,1)} custom-call(s32[2,8]{1,0:T(2,128)S(4)} %get-tuple-element.6.owners_ref, s32[1]{0:T(128)S(6)} %copy.8.rot_ref, bf16[16,64,128]{2,1,0:T(8,128)(2,1)S(1)} %bitcast.3), custom_call_target="tpu_custom_call" | custom-call | tf_op jit(solution)/shard_map/pallas_call | solution.py:372
Async XLA Ops:
  3.2 17.9 %all-to-all-start = ((bf16[32,32,128]{2,1,0:T(8,128)(2,1)}), bf16[32,32,128]{2,1,0:T(8,128)(2,1)S(1)}, u32[]{:S(2)}, u32[]{:S(2)}) async-start(bf16[32,32,128]{2,1,0:T(8,128)(2,1)} %bitcast.1), calls=%async_computation | async-start | bytes 524288 | tf_op jit(solution)/shard_map/all_to_all | solution.py:330
  10.6 11.1 %collective-permute-start.1 = (bf16[2,128,512]{2,1,0:T(8,128)(2,1)S(1)}, bf16[2,128,512]{2,1,0:T(8,128)(2,1)S(1)}, u32[]{:S(2)}, u32[]{:S(2)}) collective-permute-start(bf16[2,128,512]{2,1,0:T(8,128)(2,1)S(1)} %get-tuple-element.8.refs_0_), channel_id=1, source_target_pairs={{0,1},{1,0},{2,3},{3,2},{4,5},{5,4},{6,7},{7,6},{8,9},{9,8},{10,11... | collective-permute-start | bytes 786440 | tf_op jit(solution)/shard_map/ppermute | solution.py:277
  10.9 10.3 %collective-permute-start.2 = (bf16[2,128,256]{2,1,0:T(8,128)(2,1)S(1)}, bf16[2,128,256]{2,1,0:T(8,128)(2,1)S(1)}, u32[]{:S(2)}, u32[]{:S(2)}) collective-permute-start(bf16[2,128,256]{2,1,0:T(8,128)(2,1)S(1)} %get-tuple-element.9), channel_id=1, source_target_pairs={{0,2},{1,3},{2,0},{3,1},{4,6},{5,7},{6,4},{7,5},{8,10},{9,11},{10,... | collective-permute-start | bytes 393224 | tf_op jit(solution)/shard_map/ppermute | solution.py:274
  21.1 2.3 %collective-permute-start = (bf16[32,32,128]{2,1,0:T(8,128)(2,1)S(1)}, bf16[32,32,128]{2,1,0:T(8,128)(2,1)S(1)}, u32[]{:S(2)}, u32[]{:S(2)}) collective-permute-start(bf16[32,32,128]{2,1,0:T(8,128)(2,1)S(1)} %all-to-all-done.refs_0_), channel_id=1, source_target_pairs={{0,1},{1,0},{2,3},{3,2},{4,5},{5,4},{6,7},{7,6},{8,9},{9,8},{10,11... | collective-permute-start | bytes 786440 | tf_op jit(solution)/shard_map/ppermute | solution.py:277
  21.1 1.7 %collective-permute-start.3 = (bf16[2,128,256]{2,1,0:T(8,128)(2,1)S(1)}, bf16[2,128,256]{2,1,0:T(8,128)(2,1)S(1)}, u32[]{:S(2)}, u32[]{:S(2)}) collective-permute-start(bf16[2,128,256]{2,1,0:T(8,128)(2,1)S(1)} %collective-permute-done.2.refs_0_), channel_id=1, source_target_pairs={{0,1},{1,0},{2,3},{3,2},{4,5},{5,4},{6,7},{7,6},{8,9},{9,8},{10,11... | collective-permute-start | bytes 393224 | tf_op jit(solution)/shard_map/ppermute | solution.py:277
  23.0 8.7 %collective-permute-start.4 = (bf16[32,32,128]{2,1,0:T(8,128)(2,1)S(1)}, bf16[32,32,128]{2,1,0:T(8,128)(2,1)S(1)}, u32[]{:S(2)}, u32[]{:S(2)}) collective-permute-start(bf16[32,32,128]{2,1,0:T(8,128)(2,1)S(1)} %all-to-all-done.refs_0_), channel_id=1, source_target_pairs={{0,2},{1,3},{2,0},{3,1},{4,6},{5,7},{6,4},{7,5},{8,10},{9,11},{10,... | collective-permute-start | bytes 786440 | tf_op jit(solution)/shard_map/ppermute | solution.py:274
  28.4 13.8 %all-to-all-start.1 = ((bf16[32,32,128]{2,1,0:T(8,128)(2,1)}), bf16[32,32,128]{2,1,0:T(8,128)(2,1)S(1)}, u32[]{:S(2)}, u32[]{:S(2)}) async-start(bf16[32,32,128]{2,1,0:T(8,128)(2,1)} %shard_map.62), calls=%async_computation.1 | async-start | bytes 524288 | tf_op jit(solution)/shard_map/all_to_all | solution.py:347
  31.6 1.6 %collective-permute-start.5 = (bf16[32,32,128]{2,1,0:T(8,128)(2,1)S(1)}, bf16[32,32,128]{2,1,0:T(8,128)(2,1)S(1)}, u32[]{:S(2)}, u32[]{:S(2)}) collective-permute-start(bf16[32,32,128]{2,1,0:T(8,128)(2,1)S(1)} %collective-permute-done.4.refs_2_), channel_id=1, source_target_pairs={{0,1},{1,0},{2,3},{3,2},{4,5},{5,4},{6,7},{7,6},{8,9},{9,8},{10,11... | collective-permute-start | bytes 786440 | tf_op jit(solution)/shard_map/ppermute | solution.py:277
